TPU v7x, 32 devices: a 4x4x1 block of a 4x4x8 slice. The times are simulated.
32 devices in a mesh: sweep: 1 (over z), data: 4 (over y), ent: 8 (over x, core).
Axes of the slice: x: 4, y: 4, z: 1, core: 2. Of those that a mesh axis runs over, the one named last changes fastest.
The devices are a block of a 4x4x8 slice.
Arguments:
- ent_table: float32 [65536, 200], P(('sweep', 'ent'))
- ent_state: float32 [65536], P(('sweep', 'ent'))
- rel_table: float32 [11, 200], P('sweep')
- head_idx: int32 [8, 8, 8192], P(('sweep', 'ent'), None, 'data')
- tail_idx: int32 [8, 8, 8192], P(('sweep', 'ent'), None, 'data')
- rel_idx: int32 [8, 8, 8192], P(('sweep', 'ent'), None, 'data')
- edge_mask: int32 [8, 8, 8192], P(('sweep', 'ent'), None, 'data')
- neg_idx: int32 [8, 8, 768], P(('sweep', 'ent'))
Outputs:
- output 1: float32 [65536, 200], P(('sweep', 'ent'))
- output 2: float32 [65536], P(('sweep', 'ent'))
- output 3: float32 [11, 200], P('sweep')
- output 4: float32 [8, 8], P(('sweep', 'ent'))
All inputs are finite; a program needn't handle non-finite values.
Results may differ from a plain program's by a relative error of at most 0.001.
Values are sent between devices in bfloat16 or wider.
A program may use at most 768 MiB of HBM per device.

v0:
```python
import jax
import jax.numpy as jnp
from jax import lax
from jax.sharding import PartitionSpec as P

LR_SCALE = 0.2
EPSILON = 1e-8


def adagrad(param_rows, accum_rows, grad_rows, learn_rate):
    accum_new = accum_rows + jnp.mean(grad_rows * grad_rows, axis=-1)
    step_rows = grad_rows / jnp.sqrt(accum_new + EPSILON)[..., None]
    return param_rows - learn_rate * step_rows, accum_new


def bucket_terms(head_rows, rel_rows, tail_bf, neg_bf, weight):
    half_dim = head_rows.shape[-1] // 2
    re_h = head_rows[..., :half_dim]
    im_h = head_rows[..., half_dim:]
    re_r = rel_rows[..., :half_dim]
    im_r = rel_rows[..., half_dim:]
    query_vec = jnp.concatenate([re_h * re_r - im_h * im_r, re_h * im_r + im_h * re_r], axis=-1)
    query_bf = query_vec.astype(jnp.bfloat16)
    pos_score = jnp.einsum('...bd,...bd->...b', query_bf, tail_bf, preferred_element_type=jnp.float32)
    neg_score = jnp.einsum('...bd,...nd->...bn', query_bf, neg_bf, preferred_element_type=jnp.float32)
    top_score = jnp.maximum(jnp.max(neg_score, axis=-1), pos_score)
    pos_exp = jnp.exp(pos_score - top_score)
    neg_exp = jnp.exp(neg_score - top_score[..., None])
    exp_total = pos_exp + jnp.sum(neg_exp, axis=-1)
    log_total = top_score + jnp.log(exp_total)
    loss_sum = jnp.sum(weight * (log_total - pos_score), axis=-1)
    d_pos = weight * (pos_exp / exp_total - 1.0)
    d_neg = ((weight / exp_total)[..., None] * neg_exp).astype(jnp.bfloat16)
    grad_query = d_pos[..., None] * tail_bf + jnp.einsum('...bn,...nd->...bd', d_neg, neg_bf, preferred_element_type=jnp.float32)
    grad_tail = d_pos[..., None] * query_bf
    grad_neg = jnp.einsum('...bn,...bd->...nd', d_neg, query_bf, preferred_element_type=jnp.float32)
    re_g = grad_query[..., :half_dim]
    im_g = grad_query[..., half_dim:]
    grad_head = jnp.concatenate([re_g * re_r + im_g * im_r, im_g * re_r - re_g * im_r], axis=-1)
    grad_rel = jnp.concatenate([re_g * re_h + im_g * im_h, im_g * re_h - re_g * im_h], axis=-1)
    return loss_sum, grad_head, grad_rel, grad_tail, grad_neg


def solution(mesh):
    groups = mesh.shape['ent']
    data_reps = mesh.shape['data']
    row_spec = P(('sweep', 'ent'), None)
    edge_spec = P(('sweep', 'ent'), None, 'data')

    def device_fn(ent_table, ent_state, rel_table, head_idx, tail_idx, rel_idx, edge_mask, neg_idx):
        part_rows, emb_width = ent_table.shape
        rel_rows = rel_table.shape[0]
        bucket_edges = head_idx.shape[2] * data_reps
        learn_rate = LR_SCALE * emb_width ** -0.25
        table_now = ent_table
        state_now = ent_state
        rel_now = rel_table
        rel_state = jnp.zeros((rel_rows,), jnp.float32)
        loss_list = []
        for step_idx in range(groups):
            fetch_perm = [(source, (source - step_idx) % groups) for source in range(groups)]
            return_perm = [(source, (source + step_idx) % groups) for source in range(groups)]
            table_bf = table_now.astype(jnp.bfloat16)
            tail_table = table_bf if step_idx == 0 else lax.ppermute(table_bf, 'ent', fetch_perm)
            h_ids = head_idx[0, step_idx]
            t_ids = tail_idx[0, step_idx]
            r_ids = rel_idx[0, step_idx]
            n_ids = neg_idx[0, step_idx]
            weight = edge_mask[0, step_idx].astype(jnp.float32)
            head_rows = jnp.take(table_now, h_ids, axis=0)
            rel_rows_now = jnp.take(rel_now, r_ids, axis=0)
            tail_bf = jnp.take(tail_table, t_ids, axis=0)
            neg_bf = jnp.take(tail_table, n_ids, axis=0)
            loss_sum, g_head, g_rel, g_tail, g_neg = bucket_terms(head_rows, rel_rows_now, tail_bf, neg_bf, weight)
            sent_rows = jnp.concatenate([g_tail, g_neg], axis=0)
            sent_ids = jnp.concatenate([t_ids, n_ids])
            if step_idx > 0:
                sent_rows = lax.ppermute(sent_rows, 'ent', return_perm)
                sent_ids = lax.ppermute(sent_ids, 'ent', return_perm)
            ent_grad = jax.ops.segment_sum(jnp.concatenate([g_head, sent_rows], axis=0), jnp.concatenate([h_ids, sent_ids]), num_segments=part_rows)
            ent_grad = lax.psum(ent_grad, 'data')
            rel_grad = lax.psum(jax.ops.segment_sum(g_rel, r_ids, num_segments=rel_rows), ('data', 'ent'))
            loss_list.append(lax.psum(loss_sum, 'data') / bucket_edges)
            table_now, state_now = adagrad(table_now, state_now, ent_grad, learn_rate)
            rel_now, rel_state = adagrad(rel_now, rel_state, rel_grad, learn_rate)
        return table_now, state_now, rel_now, jnp.stack(loss_list)[None, :]

    return jax.shard_map(device_fn, mesh=mesh, in_specs=(row_spec, P(('sweep', 'ent')), P('sweep', None), edge_spec, edge_spec, edge_spec, edge_spec, P(('sweep', 'ent'), None, None)), out_specs=(row_spec, P(('sweep', 'ent')), P('sweep', None), row_spec), check_vma=False)
```

profile of v0, /device:TPU:97, one launch (start us, length us, event | category | flops | bytes accessed | tf_op | source)
XLA Modules:
  0.0 3187.7 jit_solution(1650791696577833794)
XLA Ops:
  82.2 29.7 scatter_custom_fusion
  126.0 52.0 %psum.169 = f32[11,200]{1,0:T(8,128)S(1)} all-reduce(f32[11,200]{1,0:T(8,128)S(1)} %scatter_custom_fusion.1), channel_id=1, replica_groups=mesh['sweep'=1,'data'=4,'ent'=8] {'data','ent'}, use_global_device_ids=true, to_apply=%region_6.11 | all-reduce | flops 2200 | bytes 17600 | tf_op jit(solution)/shard_map/psum | solution.py:82
  178.2 93.8 %all-reduce.10.cloned.1.call-done = f32[8192,200]{1,0:T(8,128)} async-done(((f32[8192,200]{1,0:T(8,128)}), f32[8192,200]{1,0:T(8,128)}) %all-reduce.10.cloned.1.call-update) | async-done | bytes 6553616 | tf_op jit(solution)/shard_map/psum | solution.py:81
  409.2 29.5 scatter_custom_fusion.2
  438.9 155.9 %all-reduce.12.cloned.1.call-done = f32[8192,200]{1,0:T(8,128)} async-done(((f32[8192,200]{1,0:T(8,128)}), f32[8192,200]{1,0:T(8,128)}) %all-reduce.12.cloned.1.call-update) | async-done | bytes 6553616 | tf_op jit(solution)/shard_map/psum | solution.py:81
  630.6 96.9 %psum.171 = f32[11,200]{1,0:T(8,128)S(1)} all-reduce(f32[11,200]{1,0:T(8,128)S(1)} %scatter_custom_fusion.3), channel_id=1, replica_groups=mesh['sweep'=1,'data'=4,'ent'=8] {'data','ent'}, use_global_device_ids=true, to_apply=%region_14.19 | all-reduce | flops 2200 | bytes 17600 | tf_op jit(solution)/shard_map/psum | solution.py:82
  788.5 50.2 %collective-permute-done.3 = s32[2816]{0:T(1024)S(1)} collective-permute-done((s32[2816]{0:T(1024)S(1)}, s32[2816]{0:T(1024)S(1)}, u32[]{:S(2)}, u32[]{:S(2)}) %collective-permute-start.3) | collective-permute-done | bytes 11296 | tf_op jit(solution)/shard_map/ppermute | solution.py:79
  850.1 29.5 scatter_custom_fusion.4
  880.3 152.4 %all-reduce.14.cloned.1.call-done = f32[8192,200]{1,0:T(8,128)} async-done(((f32[8192,200]{1,0:T(8,128)}), f32[8192,200]{1,0:T(8,128)}) %all-reduce.14.cloned.1.call-update) | async-done | bytes 6553616 | tf_op jit(solution)/shard_map/psum | solution.py:81
  1069.4 93.8 %psum.173 = f32[11,200]{1,0:T(8,128)S(1)} all-reduce(f32[11,200]{1,0:T(8,128)S(1)} %scatter_custom_fusion.5), channel_id=1, replica_groups=mesh['sweep'=1,'data'=4,'ent'=8] {'data','ent'}, use_global_device_ids=true, to_apply=%region_22.27 | all-reduce | flops 2200 | bytes 17600 | tf_op jit(solution)/shard_map/psum | solution.py:82
  1227.1 49.2 %collective-permute-done.6 = s32[2816]{0:T(1024)S(1)} collective-permute-done((s32[2816]{0:T(1024)S(1)}, s32[2816]{0:T(1024)S(1)}, u32[]{:S(2)}, u32[]{:S(2)}) %collective-permute-start.6) | collective-permute-done | bytes 11296 | tf_op jit(solution)/shard_map/ppermute | solution.py:79
  1318.0 152.7 %all-reduce.16.cloned.1.call-done = f32[8192,200]{1,0:T(8,128)} async-done(((f32[8192,200]{1,0:T(8,128)}), f32[8192,200]{1,0:T(8,128)}) %all-reduce.16.cloned.1.call-update) | async-done | bytes 6553616 | tf_op jit(solution)/shard_map/psum | solution.py:81
  1506.8 96.3 %psum.175 = f32[11,200]{1,0:T(8,128)S(1)} all-reduce(f32[11,200]{1,0:T(8,128)S(1)} %scatter_custom_fusion.7), channel_id=1, replica_groups=mesh['sweep'=1,'data'=4,'ent'=8] {'data','ent'}, use_global_device_ids=true, to_apply=%region_30.35 | all-reduce | flops 2200 | bytes 17600 | tf_op jit(solution)/shard_map/psum | solution.py:82
  1666.3 48.3 %collective-permute-done.9 = s32[2816]{0:T(1024)S(1)} collective-permute-done((s32[2816]{0:T(1024)S(1)}, s32[2816]{0:T(1024)S(1)}, u32[]{:S(2)}, u32[]{:S(2)}) %collective-permute-start.9) | collective-permute-done | bytes 11296 | tf_op jit(solution)/shard_map/ppermute | solution.py:79
  1756.2 153.3 %all-reduce.18.cloned.1.call-done = f32[8192,200]{1,0:T(8,128)} async-done(((f32[8192,200]{1,0:T(8,128)}), f32[8192,200]{1,0:T(8,128)}) %all-reduce.18.cloned.1.call-update) | async-done | bytes 6553616 | tf_op jit(solution)/shard_map/psum | solution.py:81
  1946.4 92.2 %psum.177 = f32[11,200]{1,0:T(8,128)S(1)} all-reduce(f32[11,200]{1,0:T(8,128)S(1)} %scatter_custom_fusion.9), channel_id=1, replica_groups=mesh['sweep'=1,'data'=4,'ent'=8] {'data','ent'}, use_global_device_ids=true, to_apply=%region_38.43 | all-reduce | flops 2200 | bytes 17600 | tf_op jit(solution)/shard_map/psum | solution.py:82
  2102.6 48.4 %collective-permute-done.12 = s32[2816]{0:T(1024)S(1)} collective-permute-done((s32[2816]{0:T(1024)S(1)}, s32[2816]{0:T(1024)S(1)}, u32[]{:S(2)}, u32[]{:S(2)}) %collective-permute-start.12) | collective-permute-done | bytes 11296 | tf_op jit(solution)/shard_map/ppermute | solution.py:79
  2192.5 153.6 %all-reduce.20.cloned.1.call-done = f32[8192,200]{1,0:T(8,128)} async-done(((f32[8192,200]{1,0:T(8,128)}), f32[8192,200]{1,0:T(8,128)}) %all-reduce.20.cloned.1.call-update) | async-done | bytes 6553616 | tf_op jit(solution)/shard_map/psum | solution.py:81
  2380.8 94.7 %psum.179 = f32[11,200]{1,0:T(8,128)S(1)} all-reduce(f32[11,200]{1,0:T(8,128)S(1)} %scatter_custom_fusion.11), channel_id=1, replica_groups=mesh['sweep'=1,'data'=4,'ent'=8] {'data','ent'}, use_global_device_ids=true, to_apply=%region_46.51 | all-reduce | flops 2200 | bytes 17600 | tf_op jit(solution)/shard_map/psum | solution.py:82
  2537.1 48.4 %collective-permute-done.15 = s32[2816]{0:T(1024)S(1)} collective-permute-done((s32[2816]{0:T(1024)S(1)}, s32[2816]{0:T(1024)S(1)}, u32[]{:S(2)}, u32[]{:S(2)}) %collective-permute-start.15) | collective-permute-done | bytes 11296 | tf_op jit(solution)/shard_map/ppermute | solution.py:79
  2627.3 153.7 %all-reduce.22.cloned.1.call-done = f32[8192,200]{1,0:T(8,128)} async-done(((f32[8192,200]{1,0:T(8,128)}), f32[8192,200]{1,0:T(8,128)}) %all-reduce.22.cloned.1.call-update) | async-done | bytes 6553616 | tf_op jit(solution)/shard_map/psum | solution.py:81
  2816.4 60.9 %psum.181 = f32[11,200]{1,0:T(8,128)S(1)} all-reduce(f32[11,200]{1,0:T(8,128)S(1)} %scatter_custom_fusion.13), channel_id=1, replica_groups=mesh['sweep'=1,'data'=4,'ent'=8] {'data','ent'}, use_global_device_ids=true, to_apply=%region_54.59 | all-reduce | flops 2200 | bytes 17600 | tf_op jit(solution)/shard_map/psum | solution.py:82
  3033.2 46.9 %psum.183 = f32[11,200]{1,0:T(8,128)S(1)} all-reduce(f32[11,200]{1,0:T(8,128)S(1)} %scatter_custom_fusion.15), channel_id=1, replica_groups=mesh['sweep'=1,'data'=4,'ent'=8] {'data','ent'}, use_global_device_ids=true, to_apply=%region_62.67 | all-reduce | flops 2200 | bytes 17600 | tf_op jit(solution)/shard_map/psum | solution.py:82
  3080.9 78.8 %all-reduce.24.cloned.1.call-done = f32[8192,200]{1,0:T(8,128)} async-done(((f32[8192,200]{1,0:T(8,128)}), f32[8192,200]{1,0:T(8,128)}) %all-reduce.24.cloned.1.call-update) | async-done | bytes 6553616 | tf_op jit(solution)/shard_map/psum | solution.py:81
  (579 shorter events, 1105.1 us)
Async XLA Ops:
  7.2 264.8 %all-reduce.10.cloned.1.call-start = ((), (), s32[]{:S(2)}) async-start(), calls=%async_computation | async-start | bytes 16777216 | tf_op jit(solution)/shard_map/psum | solution.py:81
  112.0 482.7 %all-reduce.12.cloned.1.call-start = ((), (), s32[]{:S(2)}) async-start(), calls=%async_computation.1 | async-start | bytes 16777216 | tf_op jit(solution)/shard_map/psum | solution.py:81
  438.7 594.0 %all-reduce.14.cloned.1.call-start = ((), (), s32[]{:S(2)}) async-start(), calls=%async_computation.2 | async-start | bytes 16777216 | tf_op jit(solution)/shard_map/psum | solution.py:81
  614.2 141.1 %collective-permute-start.4 = (bf16[8192,200]{0,1:T(8,128)(2,1)}, bf16[8192,200]{0,1:T(8,128)(2,1)}, u32[]{:S(2)}, u32[]{:S(2)}) collective-permute-start(bf16[8192,200]{0,1:T(8,128)(2,1)} %copy.102), channel_id=1, source_target_pairs={{0,6},{1,7},{2,0},{3,1},{4,2},{5,3},{6,4},{7,5},{8,14},{9,15},{10,... | collective-permute-start | bytes 9830408 | tf_op jit(solution)/shard_map/ppermute | solution.py:64
  787.6 54.5 %collective-permute-start.5 = (f32[2816,200]{0,1:T(8,128)S(1)}, f32[2816,200]{0,1:T(8,128)S(1)}, u32[]{:S(2)}, u32[]{:S(2)}) collective-permute-start(f32[2816,200]{0,1:T(8,128)S(1)} %pad_maximum_fusion.9), channel_id=1, source_target_pairs={{0,2},{1,3},{2,4},{3,5},{4,6},{5,7},{6,0},{7,1},{8,10},{9,11},{10,... | collective-permute-start | bytes 6758408 | tf_op jit(solution)/shard_map/ppermute | solution.py:78
  787.7 51.0 %collective-permute-start.3 = (s32[2816]{0:T(1024)S(1)}, s32[2816]{0:T(1024)S(1)}, u32[]{:S(2)}, u32[]{:S(2)}) collective-permute-start(s32[2816]{0:T(1024)S(1)} %pad_add_fusion.9), channel_id=1, source_target_pairs={{0,2},{1,3},{2,4},{3,5},{4,6},{5,7},{6,0},{7,1},{8,10},{9,11},{10,... | collective-permute-start | bytes 33800 | tf_op jit(solution)/shard_map/ppermute | solution.py:79
  879.6 591.1 %all-reduce.16.cloned.1.call-start = ((), (), s32[]{:S(2)}) async-start(), calls=%async_computation.3 | async-start | bytes 16777216 | tf_op jit(solution)/shard_map/psum | solution.py:81
  1052.2 138.8 %collective-permute-start.7 = (bf16[8192,200]{0,1:T(8,128)(2,1)}, bf16[8192,200]{0,1:T(8,128)(2,1)}, u32[]{:S(2)}, u32[]{:S(2)}) collective-permute-start(bf16[8192,200]{0,1:T(8,128)(2,1)} %copy.110), channel_id=1, source_target_pairs={{0,5},{1,6},{2,7},{3,0},{4,1},{5,2},{6,3},{7,4},{8,13},{9,14},{10,... | collective-permute-start | bytes 9830408 | tf_op jit(solution)/shard_map/ppermute | solution.py:64
  1223.4 56.2 %collective-permute-start.8 = (f32[2816,200]{0,1:T(8,128)S(1)}, f32[2816,200]{0,1:T(8,128)S(1)}, u32[]{:S(2)}, u32[]{:S(2)}) collective-permute-start(f32[2816,200]{0,1:T(8,128)S(1)} %pad_maximum_fusion.10), channel_id=1, source_target_pairs={{0,3},{1,4},{2,5},{3,6},{4,7},{5,0},{6,1},{7,2},{8,11},{9,12},{10,... | collective-permute-start | bytes 6758408 | tf_op jit(solution)/shard_map/ppermute | solution.py:78
  1225.2 51.0 %collective-permute-start.6 = (s32[2816]{0:T(1024)S(1)}, s32[2816]{0:T(1024)S(1)}, u32[]{:S(2)}, u32[]{:S(2)}) collective-permute-start(s32[2816]{0:T(1024)S(1)} %pad_add_fusion.10), channel_id=1, source_target_pairs={{0,3},{1,4},{2,5},{3,6},{4,7},{5,0},{6,1},{7,2},{8,11},{9,12},{10,... | collective-permute-start | bytes 33800 | tf_op jit(solution)/shard_map/ppermute | solution.py:79
  1317.3 592.2 %all-reduce.18.cloned.1.call-start = ((), (), s32[]{:S(2)}) async-start(), calls=%async_computation.4 | async-start | bytes 16777216 | tf_op jit(solution)/shard_map/psum | solution.py:81
  1490.1 140.8 %collective-permute-start.10 = (bf16[8192,200]{0,1:T(8,128)(2,1)}, bf16[8192,200]{0,1:T(8,128)(2,1)}, u32[]{:S(2)}, u32[]{:S(2)}) collective-permute-start(bf16[8192,200]{0,1:T(8,128)(2,1)} %copy.118), channel_id=1, source_target_pairs={{0,4},{1,5},{2,6},{3,7},{4,0},{5,1},{6,2},{7,3},{8,12},{9,13},{10,... | collective-permute-start | bytes 9830408 | tf_op jit(solution)/shard_map/ppermute | solution.py:64
  1663.2 54.7 %collective-permute-start.11 = (f32[2816,200]{0,1:T(8,128)S(1)}, f32[2816,200]{0,1:T(8,128)S(1)}, u32[]{:S(2)}, u32[]{:S(2)}) collective-permute-start(f32[2816,200]{0,1:T(8,128)S(1)} %pad_maximum_fusion.11), channel_id=1, source_target_pairs={{0,4},{1,5},{2,6},{3,7},{4,0},{5,1},{6,2},{7,3},{8,12},{9,13},{10,... | collective-permute-start | bytes 6758408 | tf_op jit(solution)/shard_map/ppermute | solution.py:78
  1664.5 50.1 %collective-permute-start.9 = (s32[2816]{0:T(1024)S(1)}, s32[2816]{0:T(1024)S(1)}, u32[]{:S(2)}, u32[]{:S(2)}) collective-permute-start(s32[2816]{0:T(1024)S(1)} %pad_add_fusion.11), channel_id=1, source_target_pairs={{0,4},{1,5},{2,6},{3,7},{4,0},{5,1},{6,2},{7,3},{8,12},{9,13},{10,... | collective-permute-start | bytes 33800 | tf_op jit(solution)/shard_map/ppermute | solution.py:79
  1755.5 590.6 %all-reduce.20.cloned.1.call-start = ((), (), s32[]{:S(2)}) async-start(), calls=%async_computation.5 | async-start | bytes 16777216 | tf_op jit(solution)/shard_map/psum | solution.py:81
  1928.9 137.5 %collective-permute-start.13 = (bf16[8192,200]{0,1:T(8,128)(2,1)}, bf16[8192,200]{0,1:T(8,128)(2,1)}, u32[]{:S(2)}, u32[]{:S(2)}) collective-permute-start(bf16[8192,200]{0,1:T(8,128)(2,1)} %copy.126), channel_id=1, source_target_pairs={{0,3},{1,4},{2,5},{3,6},{4,7},{5,0},{6,1},{7,2},{8,11},{9,12},{10,... | collective-permute-start | bytes 9830408 | tf_op jit(solution)/shard_map/ppermute | solution.py:64
  2098.8 55.5 %collective-permute-start.14 = (f32[2816,200]{0,1:T(8,128)S(1)}, f32[2816,200]{0,1:T(8,128)S(1)}, u32[]{:S(2)}, u32[]{:S(2)}) collective-permute-start(f32[2816,200]{0,1:T(8,128)S(1)} %pad_maximum_fusion.12), channel_id=1, source_target_pairs={{0,5},{1,6},{2,7},{3,0},{4,1},{5,2},{6,3},{7,4},{8,13},{9,14},{10,... | collective-permute-start | bytes 6758408 | tf_op jit(solution)/shard_map/ppermute | solution.py:78
  2101.8 49.2 %collective-permute-start.12 = (s32[2816]{0:T(1024)S(1)}, s32[2816]{0:T(1024)S(1)}, u32[]{:S(2)}, u32[]{:S(2)}) collective-permute-start(s32[2816]{0:T(1024)S(1)} %pad_add_fusion.12), channel_id=1, source_target_pairs={{0,5},{1,6},{2,7},{3,0},{4,1},{5,2},{6,3},{7,4},{8,13},{9,14},{10,... | collective-permute-start | bytes 33800 | tf_op jit(solution)/shard_map/ppermute | solution.py:79
  2191.9 589.1 %all-reduce.22.cloned.1.call-start = ((), (), s32[]{:S(2)}) async-start(), calls=%async_computation.6 | async-start | bytes 16777216 | tf_op jit(solution)/shard_map/psum | solution.py:81
  2365.6 137.6 %collective-permute-start.16 = (bf16[8192,200]{0,1:T(8,128)(2,1)}, bf16[8192,200]{0,1:T(8,128)(2,1)}, u32[]{:S(2)}, u32[]{:S(2)}) collective-permute-start(bf16[8192,200]{0,1:T(8,128)(2,1)} %copy.134), channel_id=1, source_target_pairs={{0,2},{1,3},{2,4},{3,5},{4,6},{5,7},{6,0},{7,1},{8,10},{9,11},{10,... | collective-permute-start | bytes 9830408 | tf_op jit(solution)/shard_map/ppermute | solution.py:64
  2535.6 53.3 %collective-permute-start.17 = (f32[2816,200]{0,1:T(8,128)S(1)}, f32[2816,200]{0,1:T(8,128)S(1)}, u32[]{:S(2)}, u32[]{:S(2)}) collective-permute-start(f32[2816,200]{0,1:T(8,128)S(1)} %pad_maximum_fusion.13), channel_id=1, source_target_pairs={{0,6},{1,7},{2,0},{3,1},{4,2},{5,3},{6,4},{7,5},{8,14},{9,15},{10,... | collective-permute-start | bytes 6758408 | tf_op jit(solution)/shard_map/ppermute | solution.py:78
  2536.6 48.9 %collective-permute-start.15 = (s32[2816]{0:T(1024)S(1)}, s32[2816]{0:T(1024)S(1)}, u32[]{:S(2)}, u32[]{:S(2)}) collective-permute-start(s32[2816]{0:T(1024)S(1)} %pad_add_fusion.13), channel_id=1, source_target_pairs={{0,6},{1,7},{2,0},{3,1},{4,2},{5,3},{6,4},{7,5},{8,14},{9,15},{10,... | collective-permute-start | bytes 33800 | tf_op jit(solution)/shard_map/ppermute | solution.py:79
  2626.6 533.2 %all-reduce.24.cloned.1.call-start = ((), (), s32[]{:S(2)}) async-start(), calls=%async_computation.7 | async-start | bytes 16777216 | tf_op jit(solution)/shard_map/psum | solution.py:81
  2800.4 104.7 %collective-permute-start.19 = (bf16[8192,200]{0,1:T(8,128)(2,1)}, bf16[8192,200]{0,1:T(8,128)(2,1)}, u32[]{:S(2)}, u32[]{:S(2)}) collective-permute-start(bf16[8192,200]{0,1:T(8,128)(2,1)} %copy.142), channel_id=1, source_target_pairs={{0,1},{1,2},{2,3},{3,4},{4,5},{5,6},{6,7},{7,0},{8,9},{9,10},{10,1... | collective-permute-start | bytes 9830408 | tf_op jit(solution)/shard_map/ppermute | solution.py:64
  (87 other events, 1109.5 us)
Sparse Core Ops, SparseCore 0:
  112.2 159.8 all-reduce.9
  438.8 155.8 all-reduce.11
  879.7 152.9 all-reduce.13
  1317.5 153.1 all-reduce.15
  1755.7 153.7 all-reduce.17
  2192.0 154.1 all-reduce.19
  2626.7 154.2 all-reduce.21
  3005.9 153.8 all-reduce.23
where the time goes:
time: 3200 us; the launch traced here: 3190 us
  waiting for transfers between devices  1400 us (44%)
  blocking collectives  641 us (20%)
  other arithmetic  529 us (17%)
  local copies, waits for them, and re-layouts  525 us (16%)
  matrix products  40.1 us (1%)
  starting transfers between devices  32.4 us (1%)
    psum x8, waiting for transfers between devices, device_fn(): ent_grad = lax.psum(ent_grad, 'data')  1090 us
    psum x8, blocking collectives, device_fn(): lax.psum(jax.ops.segment_sum(g_rel, r_ids, num_segments=rel_rows), ('data...  634 us
    ppermute x7, waiting for transfers between devices, device_fn(): sent_ids = lax.ppermute(sent_ids, 'ent', return_perm)  294 us
    scatter-add x8, other arithmetic, device_fn(): jax.ops.segment_sum(jnp.concatenate([g_head, sent_rows], axis=0), jnp.con...  236 us
    gather x16, local copies, waits for them, and re-layouts, device_fn(): head_rows = jnp.take(table_now, h_ids, axis=0)  115 us
    gather x16, local copies, waits for them, and re-layouts, device_fn(): tail_bf = jnp.take(tail_table, t_ids, axis=0)  104 us
    scatter-add x8, other arithmetic, device_fn(): jax.ops.segment_sum(g_rel, r_ids, num_segments=rel_rows)  95.7 us
    gather x16, local copies, waits for them, and re-layouts, device_fn(): rel_rows_now = jnp.take(rel_now, r_ids, axis=0)  66.8 us
  transfers between devices with their start and end apart: 29, of which 16 were waited for; matrix products, arithmetic and copies ran while one was open for 10% of the time, Pallas kernels for 0%

commit v1 on v0

v1 whole, which is shorter than its diff:
```python
import functools

import jax
import jax.numpy as jnp
from jax import lax
from jax.experimental import pallas as pl
from jax.experimental.pallas import tpu as pltpu
from jax.sharding import PartitionSpec as P

LR_SCALE = 0.2
EPSILON = 1e-8
LANES = 128
EDGE_BLOCK = 256
GATHER_UNROLL = 16
SYNC_CHUNKS = 2
VMEM_LIMIT = 60 * 1024 * 1024
MESH = pl.DeviceIdType.MESH
VM = pltpu.VMEM
F32 = jnp.float32
BF16 = jnp.bfloat16


def interleave(table):
    rows, width = table.shape
    half = width // 2
    return jnp.pad(table.reshape(rows, 2, half), ((0, 0), (0, 0), (0, LANES - half))).reshape(rows * 2, LANES)


def deinterleave(table, width):
    rows = table.shape[0] // 2
    return table.reshape(rows, 2, LANES)[:, :, :width // 2].reshape(rows, width)


def pair(row):
    return pl.ds(pl.multiple_of(row * 2, 2), 2)


def gather_kernel(shift, h_ids, r_ids, t_ids, n_ids, table, rel, h_rows, r_rows, q_out, t_out, n_out, t_rows, n_rows):
    edges = t_out.shape[0]
    negs = n_out.shape[0]

    def gather_edges(step, _):
        base = step * GATHER_UNROLL
        for off in range(GATHER_UNROLL):
            at = base + off
            h_rows[pair(at), :] = table[pair(h_ids[shift, at]), :]
            r_rows[pair(at), :] = rel[pair(r_ids[shift, at]), :]
            t_rows[pair(at), :] = table[pair(t_ids[0, at]), :]
        return 0

    lax.fori_loop(0, edges // GATHER_UNROLL, gather_edges, 0)

    def gather_negs(step, _):
        base = step * GATHER_UNROLL
        for off in range(GATHER_UNROLL):
            at = base + off
            n_rows[pair(at), :] = table[pair(n_ids[0, at]), :]
        return 0

    lax.fori_loop(0, negs // GATHER_UNROLL, gather_negs, 0)

    def form(step, _):
        base = pl.multiple_of(step * LANES, LANES)
        rows = pl.ds(base, LANES)
        even = pl.ds(pl.multiple_of(2 * base, 2), LANES, stride=2)
        odd = pl.ds(2 * base + 1, LANES, stride=2)
        re_h, im_h = h_rows[even, :], h_rows[odd, :]
        re_r, im_r = r_rows[even, :], r_rows[odd, :]
        q_out[rows, 0:LANES] = (re_h * re_r - im_h * im_r).astype(BF16)
        q_out[rows, LANES:2 * LANES] = (re_h * im_r + im_h * re_r).astype(BF16)
        t_out[rows, 0:LANES] = t_rows[even, :].astype(BF16)
        t_out[rows, LANES:2 * LANES] = t_rows[odd, :].astype(BF16)
        return 0

    lax.fori_loop(0, edges // LANES, form, 0)

    def form_negs(step, _):
        base = pl.multiple_of(step * LANES, LANES)
        rows = pl.ds(base, LANES)
        n_out[rows, 0:LANES] = n_rows[pl.ds(pl.multiple_of(2 * base, 2), LANES, stride=2), :].astype(BF16)
        n_out[rows, LANES:2 * LANES] = n_rows[pl.ds(2 * base + 1, LANES, stride=2), :].astype(BF16)
        return 0

    lax.fori_loop(0, negs // LANES, form_negs, 0)


def bucket_kernel(shift, group, q_ref, t_ref, n_ref, w_ref, gq_ref, gt_ref, gn_ref, loss_ref, *scratch):
    edges = q_ref.shape[0]
    negs = n_ref.shape[0]
    steps = edges // EDGE_BLOCK
    if shift:
        gn_acc, q_got, gq_send, q_sems, gq_sems = scratch
        me = lax.axis_index('ent')
        ahead = lax.rem(me + shift, group)
        behind = lax.rem(me + group - shift, group)

        def block(step):
            return pl.ds(pl.multiple_of(step * EDGE_BLOCK, EDGE_BLOCK), EDGE_BLOCK)

        def q_copy(step):
            return pltpu.make_async_remote_copy(
                src_ref=q_ref.at[block(step), :], dst_ref=q_got.at[block(step), :],
                send_sem=q_sems.at[0, step], recv_sem=q_sems.at[1, step],
                device_id={'ent': ahead}, device_id_type=MESH)

        def gq_copy(step):
            return pltpu.make_async_remote_copy(
                src_ref=gq_send.at[block(step), :], dst_ref=gq_ref.at[block(step), :],
                send_sem=gq_sems.at[0, step], recv_sem=gq_sems.at[1, step],
                device_id={'ent': behind}, device_id_type=MESH)

        barrier = pltpu.get_barrier_semaphore()
        pl.semaphore_signal(barrier, inc=1, device_id={'ent': ahead}, device_id_type=MESH)
        pl.semaphore_signal(barrier, inc=1, device_id={'ent': behind}, device_id_type=MESH)
        pl.semaphore_wait(barrier, 2)
        for step in range(steps):
            q_copy(step).start()
        q_src, gq_dst = q_got, gq_send
    else:
        gn_acc, = scratch
        q_src, gq_dst = q_ref, gq_ref

    gn_acc[...] = jnp.zeros_like(gn_acc)
    eye = lax.broadcasted_iota(jnp.int32, (LANES, LANES), 0) == lax.broadcasted_iota(jnp.int32, (LANES, LANES), 1)
    per_block = EDGE_BLOCK // LANES

    def one_block(step, loss_acc):
        if shift:
            q_copy(step).wait_recv()
        base = pl.multiple_of(step * EDGE_BLOCK, EDGE_BLOCK)
        rows = pl.ds(base, EDGE_BLOCK)
        q = q_src[rows, :]
        t = t_ref[rows, :].astype(F32)
        q_wide = q.astype(F32)
        n = n_ref[...]
        w = jnp.concatenate(
            [jnp.sum(jnp.where(eye, w_ref[pl.ds(step * per_block + k, 1), :], 0.0), axis=1, keepdims=True) for k in range(per_block)], axis=0)
        pos = jnp.sum(q_wide * t, axis=1, keepdims=True)
        score = lax.dot_general(q, n, (((1,), (1,)), ((), ())), preferred_element_type=F32)
        top = jnp.maximum(jnp.max(score, axis=1, keepdims=True), pos)
        pos_exp = jnp.exp(pos - top)
        neg_exp = jnp.exp(score - top)
        total = pos_exp + jnp.sum(neg_exp, axis=1, keepdims=True)
        loss_acc = loss_acc + jnp.sum(w * (top + jnp.log(total) - pos), axis=0, keepdims=True)
        d_pos = w * (pos_exp / total - 1.0)
        d_neg = ((w / total) * neg_exp).astype(BF16)
        gq_dst[rows, :] = (d_pos * t + jnp.dot(d_neg, n, preferred_element_type=F32)).astype(gq_dst.dtype)
        g_tail = d_pos * q_wide
        gt_ref[pl.ds(pl.multiple_of(2 * base, 2), EDGE_BLOCK, stride=2), :] = g_tail[:, 0:LANES]
        gt_ref[pl.ds(2 * base + 1, EDGE_BLOCK, stride=2), :] = g_tail[:, LANES:2 * LANES]
        gn_acc[...] += lax.dot_general(q, d_neg, (((0,), (0,)), ((), ())), preferred_element_type=F32)
        if shift:
            gq_copy(step).start()
        return loss_acc

    loss = lax.fori_loop(0, steps, one_block, jnp.zeros((1, 1), F32))
    loss_ref[...] = jnp.broadcast_to(loss, loss_ref.shape)
    for half in range(2):
        gn_ref[pl.ds(half, negs, stride=2), :] = gn_acc[half * LANES:(half + 1) * LANES, :].T
    if shift:
        for step in range(steps):
            q_copy(step).wait_send()
            gq_copy(step).wait()


def scatter_kernel(shift, h_ids, t_ids, n_ids, r_ref, gq_ref, h_rows, r_rows, gt_ref, gn_ref, acc, grel, acc_b, acc_c, acc_d, gh):
    edges = gq_ref.shape[0]
    negs = gn_ref.shape[0] // 2
    table_rows = acc.shape[0]
    rel_pad = grel.shape[0] // 2

    zero_rows = 512

    def clear(step, _):
        rows = pl.ds(pl.multiple_of(step * zero_rows, zero_rows), zero_rows)
        for ref in (acc, acc_b, acc_c, acc_d):
            ref[rows, :] = jnp.zeros((zero_rows, LANES), F32)
        return 0

    lax.fori_loop(0, table_rows // zero_rows, clear, 0)

    def form(step, carry):
        rel_re, rel_im = carry
        base = pl.multiple_of(step * LANES, LANES)
        rows = pl.ds(base, LANES)
        even = pl.ds(pl.multiple_of(2 * base, 2), LANES, stride=2)
        odd = pl.ds(2 * base + 1, LANES, stride=2)
        re_g = gq_ref[rows, 0:LANES].astype(F32)
        im_g = gq_ref[rows, LANES:2 * LANES].astype(F32)
        re_r, im_r = r_rows[even, :], r_rows[odd, :]
        gh[even, :] = re_g * re_r + im_g * im_r
        gh[odd, :] = im_g * re_r - re_g * im_r
        re_h, im_h = h_rows[even, :], h_rows[odd, :]
        hot = (lax.broadcasted_iota(jnp.int32, (rel_pad, LANES), 0) == r_ref[pl.ds(step, 1), :]).astype(F32)
        rel_re = rel_re + jnp.dot(hot, re_g * re_h + im_g * im_h, precision=lax.Precision.HIGHEST, preferred_element_type=F32)
        rel_im = rel_im + jnp.dot(hot, im_g * re_h - re_g * im_h, precision=lax.Precision.HIGHEST, preferred_element_type=F32)
        return rel_re, rel_im

    zero = jnp.zeros((rel_pad, LANES), F32)
    rel_re, rel_im = lax.fori_loop(0, edges // LANES, form, (zero, zero))
    grel[pl.ds(0, rel_pad, stride=2), :] = rel_re
    grel[pl.ds(1, rel_pad, stride=2), :] = rel_im

    def add_edges(step, _):
        base = step * GATHER_UNROLL
        for off in range(0, GATHER_UNROLL, 2):
            at = base + off
            places = (pair(h_ids[shift, at]), pair(h_ids[shift, at + 1]), pair(t_ids[0, at]), pair(t_ids[0, at + 1]))
            refs = (acc, acc_b, acc_c, acc_d)
            terms = (gh[pair(at), :], gh[pair(at + 1), :], gt_ref[pair(at), :], gt_ref[pair(at + 1), :])
            sums = [ref[place, :] + term for ref, place, term in zip(refs, places, terms)]
            for ref, place, total in zip(refs, places, sums):
                ref[place, :] = total
        return 0

    lax.fori_loop(0, edges // GATHER_UNROLL, add_edges, 0)

    def add_negs(step, _):
        base = step * GATHER_UNROLL
        for off in range(0, GATHER_UNROLL, 4):
            at = base + off
            places = [pair(n_ids[0, at + k]) for k in range(4)]
            refs = (acc, acc_b, acc_c, acc_d)
            sums = [ref[place, :] + gn_ref[pair(at + k), :] for k, (ref, place) in enumerate(zip(refs, places))]
            for ref, place, total in zip(refs, places, sums):
                ref[place, :] = total
        return 0

    lax.fori_loop(0, negs // GATHER_UNROLL, add_negs, 0)

    def combine(step, _):
        rows = pl.ds(pl.multiple_of(step * zero_rows, zero_rows), zero_rows)
        acc[rows, :] = (acc[rows, :] + acc_b[rows, :]) + (acc_c[rows, :] + acc_d[rows, :])
        return 0

    lax.fori_loop(0, table_rows // zero_rows, combine, 0)


def update_kernel(width, learn_rate, groups, reps, acc_in, table_in, state_in, grel_in, rel_in, rel_state_in,
                  table_out, state_out, rel_out, rel_state_out,
                  first_send, first_got, plain_send, plain_got, merged_send, merged_got, work,
                  step_own, step_got, step_far, rel_x, rel_y, rel_send,
                  first_sems, plain_sems, merged_sems, own_sems, far_sems, rel_x_sems, rel_y_sems):
    me = lax.axis_index('data')
    ent = lax.axis_index('ent')
    peers = (lax.rem(me + 1, reps), lax.rem(me + reps - 1, reps))
    far = lax.rem(me + 2, reps)
    quarter = acc_in.shape[0] // reps
    half = quarter // 2
    chunk = half // SYNC_CHUNKS

    barrier = pltpu.get_barrier_semaphore()
    for off in range(1, reps):
        pl.semaphore_signal(barrier, inc=1, device_id={'data': lax.rem(me + off, reps)}, device_id_type=MESH)
    for off in range(1, groups):
        pl.semaphore_signal(barrier, inc=1, device_id={'ent': lax.rem(ent + off, groups)}, device_id_type=MESH)
    pl.semaphore_wait(barrier, reps + groups - 2)

    def remote(src, dst, sems, place, to):
        return pltpu.make_async_remote_copy(
            src_ref=src, dst_ref=dst, send_sem=sems.at[(0,) + place], recv_sem=sems.at[(1,) + place],
            device_id=to, device_id_type=MESH)

    rel_x[0] = grel_in[...]
    rel_send[...] = grel_in[...]
    x_copies = [remote(rel_send, rel_x.at[off], rel_x_sems, (off - 1,), {'ent': lax.rem(ent + off, groups)}) for off in range(1, groups)]
    for copy in x_copies:
        copy.start()

    def rows_of(owner, which, k):
        return pl.ds(pl.multiple_of(owner * quarter + which * half + k * chunk, chunk), chunk)

    def at_chunk(k):
        return pl.ds(k * chunk, chunk)

    first, plain, merged = {}, {}, {}
    for k in range(SYNC_CHUNKS):
        for side in range(2):
            first_send[side, at_chunk(k), :] = acc_in[rows_of(far, side, k), :].astype(BF16)
            first[side, k] = remote(first_send.at[side, at_chunk(k), :], first_got.at[side, at_chunk(k), :], first_sems, (side, k), {'data': peers[side]})
            first[side, k].start()
    for k in range(SYNC_CHUNKS):
        for side in range(2):
            plain_send[side, at_chunk(k), :] = acc_in[rows_of(peers[side], 1 - side, k), :].astype(BF16)
            plain[side, k] = remote(plain_send.at[side, at_chunk(k), :], plain_got.at[side, at_chunk(k), :], plain_sems, (side, k), {'data': peers[side]})
            plain[side, k].start()
    for k in range(SYNC_CHUNKS):
        for side in range(2):
            first[side, k].wait_recv()
            merged_send[side, at_chunk(k), :] = (first_got[side, at_chunk(k), :].astype(F32) + acc_in[rows_of(peers[side], side, k), :]).astype(BF16)
            merged[side, k] = remote(merged_send.at[side, at_chunk(k), :], merged_got.at[side, at_chunk(k), :], merged_sems, (side, k), {'data': peers[side]})
            merged[side, k].start()

    for copy in x_copies:
        copy.wait()
    total = rel_x[lax.rem(ent, groups)]
    for src in range(1, groups):
        total = total + rel_x[lax.rem(ent + groups - src, groups)]
    rel_y[0] = total
    rel_send[...] = total
    y_copies = [remote(rel_send, rel_y.at[off], rel_y_sems, (off - 1,), {'data': lax.rem(me + off, reps)}) for off in range(1, reps)]
    for copy in y_copies:
        copy.start()

    own = {}
    for k in range(SYNC_CHUNKS):
        for which in range(2):
            merged[which, k].wait_recv()
            plain[1 - which, k].wait_recv()
            work[...] = acc_in[rows_of(me, which, k), :] + (merged_got[which, at_chunk(k), :].astype(F32) + plain_got[1 - which, at_chunk(k), :].astype(F32))
            n = chunk // 2
            re_g, im_g = work[pl.ds(0, n, stride=2), :], work[pl.ds(1, n, stride=2), :]
            places = pl.ds(which * (half // 2) + k * n, n)
            state = state_in[places, :] + jnp.sum(re_g * re_g + im_g * im_g, axis=1, keepdims=True) / width
            state_out[places, :] = state
            scale = learn_rate / jnp.sqrt(state + EPSILON)
            work[pl.ds(0, n, stride=2), :] = re_g * scale
            work[pl.ds(1, n, stride=2), :] = im_g * scale
            step_own[which, at_chunk(k), :] = work[...].astype(BF16)
            for side in range(2):
                own[side, which, k] = remote(step_own.at[which, at_chunk(k), :], step_got.at[side, which, at_chunk(k), :], own_sems, (side, which, k), {'data': peers[side]})
                own[side, which, k].start()

    spread = {}
    for k in range(SYNC_CHUNKS):
        for which in range(2):
            for side in range(2):
                own[side, which, k].wait_recv()
                if side == which:
                    spread[side, k] = remote(step_got.at[side, which, at_chunk(k), :], step_far.at[side, at_chunk(k), :], far_sems, (side, k), {'data': peers[side]})
                    spread[side, k].start()
            for owner, ref in ((me, step_own.at[which]), (peers[1], step_got.at[0, which]), (peers[0], step_got.at[1, which])):
                rows = rows_of(owner, which, k)
                table_out[rows, :] = table_in[rows, :] - ref[at_chunk(k), :].astype(F32)

    for copy in y_copies:
        copy.wait()
    total = rel_y[lax.rem(me, reps)]
    for src in range(1, reps):
        total = total + rel_y[lax.rem(me + reps - src, reps)]
    rel_send[...] = total
    rel_rows = rel_send.shape[0] // 2
    re_g, im_g = rel_send[pl.ds(0, rel_rows, stride=2), :], rel_send[pl.ds(1, rel_rows, stride=2), :]
    state = rel_state_in[...] + jnp.sum(re_g * re_g + im_g * im_g, axis=1, keepdims=True) / width
    rel_state_out[...] = state
    scale = learn_rate / jnp.sqrt(state + EPSILON)
    rel_out[pl.ds(0, rel_rows, stride=2), :] = rel_in[pl.ds(0, rel_rows, stride=2), :] - re_g * scale
    rel_out[pl.ds(1, rel_rows, stride=2), :] = rel_in[pl.ds(1, rel_rows, stride=2), :] - im_g * scale

    for k in range(SYNC_CHUNKS):
        for side in range(2):
            spread[side, k].wait_recv()
            rows = rows_of(far, side, k)
            table_out[rows, :] = table_in[rows, :] - step_far[side, at_chunk(k), :].astype(F32)
    for group_of in (first, plain, merged, own, spread):
        for copy in group_of.values():
            copy.wait_send()


def solution(mesh):
    groups = mesh.shape['ent']
    reps = mesh.shape['data']
    row_spec = P(('sweep', 'ent'), None)
    edge_spec = P(('sweep', 'ent'), None, 'data')
    vmem = pl.BlockSpec(memory_space=VM)

    def device_fn(ent_table, ent_state, rel_table, head_idx, tail_idx, rel_idx, edge_mask, neg_idx):
        part_rows, width = ent_table.shape
        rel_count = rel_table.shape[0]
        edges = head_idx.shape[2]
        negs = neg_idx.shape[2]
        bucket_edges = edges * reps
        learn_rate = LR_SCALE * width ** -0.25
        rel_pad = -(-rel_count // 8) * 8
        quarter = part_rows // reps
        me = lax.axis_index('data')
        ent = lax.axis_index('ent')

        packed = jnp.concatenate([tail_idx[0], edge_mask[0], neg_idx[0]], axis=1)
        moved = [packed[0:1]]
        for shift in range(1, groups):
            moved.append(lax.ppermute(packed[shift:shift + 1], 'ent', [(src, (src + shift) % groups) for src in range(groups)]))

        h_all = head_idx[0]
        r_all = rel_idx[0]
        r_vec = rel_idx.reshape(groups, edges // LANES, LANES)

        table = interleave(ent_table)
        rel = interleave(jnp.pad(rel_table, ((0, rel_pad - rel_count), (0, 0))))
        rel_state = jnp.zeros((rel_pad, LANES), F32)
        state = jnp.broadcast_to(lax.dynamic_slice_in_dim(ent_state, me * quarter, quarter)[:, None], (quarter, LANES))
        losses = []

        smem = pl.BlockSpec(memory_space=pltpu.SMEM)
        params = pltpu.CompilerParams(vmem_limit_bytes=VMEM_LIMIT)
        for shift in range(groups):
            got = moved[shift]
            t_ids = got[:, :edges]
            n_ids = got[:, 2 * edges:]
            weight = got[:, edges:2 * edges].reshape(edges // LANES, LANES).astype(F32)

            h_rows, r_rows, q, t, n = pl.pallas_call(
                functools.partial(gather_kernel, shift),
                out_shape=[jax.ShapeDtypeStruct((2 * edges, LANES), F32)] * 2
                + [jax.ShapeDtypeStruct((edges, 2 * LANES), BF16)] * 2 + [jax.ShapeDtypeStruct((negs, 2 * LANES), BF16)],
                in_specs=[smem] * 4 + [vmem] * 2,
                out_specs=[vmem] * 5,
                scratch_shapes=[VM((2 * edges, LANES), F32), VM((2 * negs, LANES), F32)],
                compiler_params=params, name='gather_rows',
            )(h_all, r_all, t_ids, n_ids, table, rel)

            scratch = [VM((2 * LANES, negs), F32)]
            if shift:
                steps = edges // EDGE_BLOCK
                scratch += [VM((edges, 2 * LANES), BF16), VM((edges, 2 * LANES), BF16),
                            pltpu.SemaphoreType.DMA((2, steps)), pltpu.SemaphoreType.DMA((2, steps))]
            g_q, g_t, g_n, loss = pl.pallas_call(
                functools.partial(bucket_kernel, shift, groups),
                out_shape=[jax.ShapeDtypeStruct((edges, 2 * LANES), BF16 if shift else F32), jax.ShapeDtypeStruct((2 * edges, LANES), F32),
                           jax.ShapeDtypeStruct((2 * negs, LANES), F32), jax.ShapeDtypeStruct((8, LANES), F32)],
                in_specs=[vmem] * 4, out_specs=[vmem] * 4, scratch_shapes=scratch,
                compiler_params=pltpu.CompilerParams(vmem_limit_bytes=VMEM_LIMIT, collective_id=0, has_side_effects=True) if shift else params,
                name='bucket',
            )(q, t, n, weight)
            losses.append(loss[0, 0])

            acc, g_rel = pl.pallas_call(
                functools.partial(scatter_kernel, shift),
                out_shape=[jax.ShapeDtypeStruct((2 * part_rows, LANES), F32), jax.ShapeDtypeStruct((2 * rel_pad, LANES), F32)],
                in_specs=[smem] * 3 + [vmem] * 6, out_specs=[vmem] * 2,
                scratch_shapes=[VM((2 * part_rows, LANES), F32)] * 3 + [VM((2 * edges, LANES), F32)],
                compiler_params=params, name='scatter_rows',
            )(h_all, t_ids, n_ids, r_vec[shift], g_q, h_rows, r_rows, g_t, g_n)

            half = (2 * part_rows) // reps // 2
            block = VM((2, half, LANES), BF16)
            sems = pltpu.SemaphoreType.DMA
            table, state, rel, rel_state = pl.pallas_call(
                functools.partial(update_kernel, width, learn_rate, groups, reps),
                out_shape=[jax.ShapeDtypeStruct(table.shape, F32), jax.ShapeDtypeStruct(state.shape, F32),
                           jax.ShapeDtypeStruct(rel.shape, F32), jax.ShapeDtypeStruct(rel_state.shape, F32)],
                in_specs=[vmem] * 6, out_specs=[vmem] * 4,
                scratch_shapes=[block] * 6 + [VM((half // SYNC_CHUNKS, LANES), F32), block, VM((2, 2, half, LANES), BF16), block,
                                              VM((groups, 2 * rel_pad, LANES), F32), VM((reps, 2 * rel_pad, LANES), F32), VM((2 * rel_pad, LANES), F32),
                                              sems((2, 2, SYNC_CHUNKS)), sems((2, 2, SYNC_CHUNKS)), sems((2, 2, SYNC_CHUNKS)),
                                              sems((2, 2, 2, SYNC_CHUNKS)), sems((2, 2, SYNC_CHUNKS)), sems((2, groups - 1)), sems((2, reps - 1))],
                compiler_params=pltpu.CompilerParams(vmem_limit_bytes=VMEM_LIMIT, collective_id=1, has_side_effects=True), name='update',
            )(acc, table, state, g_rel, rel, rel_state)

        ent_out = deinterleave(table, width)
        state_out = lax.all_gather(state[:, 0], 'data', tiled=True)
        rel_out = deinterleave(rel, width)[:rel_count]
        mine = jnp.stack(losses)
        home = lax.rem(ent + groups - jnp.arange(groups), groups)
        spread = jnp.zeros((groups, groups), F32).at[home, jnp.arange(groups)].set(mine)
        bucket_loss = lax.psum(spread, ('data', 'ent'))
        loss_out = lax.dynamic_slice_in_dim(bucket_loss, ent, 1) / bucket_edges
        return ent_out, state_out, rel_out, loss_out

    return jax.shard_map(device_fn, mesh=mesh, in_specs=(row_spec, P(('sweep', 'ent')), P('sweep', None), edge_spec, edge_spec, edge_spec, edge_spec, P(('sweep', 'ent'), None, None)), out_specs=(row_spec, P(('sweep', 'ent')), P('sweep', None), row_spec), check_vma=False)
```

time: 3200 us -> 1440 us (0.45)
  waiting for transfers between devices: 1400 us -> 0.02 us
  Pallas kernels: 0 us -> 1250 us
  blocking collectives: 641 us -> 82.7 us
  other arithmetic: 529 us -> 12.7 us
  local copies, waits for them, and re-layouts: 525 us -> 74.7 us
  matrix products: 40.1 us -> 0 us
    pallas_call x0 -> x32, Pallas kernels: none -> 1250 us  [the longest x8 667 us: device_fn(): pl.pallas_call(functools.partial(update_kernel, width, learn_rate, groups...]
    psum x8 -> x0, waiting for transfers between devices: 1090 us -> none  [device_fn(): ent_grad = lax.psum(ent_grad, 'data')]
    psum x9 -> x1, blocking collectives: 641 us -> 46 us  [device_fn(): bucket_loss = lax.psum(spread, ('data', 'ent'))]
    gather x56 -> x0, local copies, waits for them, and re-layouts: 342 us -> none  [the longest x16 115 us: device_fn(): head_rows = jnp.take(table_now, h_ids, axis=0)]
    scatter-add x16 -> x0, other arithmetic: 332 us -> none  [the longest x8 236 us: device_fn(): jax.ops.segment_sum(jnp.concatenate([g_head, sent_rows], axis=0), jnp.con...]
    ppermute x21 -> x7, waiting for transfers between devices: 303 us -> 0.02 us  [device_fn(): lax.ppermute(packed[shift:shift + 1], 'ent', [(src, (src + shift) % group...]
    concatenate x16 -> x0, local copies, waits for them, and re-layouts: 61.2 us -> none  [the longest x8 46.9 us: device_fn(): jnp.concatenate([g_head, sent_rows], axis=0)]
    convert_element_type x9 -> x8, other arithmetic: 58.9 us -> 5.7 us  [device_fn(): weight = got[:, edges:2 * edges].reshape(edges // LANES, LANES).astype(F32)]
  transfers between devices with their start and end apart: 29 -> 7, of which waited for: 16 -> 0; matrix products, arithmetic and copies ran while one was open for 10% -> 3% of each run, Pallas kernels for 0% -> 77%
where the time goes in v1:
time: 1440 us; the launch traced here: 1430 us
  Pallas kernels  1250 us (87%)
  blocking collectives  82.7 us (6%)
  local copies, waits for them, and re-layouts  74.7 us (5%)
    pallas_call x8, Pallas kernels, device_fn(): pl.pallas_call(functools.partial(update_kernel, width, learn_rate, groups...  667 us
    pallas_call x8, Pallas kernels, device_fn(): pl.pallas_call(functools.partial(bucket_kernel, shift, groups), out_shape...  261 us
    pallas_call x8, Pallas kernels, device_fn(): pl.pallas_call(functools.partial(scatter_kernel, shift), out_shape=[jax.S...  185 us
    pallas_call x8, Pallas kernels, device_fn(): pl.pallas_call(functools.partial(gather_kernel, shift), out_shape=[jax.Sh...  132 us
    psum x1, blocking collectives, device_fn(): bucket_loss = lax.psum(spread, ('data', 'ent'))  46 us
    all_gather x1, blocking collectives, device_fn(): state_out = lax.all_gather(state[:, 0], 'data', tiled=True)  36.7 us
  transfers between devices with their start and end apart: 7, of which 0 were waited for; matrix products, arithmetic and copies ran while one was open for 3% of the time, Pallas kernels for 77%

profile of v1, /device:TPU:97, one launch (start us, length us, event | category | flops | bytes accessed | tf_op | source)
XLA Modules:
  0.0 1428.4 jit_solution(16653295448950651980)
XLA Ops:
  74.5 22.9 %scatter_rows.8 = (f32[16384,128]{1,0:T(8,128)}, f32[32,128]{1,0:T(8,128)}) custom-call(s32[8,2048]{1,0:T(8,128)} %bitcast.48, s32[1,2048]{1,0:T(1,128)} %slice_bitcast_fusion.t_ids, s32[1,768]{1,0:T(1,128)} %slice_bitcast_fusion.1.n_ids, s32[16,128]{1,0:T(8,128)} %bitcast.96, f32[2048,256]{1,0:T(8,128)} %get-tuple-element.126.gq_ref, ...), custom_call_target="tpu_custom_call" | custom-call | tf_op jit(solution)/shard_map/scatter_rows/pallas_call | solution.py:427
  99.2 85.2 %update.8 = (f32[16384,128]{1,0:T(8,128)}, f32[2048,128]{1,0:T(8,128)}, f32[32,128]{1,0:T(8,128)}, f32[16,128]{1,0:T(8,128)}) custom-call(f32[16384,128]{1,0:T(8,128)} %get-tuple-element.131.acc_in, f32[16384,128]{1,0:T(8,128)} %bitcast.46, f32[2048,128]{1,0:T(8,128)} %broadcast_in_dim.6.state_in, f32[32,128]{1,0:T(8,128)} %get-tuple-element.132.grel_in, ...), custom_call_target="tpu_custom_call" | custom-call | tf_op jit(solution)/shard_map/update/pallas_call | solution.py:438
  230.7 23.1 %scatter_rows.9 = (f32[16384,128]{1,0:T(8,128)}, f32[32,128]{1,0:T(8,128)}) custom-call(s32[8,2048]{1,0:T(8,128)} %bitcast.50, s32[1,2048]{1,0:T(1,128)} %get-tuple-element.269.t_ids, s32[1,768]{1,0:T(1,128)} %slice.245.n_ids, s32[16,128]{1,0:T(8,128)} %bitcast.87, bf16[2048,256]{1,0:T(8,128)(2,1)} %get-tuple-element.138.gq_ref, ...), custom_call_target="tpu_custom_call" | custom-call | tf_op jit(solution)/shard_map/scatter_rows/pallas_call | solution.py:427
  253.8 82.9 %update.9 = (f32[16384,128]{1,0:T(8,128)}, f32[2048,128]{1,0:T(8,128)}, f32[32,128]{1,0:T(8,128)}, f32[16,128]{1,0:T(8,128)}) custom-call(f32[16384,128]{1,0:T(8,128)} %get-tuple-element.143.acc_in, f32[16384,128]{1,0:T(8,128)} %get-tuple-element.133.table.table_in, f32[2048,128]{1,0:T(8,128)} %get-tuple-element.144.state_in, ...), custom_call_target="tpu_custom_call" | custom-call | tf_op jit(solution)/shard_map/update/pallas_call | solution.py:438
  353.9 34.0 %bucket.10 = (bf16[2048,256]{1,0:T(8,128)(2,1)}, f32[4096,128]{1,0:T(8,128)}, f32[1536,128]{1,0:T(8,128)}, f32[8,128]{1,0:T(8,128)}) custom-call(bf16[2048,256]{1,0:T(8,128)(2,1)} %get-tuple-element.149.q_ref, bf16[2048,256]{1,0:T(8,128)(2,1)} %get-tuple-element.150.t_ref, bf16[768,256]{1,0:T(8,128)(2,1)} %get-tuple-element.151.n_ref, f32[16,128]{1,0:T(8,128)} %bitcast.93), custom_call_target="tpu_custom_call" | custom-call | tf_op jit(solution)/shard_map/bucket/pallas_call | solution.py:417
  387.9 23.1 %scatter_rows.10 = (f32[16384,128]{1,0:T(8,128)}, f32[32,128]{1,0:T(8,128)}) custom-call(s32[8,2048]{1,0:T(8,128)} %bitcast.52, s32[1,2048]{1,0:T(1,128)} %get-tuple-element.267.t_ids, s32[1,768]{1,0:T(1,128)} %slice.243.n_ids, s32[16,128]{1,0:T(8,128)} %bitcast.86, bf16[2048,256]{1,0:T(8,128)(2,1)} %get-tuple-element.152.gq_ref, ...), custom_call_target="tpu_custom_call" | custom-call | tf_op jit(solution)/shard_map/scatter_rows/pallas_call | solution.py:427
  411.0 85.7 %update.10 = (f32[16384,128]{1,0:T(8,128)}, f32[2048,128]{1,0:T(8,128)}, f32[32,128]{1,0:T(8,128)}, f32[16,128]{1,0:T(8,128)}) custom-call(f32[16384,128]{1,0:T(8,128)} %get-tuple-element.157.acc_in, f32[16384,128]{1,0:T(8,128)} %get-tuple-element.147.table.table_in, f32[2048,128]{1,0:T(8,128)} %get-tuple-element.158.state_in, ...), custom_call_target="tpu_custom_call" | custom-call | tf_op jit(solution)/shard_map/update/pallas_call | solution.py:438
  513.9 42.3 %bucket.11 = (bf16[2048,256]{1,0:T(8,128)(2,1)}, f32[4096,128]{1,0:T(8,128)}, f32[1536,128]{1,0:T(8,128)}, f32[8,128]{1,0:T(8,128)}) custom-call(bf16[2048,256]{1,0:T(8,128)(2,1)} %get-tuple-element.163.q_ref, bf16[2048,256]{1,0:T(8,128)(2,1)} %get-tuple-element.164.t_ref, bf16[768,256]{1,0:T(8,128)(2,1)} %get-tuple-element.165.n_ref, f32[16,128]{1,0:T(8,128)} %bitcast.92), custom_call_target="tpu_custom_call" | custom-call | tf_op jit(solution)/shard_map/bucket/pallas_call | solution.py:417
  556.3 23.3 %scatter_rows.11 = (f32[16384,128]{1,0:T(8,128)}, f32[32,128]{1,0:T(8,128)}) custom-call(s32[8,2048]{1,0:T(8,128)} %bitcast.54, s32[1,2048]{1,0:T(1,128)} %get-tuple-element.265.t_ids, s32[1,768]{1,0:T(1,128)} %slice.241.n_ids, s32[16,128]{1,0:T(8,128)} %bitcast.85, bf16[2048,256]{1,0:T(8,128)(2,1)} %get-tuple-element.166.gq_ref, ...), custom_call_target="tpu_custom_call" | custom-call | tf_op jit(solution)/shard_map/scatter_rows/pallas_call | solution.py:427
  579.6 82.5 %update.11 = (f32[16384,128]{1,0:T(8,128)}, f32[2048,128]{1,0:T(8,128)}, f32[32,128]{1,0:T(8,128)}, f32[16,128]{1,0:T(8,128)}) custom-call(f32[16384,128]{1,0:T(8,128)} %get-tuple-element.171.acc_in, f32[16384,128]{1,0:T(8,128)} %get-tuple-element.161.table.table_in, f32[2048,128]{1,0:T(8,128)} %get-tuple-element.172.state_in, ...), custom_call_target="tpu_custom_call" | custom-call | tf_op jit(solution)/shard_map/update/pallas_call | solution.py:438
  679.2 52.0 %bucket.12 = (bf16[2048,256]{1,0:T(8,128)(2,1)}, f32[4096,128]{1,0:T(8,128)}, f32[1536,128]{1,0:T(8,128)}, f32[8,128]{1,0:T(8,128)}) custom-call(bf16[2048,256]{1,0:T(8,128)(2,1)} %get-tuple-element.177.q_ref, bf16[2048,256]{1,0:T(8,128)(2,1)} %get-tuple-element.178.t_ref, bf16[768,256]{1,0:T(8,128)(2,1)} %get-tuple-element.179.n_ref, f32[16,128]{1,0:T(8,128)} %bitcast.91), custom_call_target="tpu_custom_call" | custom-call | tf_op jit(solution)/shard_map/bucket/pallas_call | solution.py:417
  731.3 23.1 %scatter_rows.12 = (f32[16384,128]{1,0:T(8,128)}, f32[32,128]{1,0:T(8,128)}) custom-call(s32[8,2048]{1,0:T(8,128)} %bitcast.56, s32[1,2048]{1,0:T(1,128)} %get-tuple-element.263.t_ids, s32[1,768]{1,0:T(1,128)} %slice.239.n_ids, s32[16,128]{1,0:T(8,128)} %bitcast.84, bf16[2048,256]{1,0:T(8,128)(2,1)} %get-tuple-element.180.gq_ref, ...), custom_call_target="tpu_custom_call" | custom-call | tf_op jit(solution)/shard_map/scatter_rows/pallas_call | solution.py:427
  754.4 83.5 %update.12 = (f32[16384,128]{1,0:T(8,128)}, f32[2048,128]{1,0:T(8,128)}, f32[32,128]{1,0:T(8,128)}, f32[16,128]{1,0:T(8,128)}) custom-call(f32[16384,128]{1,0:T(8,128)} %get-tuple-element.185.acc_in, f32[16384,128]{1,0:T(8,128)} %get-tuple-element.175.table.table_in, f32[2048,128]{1,0:T(8,128)} %get-tuple-element.186.state_in, ...), custom_call_target="tpu_custom_call" | custom-call | tf_op jit(solution)/shard_map/update/pallas_call | solution.py:438
  855.1 42.1 %bucket.13 = (bf16[2048,256]{1,0:T(8,128)(2,1)}, f32[4096,128]{1,0:T(8,128)}, f32[1536,128]{1,0:T(8,128)}, f32[8,128]{1,0:T(8,128)}) custom-call(bf16[2048,256]{1,0:T(8,128)(2,1)} %get-tuple-element.191.q_ref, bf16[2048,256]{1,0:T(8,128)(2,1)} %get-tuple-element.192.t_ref, bf16[768,256]{1,0:T(8,128)(2,1)} %get-tuple-element.193.n_ref, f32[16,128]{1,0:T(8,128)} %bitcast.90), custom_call_target="tpu_custom_call" | custom-call | tf_op jit(solution)/shard_map/bucket/pallas_call | solution.py:417
  897.2 23.5 %scatter_rows.13 = (f32[16384,128]{1,0:T(8,128)}, f32[32,128]{1,0:T(8,128)}) custom-call(s32[8,2048]{1,0:T(8,128)} %bitcast.58, s32[1,2048]{1,0:T(1,128)} %get-tuple-element.261.t_ids, s32[1,768]{1,0:T(1,128)} %slice.237.n_ids, s32[16,128]{1,0:T(8,128)} %bitcast.83, bf16[2048,256]{1,0:T(8,128)(2,1)} %get-tuple-element.194.gq_ref, ...), custom_call_target="tpu_custom_call" | custom-call | tf_op jit(solution)/shard_map/scatter_rows/pallas_call | solution.py:427
  920.7 82.1 %update.13 = (f32[16384,128]{1,0:T(8,128)}, f32[2048,128]{1,0:T(8,128)}, f32[32,128]{1,0:T(8,128)}, f32[16,128]{1,0:T(8,128)}) custom-call(f32[16384,128]{1,0:T(8,128)} %get-tuple-element.199.acc_in, f32[16384,128]{1,0:T(8,128)} %get-tuple-element.189.table.table_in, f32[2048,128]{1,0:T(8,128)} %get-tuple-element.200.state_in, ...), custom_call_target="tpu_custom_call" | custom-call | tf_op jit(solution)/shard_map/update/pallas_call | solution.py:438
  1020.0 34.0 %bucket.14 = (bf16[2048,256]{1,0:T(8,128)(2,1)}, f32[4096,128]{1,0:T(8,128)}, f32[1536,128]{1,0:T(8,128)}, f32[8,128]{1,0:T(8,128)}) custom-call(bf16[2048,256]{1,0:T(8,128)(2,1)} %get-tuple-element.205.q_ref, bf16[2048,256]{1,0:T(8,128)(2,1)} %get-tuple-element.206.t_ref, bf16[768,256]{1,0:T(8,128)(2,1)} %get-tuple-element.207.n_ref, f32[16,128]{1,0:T(8,128)} %bitcast.89), custom_call_target="tpu_custom_call" | custom-call | tf_op jit(solution)/shard_map/bucket/pallas_call | solution.py:417
  1054.0 23.1 %scatter_rows.14 = (f32[16384,128]{1,0:T(8,128)}, f32[32,128]{1,0:T(8,128)}) custom-call(s32[8,2048]{1,0:T(8,128)} %bitcast.60, s32[1,2048]{1,0:T(1,128)} %get-tuple-element.259.t_ids, s32[1,768]{1,0:T(1,128)} %slice.235.n_ids, s32[16,128]{1,0:T(8,128)} %bitcast.82, bf16[2048,256]{1,0:T(8,128)(2,1)} %get-tuple-element.208.gq_ref, ...), custom_call_target="tpu_custom_call" | custom-call | tf_op jit(solution)/shard_map/scatter_rows/pallas_call | solution.py:427
  1077.1 83.1 %update.14 = (f32[16384,128]{1,0:T(8,128)}, f32[2048,128]{1,0:T(8,128)}, f32[32,128]{1,0:T(8,128)}, f32[16,128]{1,0:T(8,128)}) custom-call(f32[16384,128]{1,0:T(8,128)} %get-tuple-element.213.acc_in, f32[16384,128]{1,0:T(8,128)} %get-tuple-element.203.table.table_in, f32[2048,128]{1,0:T(8,128)} %get-tuple-element.214.state_in, ...), custom_call_target="tpu_custom_call" | custom-call | tf_op jit(solution)/shard_map/update/pallas_call | solution.py:438
  1178.1 22.9 %bucket.15 = (bf16[2048,256]{1,0:T(8,128)(2,1)}, f32[4096,128]{1,0:T(8,128)}, f32[1536,128]{1,0:T(8,128)}, f32[8,128]{1,0:T(8,128)}) custom-call(bf16[2048,256]{1,0:T(8,128)(2,1)} %get-tuple-element.219.q_ref, bf16[2048,256]{1,0:T(8,128)(2,1)} %get-tuple-element.220.t_ref, bf16[768,256]{1,0:T(8,128)(2,1)} %get-tuple-element.221.n_ref, f32[16,128]{1,0:T(8,128)} %bitcast.95), custom_call_target="tpu_custom_call" | custom-call | tf_op jit(solution)/shard_map/bucket/pallas_call | solution.py:417
  1215.6 46.0 %psum.7 = f32[8,8]{1,0:T(8,128)S(1)} all-reduce(f32[8,8]{1,0:T(8,128)S(1)} %scatter_fusion), channel_id=1, replica_groups=mesh['sweep'=1,'data'=4,'ent'=8] {'data','ent'}, use_global_device_ids=true, to_apply=%region_1.2 | all-reduce | flops 64 | bytes 512 | tf_op jit(solution)/shard_map/psum | solution.py:456
  1261.6 23.1 %scatter_rows.15 = (f32[16384,128]{1,0:T(8,128)}, f32[32,128]{1,0:T(8,128)}) custom-call(s32[8,2048]{1,0:T(8,128)} %bitcast.62, s32[1,2048]{1,0:T(1,128)} %get-tuple-element.257.t_ids, s32[1,768]{1,0:T(1,128)} %slice.233.n_ids, s32[16,128]{1,0:T(8,128)} %bitcast.81, bf16[2048,256]{1,0:T(8,128)(2,1)} %get-tuple-element.222.gq_ref, ...), custom_call_target="tpu_custom_call" | custom-call | tf_op jit(solution)/shard_map/scatter_rows/pallas_call | solution.py:427
  1284.7 82.2 %update.15 = (f32[16384,128]{1,0:T(8,128)}, f32[2048,128]{1,0:T(8,128)}, f32[32,128]{1,0:T(8,128)}, f32[16,128]{1,0:T(8,128)}) custom-call(f32[16384,128]{1,0:T(8,128)} %get-tuple-element.227.acc_in, f32[16384,128]{1,0:T(8,128)} %get-tuple-element.217.table.table_in, f32[2048,128]{1,0:T(8,128)} %get-tuple-element.228.state_in, ...), custom_call_target="tpu_custom_call" | custom-call | tf_op jit(solution)/shard_map/update/pallas_call | solution.py:438
  1386.4 36.7 %all-gather = f32[8192,1]{1,0:T(8,128)} all-gather(f32[2048,1]{1,0:T(8,128)S(1)} %bitcast.72), channel_id=2, replica_groups=mesh['sweep'=1,'data'=4,'ent'=8] {'data'}, dimensions={0}, use_global_device_ids=true | all-gather | bytes 40960 | tf_op jit(solution)/shard_map/all_gather | solution.py:451
  (78 shorter events, 264.9 us)
Async XLA Ops:
  2.2 182.2 %collective-permute-start.6 = (s32[1,4864]{1,0:T(1,128)S(1)}, s32[1,4864]{1,0:T(1,128)S(1)}, u32[]{:S(2)}, u32[]{:S(2)}) collective-permute-start(s32[1,4864]{1,0:T(1,128)S(1)} %get-tuple-element.242), channel_id=1, source_target_pairs={{0,1},{1,2},{2,3},{3,4},{4,5},{5,6},{6,7},{7,0},{8,9},{9,10},{10,1... | collective-permute-start | bytes 58376 | tf_op jit(solution)/shard_map/ppermute | solution.py:382
  4.9 181.9 %collective-permute-start.5 = (s32[1,4864]{1,0:T(1,128)S(1)}, s32[1,4864]{1,0:T(1,128)S(1)}, u32[]{:S(2)}, u32[]{:S(2)}) collective-permute-start(s32[1,4864]{1,0:T(1,128)S(1)} %get-tuple-element.243), channel_id=1, source_target_pairs={{0,2},{1,3},{2,4},{3,5},{4,6},{5,7},{6,0},{7,1},{8,10},{9,11},{10,... | collective-permute-start | bytes 58376 | tf_op jit(solution)/shard_map/ppermute | solution.py:382
  6.3 182.4 %collective-permute-start.4 = (s32[1,4864]{1,0:T(1,128)S(1)}, s32[1,4864]{1,0:T(1,128)S(1)}, u32[]{:S(2)}, u32[]{:S(2)}) collective-permute-start(s32[1,4864]{1,0:T(1,128)S(1)} %get-tuple-element.244), channel_id=1, source_target_pairs={{0,3},{1,4},{2,5},{3,6},{4,7},{5,0},{6,1},{7,2},{8,11},{9,12},{10,... | collective-permute-start | bytes 58376 | tf_op jit(solution)/shard_map/ppermute | solution.py:382
  8.0 181.3 %collective-permute-start.3 = (s32[1,4864]{1,0:T(1,128)S(1)}, s32[1,4864]{1,0:T(1,128)S(1)}, u32[]{:S(2)}, u32[]{:S(2)}) collective-permute-start(s32[1,4864]{1,0:T(1,128)S(1)} %get-tuple-element.245), channel_id=1, source_target_pairs={{0,4},{1,5},{2,6},{3,7},{4,0},{5,1},{6,2},{7,3},{8,12},{9,13},{10,... | collective-permute-start | bytes 58376 | tf_op jit(solution)/shard_map/ppermute | solution.py:382
  8.3 181.6 %collective-permute-start.2 = (s32[1,4864]{1,0:T(1,128)S(1)}, s32[1,4864]{1,0:T(1,128)S(1)}, u32[]{:S(2)}, u32[]{:S(2)}) collective-permute-start(s32[1,4864]{1,0:T(1,128)S(1)} %get-tuple-element.246), channel_id=1, source_target_pairs={{0,5},{1,6},{2,7},{3,0},{4,1},{5,2},{6,3},{7,4},{8,13},{9,14},{10,... | collective-permute-start | bytes 58376 | tf_op jit(solution)/shard_map/ppermute | solution.py:382
  36.9 8.1 copy-start.1
  74.5 22.9 %dynamic-slice-start = ((f32[8192]{0:T(1024)}, s32[]{:T(128)}), f32[2048]{0:T(1024)S(1)}, s32[]{:S(2)}) async-start(f32[8192]{0:T(1024)} %param.9, s32[]{:T(128)} %select_n.17), calls=%async_computation | async-start | bytes 16896 | tf_op jit(solution)/shard_map/dynamic_slice | solution.py:391
  184.4 6.1 collective-permute-start.1
  186.8 973.5 %collective-permute-start = (s32[1,4864]{1,0:T(1,128)S(1)}, s32[1,4864]{1,0:T(1,128)S(1)}, u32[]{:S(2)}, u32[]{:S(2)}) collective-permute-start(s32[1,4864]{1,0:T(1,128)S(1)} %pad_add_fusion.7), channel_id=1, source_target_pairs={{0,7},{1,0},{2,1},{3,2},{4,3},{5,4},{6,5},{7,6},{8,15},{9,8},{10,9... | collective-permute-start | bytes 58376 | tf_op jit(solution)/shard_map/ppermute | solution.py:382
  1379.9 6.5 copy-start
  1386.4 36.7 %copy-start.2 = (f32[32,128]{1,0:T(8,128)S(1)}, f32[32,128]{1,0:T(8,128)}, u32[]{:S(2)}) copy-start(f32[32,128]{1,0:T(8,128)} %get-tuple-element.233) | copy-start | bytes 49156

commit v2 on v1

v2 whole, which is shorter than its diff:
```python
import functools

import jax
import jax.numpy as jnp
from jax import lax
from jax.experimental import pallas as pl
from jax.experimental.pallas import tpu as pltpu
from jax.sharding import PartitionSpec as P

LR_SCALE = 0.2
EPSILON = 1e-8
LANES = 128
EDGE_BLOCK = 256
GATHER_UNROLL = 16
SYNC_CHUNKS = 2
VMEM_LIMIT = 60 * 1024 * 1024
MESH = pl.DeviceIdType.MESH
VM = pltpu.VMEM
F32 = jnp.float32
BF16 = jnp.bfloat16


def interleave(table):
    rows, width = table.shape
    half = width // 2
    return jnp.pad(table.reshape(rows, 2, half), ((0, 0), (0, 0), (0, LANES - half))).reshape(rows * 2, LANES)


def deinterleave(table, width):
    rows = table.shape[0] // 2
    return table.reshape(rows, 2, LANES)[:, :, :width // 2].reshape(rows, width)


def pair(row):
    return pl.ds(pl.multiple_of(row * 2, 2), 2)


def load_kernel(half, table_t, table, staged):
    width, cols = table_t.shape
    staged[0:width, :] = table_t[...]
    staged[width:2 * LANES, :] = jnp.zeros((2 * LANES - width, cols), F32)
    lane = lax.broadcasted_iota(jnp.int32, (LANES, LANES), 1)
    for at in range(0, cols, LANES):
        low = staged[0:LANES, at:at + LANES].T
        high = staged[LANES:2 * LANES, at:at + LANES].T
        table[pl.ds(2 * at, LANES, stride=2), :] = jnp.where(lane < half, low, 0.0)
        moved = jnp.where(lane < LANES - half, pltpu.roll(low, LANES - half, 1), pltpu.roll(high, LANES - half, 1))
        table[pl.ds(2 * at + 1, LANES, stride=2), :] = jnp.where(lane < half, moved, 0.0)


def store_kernel(half, table, table_t):
    width, cols = table_t.shape
    lane = lax.broadcasted_iota(jnp.int32, (LANES, LANES), 1)
    for at in range(0, cols, LANES):
        re = table[pl.ds(2 * at, LANES, stride=2), :]
        moved = pltpu.roll(table[pl.ds(2 * at + 1, LANES, stride=2), :], half, 1)
        table_t[0:LANES, at:at + LANES] = jnp.where(lane < half, re, moved).T
        table_t[LANES:width, at:at + LANES] = moved.T[0:width - LANES, :]


def bucket_kernel(shift, group, h_ids, r_ids, tail_ids, table, rel, r_vec, tail_vec,
                  gh_ref, gt_ref, gn_ref, grel_ref, loss_ref,
                  h_rows, r_rows, t_rows, n_rows, q_own, n_bf, gn_acc, *scratch):
    edges = q_own.shape[0]
    negs = n_bf.shape[0]
    rel_pad = grel_ref.shape[0] // 2
    steps = edges // EDGE_BLOCK

    def block(step):
        return pl.ds(pl.multiple_of(step * EDGE_BLOCK, EDGE_BLOCK), EDGE_BLOCK)

    def halves(base, count):
        return pl.ds(pl.multiple_of(2 * base, 2), count, stride=2), pl.ds(2 * base + 1, count, stride=2)

    if shift:
        q_got, gq_send, gq_got, loss_send, q_sems, gq_sems, loss_sems = scratch
        me = lax.axis_index('ent')
        ahead = lax.rem(me + shift, group)
        behind = lax.rem(me + group - shift, group)

        def q_copy(step):
            return pltpu.make_async_remote_copy(
                src_ref=q_own.at[block(step), :], dst_ref=q_got.at[block(step), :],
                send_sem=q_sems.at[0, step], recv_sem=q_sems.at[1, step],
                device_id={'ent': ahead}, device_id_type=MESH)

        def gq_copy(step):
            return pltpu.make_async_remote_copy(
                src_ref=gq_send.at[block(step), :], dst_ref=gq_got.at[block(step), :],
                send_sem=gq_sems.at[0, step], recv_sem=gq_sems.at[1, step],
                device_id={'ent': behind}, device_id_type=MESH)

        barrier = pltpu.get_barrier_semaphore()
        pl.semaphore_signal(barrier, inc=1, device_id={'ent': ahead}, device_id_type=MESH)
        pl.semaphore_signal(barrier, inc=1, device_id={'ent': behind}, device_id_type=MESH)
        pl.semaphore_wait(barrier, 2)
        q_src, gq_src, gq_dst = q_got, gq_got, gq_send
    else:
        gq_got, = scratch
        q_src, gq_src, gq_dst = q_own, gq_got, gq_got

    def ask(step, _):
        def gather(part, _):
            base = step * EDGE_BLOCK + part * GATHER_UNROLL
            for off in range(GATHER_UNROLL):
                at = base + off
                h_rows[pair(at), :] = table[h_ids[shift, at]]
                r_rows[pair(at), :] = rel[r_ids[shift, at]]
            return 0

        lax.fori_loop(0, EDGE_BLOCK // GATHER_UNROLL, gather, 0)
        rows = block(step)
        even, odd = halves(step * EDGE_BLOCK, EDGE_BLOCK)
        re_h, im_h = h_rows[even, :], h_rows[odd, :]
        re_r, im_r = r_rows[even, :], r_rows[odd, :]
        q_own[rows, 0:LANES] = (re_h * re_r - im_h * im_r).astype(BF16)
        q_own[rows, LANES:2 * LANES] = (re_h * im_r + im_h * re_r).astype(BF16)
        if shift:
            q_copy(step).start()
        return 0

    lax.fori_loop(0, steps, ask, 0)

    def gather_negs(part, _):
        for off in range(GATHER_UNROLL):
            at = part * GATHER_UNROLL + off
            n_rows[pair(at), :] = table[tail_ids[0, 2 * edges + at]]
        return 0

    lax.fori_loop(0, negs // GATHER_UNROLL, gather_negs, 0)
    n_even, n_odd = halves(0, negs)
    n_bf[:, 0:LANES] = n_rows[n_even, :].astype(BF16)
    n_bf[:, LANES:2 * LANES] = n_rows[n_odd, :].astype(BF16)

    def gather_tails(part, _):
        for off in range(GATHER_UNROLL):
            at = part * GATHER_UNROLL + off
            t_rows[pair(at), :] = table[tail_ids[0, at]]
        return 0

    lax.fori_loop(0, edges // GATHER_UNROLL, gather_tails, 0)

    gn_acc[...] = jnp.zeros_like(gn_acc)
    eye = lax.broadcasted_iota(jnp.int32, (LANES, LANES), 0) == lax.broadcasted_iota(jnp.int32, (LANES, LANES), 1)
    per_block = EDGE_BLOCK // LANES

    def answer(step, loss_acc):
        if shift:
            q_copy(step).wait_recv()
        rows = block(step)
        even, odd = halves(step * EDGE_BLOCK, EDGE_BLOCK)
        q = q_src[rows, :]
        t = jnp.concatenate([t_rows[even, :].astype(BF16), t_rows[odd, :].astype(BF16)], axis=1).astype(F32)
        q_wide = q.astype(F32)
        n = n_bf[...]
        masks = [tail_vec[0:1, pl.ds(pl.multiple_of(edges + step * EDGE_BLOCK + k * LANES, LANES), LANES)].astype(F32) for k in range(per_block)]
        w = jnp.concatenate([jnp.sum(jnp.where(eye, mask, 0.0), axis=1, keepdims=True) for mask in masks], axis=0)
        pos = jnp.sum(q_wide * t, axis=1, keepdims=True)
        score = lax.dot_general(q, n, (((1,), (1,)), ((), ())), preferred_element_type=F32)
        top = jnp.maximum(jnp.max(score, axis=1, keepdims=True), pos)
        pos_exp = jnp.exp(pos - top)
        neg_exp = jnp.exp(score - top)
        total = pos_exp + jnp.sum(neg_exp, axis=1, keepdims=True)
        loss_acc = loss_acc + jnp.sum(w * (top + jnp.log(total) - pos), axis=0, keepdims=True)
        d_pos = w * (pos_exp / total - 1.0)
        d_neg = ((w / total) * neg_exp).astype(BF16)
        gq_dst[rows, :] = (d_pos * t + jnp.dot(d_neg, n, preferred_element_type=F32)).astype(gq_dst.dtype)
        g_tail = d_pos * q_wide
        gt_ref[even, :] = g_tail[:, 0:LANES]
        gt_ref[odd, :] = g_tail[:, LANES:2 * LANES]
        gn_acc[...] += lax.dot_general(q, d_neg, (((0,), (0,)), ((), ())), preferred_element_type=F32)
        if shift:
            gq_copy(step).start()
        return loss_acc

    loss = lax.fori_loop(0, steps, answer, jnp.zeros((1, 1), F32))
    if shift:
        loss_send[...] = jnp.broadcast_to(loss, loss_send.shape)
        loss_copy = pltpu.make_async_remote_copy(
            src_ref=loss_send, dst_ref=loss_ref, send_sem=loss_sems.at[0], recv_sem=loss_sems.at[1],
            device_id={'ent': behind}, device_id_type=MESH)
        loss_copy.start()
    else:
        loss_ref[...] = jnp.broadcast_to(loss, loss_ref.shape)
    for half in range(2):
        gn_ref[pl.ds(half, negs, stride=2), :] = gn_acc[half * LANES:(half + 1) * LANES, :].T

    def finish(step, carry):
        rel_re, rel_im = carry
        if shift:
            gq_copy(step).wait_recv()
        rows = block(step)
        even, odd = halves(step * EDGE_BLOCK, EDGE_BLOCK)
        re_g, im_g = gq_src[rows, 0:LANES].astype(F32), gq_src[rows, LANES:2 * LANES].astype(F32)
        re_r, im_r = r_rows[even, :], r_rows[odd, :]
        gh_ref[even, :] = re_g * re_r + im_g * im_r
        gh_ref[odd, :] = im_g * re_r - re_g * im_r
        re_h, im_h = h_rows[even, :], h_rows[odd, :]
        ids = r_vec[shift:shift + 1, pl.ds(pl.multiple_of(step * EDGE_BLOCK, EDGE_BLOCK), EDGE_BLOCK)]
        hot = (lax.broadcasted_iota(jnp.int32, (rel_pad, EDGE_BLOCK), 0) == ids).astype(F32)
        rel_re = rel_re + jnp.dot(hot, re_g * re_h + im_g * im_h, precision=lax.Precision.HIGHEST, preferred_element_type=F32)
        rel_im = rel_im + jnp.dot(hot, im_g * re_h - re_g * im_h, precision=lax.Precision.HIGHEST, preferred_element_type=F32)
        return rel_re, rel_im

    zero = jnp.zeros((rel_pad, LANES), F32)
    rel_re, rel_im = lax.fori_loop(0, steps, finish, (zero, zero))
    grel_ref[pl.ds(0, rel_pad, stride=2), :] = rel_re
    grel_ref[pl.ds(1, rel_pad, stride=2), :] = rel_im
    if shift:
        loss_copy.wait()

        def drain(step, _):
            q_copy(step).wait_send()
            gq_copy(step).wait_send()
            return 0

        lax.fori_loop(0, steps, drain, 0)


def scatter_kernel(shift, h_ids, tail_ids, gh, gt_ref, gn_ref, acc, acc_b, acc_c, acc_d):
    edges = gh.shape[0] // 2
    negs = gn_ref.shape[0] // 2
    table_rows = acc.shape[0]

    zero_rows = 512

    def clear(step, _):
        rows = pl.ds(pl.multiple_of(step * zero_rows, zero_rows), zero_rows)
        for ref in (acc, acc_b, acc_c, acc_d):
            ref[rows, :] = jnp.zeros((zero_rows, LANES), F32)
        return 0

    lax.fori_loop(0, table_rows // zero_rows, clear, 0)

    def add_edges(step, _):
        base = step * GATHER_UNROLL
        for off in range(0, GATHER_UNROLL, 2):
            at = base + off
            places = (pair(h_ids[shift, at]), pair(h_ids[shift, at + 1]), pair(tail_ids[0, at]), pair(tail_ids[0, at + 1]))
            refs = (acc, acc_b, acc_c, acc_d)
            terms = (gh[pair(at), :], gh[pair(at + 1), :], gt_ref[pair(at), :], gt_ref[pair(at + 1), :])
            sums = [ref[place, :] + term for ref, place, term in zip(refs, places, terms)]
            for ref, place, total in zip(refs, places, sums):
                ref[place, :] = total
        return 0

    lax.fori_loop(0, edges // GATHER_UNROLL, add_edges, 0)

    def add_negs(step, _):
        base = step * GATHER_UNROLL
        for off in range(0, GATHER_UNROLL, 4):
            at = base + off
            places = [pair(tail_ids[0, 2 * edges + at + k]) for k in range(4)]
            refs = (acc, acc_b, acc_c, acc_d)
            sums = [ref[place, :] + gn_ref[pair(at + k), :] for k, (ref, place) in enumerate(zip(refs, places))]
            for ref, place, total in zip(refs, places, sums):
                ref[place, :] = total
        return 0

    lax.fori_loop(0, negs // GATHER_UNROLL, add_negs, 0)

    def combine(step, _):
        rows = pl.ds(pl.multiple_of(step * zero_rows, zero_rows), zero_rows)
        acc[rows, :] = (acc[rows, :] + acc_b[rows, :]) + (acc_c[rows, :] + acc_d[rows, :])
        return 0

    lax.fori_loop(0, table_rows // zero_rows, combine, 0)


def update_kernel(width, learn_rate, groups, reps, shift, bucket_edges, acc_in, table_in, state_in, grel_in, rel_in, rel_state_in, loss_in, losses_in,
                  table_out, state_out, rel_out, rel_state_out, losses_out, state_all,
                  first_send, first_got, plain_send, plain_got, merged_send, merged_got, work,
                  step_own, step_got, step_far, rel_x, rel_y, rel_send, rel_send_y, state_own,
                  first_sems, plain_sems, merged_sems, own_sems, far_sems, rel_x_sems, rel_y_sems, state_sems):
    me = lax.axis_index('data')
    ent = lax.axis_index('ent')
    peers = (lax.rem(me + 1, reps), lax.rem(me + reps - 1, reps))
    far = lax.rem(me + 2, reps)
    quarter = acc_in.shape[0] // reps
    half = quarter // 2
    chunk = half // SYNC_CHUNKS

    barrier = pltpu.get_barrier_semaphore()
    for off in range(1, reps):
        pl.semaphore_signal(barrier, inc=1, device_id={'data': lax.rem(me + off, reps)}, device_id_type=MESH)
    for off in range(1, groups):
        pl.semaphore_signal(barrier, inc=1, device_id={'ent': lax.rem(ent + off, groups)}, device_id_type=MESH)
    pl.semaphore_wait(barrier, reps + groups - 2)

    def remote(src, dst, sems, place, to):
        return pltpu.make_async_remote_copy(
            src_ref=src, dst_ref=dst, send_sem=sems.at[(0,) + place], recv_sem=sems.at[(1,) + place],
            device_id=to, device_id_type=MESH)

    rel_x[0] = grel_in[...]
    rel_send[...] = grel_in[...]
    x_copies = [remote(rel_send, rel_x.at[off], rel_x_sems, (off - 1,), {'ent': lax.rem(ent + off, groups)}) for off in range(1, groups)]
    for copy in x_copies:
        copy.start()

    def rows_of(owner, which, k):
        return pl.ds(pl.multiple_of(owner * quarter + which * half + k * chunk, chunk), chunk)

    def at_chunk(k):
        return pl.ds(k * chunk, chunk)

    first, plain, merged = {}, {}, {}
    for k in range(SYNC_CHUNKS):
        for side in range(2):
            first_send[side, at_chunk(k), :] = acc_in[rows_of(far, side, k), :].astype(BF16)
            first[side, k] = remote(first_send.at[side, at_chunk(k), :], first_got.at[side, at_chunk(k), :], first_sems, (side, k), {'data': peers[side]})
            first[side, k].start()
    for k in range(SYNC_CHUNKS):
        for side in range(2):
            plain_send[side, at_chunk(k), :] = acc_in[rows_of(peers[side], 1 - side, k), :].astype(BF16)
            plain[side, k] = remote(plain_send.at[side, at_chunk(k), :], plain_got.at[side, at_chunk(k), :], plain_sems, (side, k), {'data': peers[side]})
            plain[side, k].start()
    for k in range(SYNC_CHUNKS):
        for side in range(2):
            first[side, k].wait_recv()
            merged_send[side, at_chunk(k), :] = (first_got[side, at_chunk(k), :].astype(F32) + acc_in[rows_of(peers[side], side, k), :]).astype(BF16)
            merged[side, k] = remote(merged_send.at[side, at_chunk(k), :], merged_got.at[side, at_chunk(k), :], merged_sems, (side, k), {'data': peers[side]})
            merged[side, k].start()

    for copy in x_copies:
        copy.wait()
    total = rel_x[lax.rem(ent, groups)]
    for src in range(1, groups):
        total = total + rel_x[lax.rem(ent + groups - src, groups)]
    span = total.shape[0]
    rel_send_y[0:span, :] = total
    rel_send_y[span:, :] = loss_in[...]
    rel_y[0] = rel_send_y[...]
    y_copies = [remote(rel_send_y, rel_y.at[off], rel_y_sems, (off - 1,), {'data': lax.rem(me + off, reps)}) for off in range(1, reps)]
    for copy in y_copies:
        copy.start()

    own = {}
    for k in range(SYNC_CHUNKS):
        for which in range(2):
            merged[which, k].wait_recv()
            plain[1 - which, k].wait_recv()
            work[...] = acc_in[rows_of(me, which, k), :] + (merged_got[which, at_chunk(k), :].astype(F32) + plain_got[1 - which, at_chunk(k), :].astype(F32))
            n = chunk // 2
            re_g, im_g = work[pl.ds(0, n, stride=2), :], work[pl.ds(1, n, stride=2), :]
            places = pl.ds(which * (half // 2) + k * n, n)
            state = state_in[places, :] + jnp.sum(re_g * re_g + im_g * im_g, axis=1, keepdims=True) / width
            state_out[places, :] = state
            scale = learn_rate / jnp.sqrt(state + EPSILON)
            work[pl.ds(0, n, stride=2), :] = re_g * scale
            work[pl.ds(1, n, stride=2), :] = im_g * scale
            step_own[which, at_chunk(k), :] = work[...].astype(BF16)
            for side in range(2):
                own[side, which, k] = remote(step_own.at[which, at_chunk(k), :], step_got.at[side, which, at_chunk(k), :], own_sems, (side, which, k), {'data': peers[side]})
                own[side, which, k].start()

    spread = {}
    for k in range(SYNC_CHUNKS):
        for which in range(2):
            for side in range(2):
                own[side, which, k].wait_recv()
                if side == which:
                    spread[side, k] = remote(step_got.at[side, which, at_chunk(k), :], step_far.at[side, at_chunk(k), :], far_sems, (side, k), {'data': peers[side]})
                    spread[side, k].start()
            for owner, ref in ((me, step_own.at[which]), (peers[1], step_got.at[0, which]), (peers[0], step_got.at[1, which])):
                rows = rows_of(owner, which, k)
                table_out[rows, :] = table_in[rows, :] - ref[at_chunk(k), :].astype(F32)

    for copy in y_copies:
        copy.wait()
    total = rel_y[lax.rem(me, reps)]
    for src in range(1, reps):
        total = total + rel_y[lax.rem(me + reps - src, reps)]
    losses_out[...] = jnp.where(lax.broadcasted_iota(jnp.int32, losses_in.shape, 0) == shift, total[span:, :] / bucket_edges, losses_in[...])
    rel_send[...] = total[0:span, :]
    rel_rows = rel_send.shape[0] // 2
    re_g, im_g = rel_send[pl.ds(0, rel_rows, stride=2), :], rel_send[pl.ds(1, rel_rows, stride=2), :]
    state = rel_state_in[...] + jnp.sum(re_g * re_g + im_g * im_g, axis=1, keepdims=True) / width
    rel_state_out[...] = state
    scale = learn_rate / jnp.sqrt(state + EPSILON)
    rel_out[pl.ds(0, rel_rows, stride=2), :] = rel_in[pl.ds(0, rel_rows, stride=2), :] - re_g * scale
    rel_out[pl.ds(1, rel_rows, stride=2), :] = rel_in[pl.ds(1, rel_rows, stride=2), :] - im_g * scale

    state_copies = []
    if shift == groups - 1:
        eye = lax.broadcasted_iota(jnp.int32, (LANES, LANES), 0) == lax.broadcasted_iota(jnp.int32, (LANES, LANES), 1)
        blocks = state_own.shape[0]
        for at in range(blocks):
            state_own[at:at + 1, :] = jnp.sum(jnp.where(eye, state_out[at * LANES:(at + 1) * LANES, :], 0.0), axis=0, keepdims=True)
        place = pl.ds(pl.multiple_of(me * blocks, blocks), blocks)
        state_all[place, :] = state_own[...]
        state_copies = [remote(state_own, state_all.at[place, :], state_sems, (off - 1,), {'data': lax.rem(me + off, reps)}) for off in range(1, reps)]
        for copy in state_copies:
            copy.start()
    else:
        state_all[...] = jnp.zeros_like(state_all)

    for k in range(SYNC_CHUNKS):
        for side in range(2):
            spread[side, k].wait_recv()
            rows = rows_of(far, side, k)
            table_out[rows, :] = table_in[rows, :] - step_far[side, at_chunk(k), :].astype(F32)
    for group_of in (first, plain, merged, own, spread):
        for copy in group_of.values():
            copy.wait_send()
    for copy in state_copies:
        copy.wait()


def solution(mesh):
    groups = mesh.shape['ent']
    reps = mesh.shape['data']
    row_spec = P(('sweep', 'ent'), None)
    edge_spec = P(('sweep', 'ent'), None, 'data')
    vmem = pl.BlockSpec(memory_space=VM)

    def device_fn(ent_table, ent_state, rel_table, head_idx, tail_idx, rel_idx, edge_mask, neg_idx):
        part_rows, width = ent_table.shape
        rel_count = rel_table.shape[0]
        edges = head_idx.shape[2]
        negs = neg_idx.shape[2]
        bucket_edges = edges * reps
        learn_rate = LR_SCALE * width ** -0.25
        rel_pad = -(-rel_count // 8) * 8
        quarter = part_rows // reps
        me = lax.axis_index('data')

        packed = jnp.concatenate([tail_idx[0], edge_mask[0], neg_idx[0]], axis=1)
        moved = [packed[0:1]]
        for shift in range(1, groups):
            moved.append(lax.ppermute(packed[shift:shift + 1], 'ent', [(src, (src + shift) % groups) for src in range(groups)]))

        h_all = head_idx[0]
        r_all = rel_idx[0]
        row_grid = 8
        params = pltpu.CompilerParams(vmem_limit_bytes=VMEM_LIMIT)
        table = pl.pallas_call(
            functools.partial(load_kernel, width // 2), grid=(row_grid,),
            out_shape=jax.ShapeDtypeStruct((2 * part_rows, LANES), F32),
            in_specs=[pl.BlockSpec((width, part_rows // row_grid), lambda i: (0, i))],
            out_specs=pl.BlockSpec((2 * part_rows // row_grid, LANES), lambda i: (i, 0)),
            scratch_shapes=[VM((2 * LANES, part_rows // row_grid), F32)], name='load_table')(ent_table.T)
        rel = interleave(jnp.pad(rel_table, ((0, rel_pad - rel_count), (0, 0))))
        rel_state = jnp.zeros((rel_pad, LANES), F32)
        state = jnp.broadcast_to(lax.dynamic_slice_in_dim(ent_state, me * quarter, quarter)[:, None], (quarter, LANES))
        losses = jnp.zeros((-(-groups // 8) * 8, LANES), F32)

        smem = pl.BlockSpec(memory_space=pltpu.SMEM)
        sems = pltpu.SemaphoreType.DMA
        steps = edges // EDGE_BLOCK
        for shift in range(groups):
            tail = moved[shift]
            scratch = [VM((2 * edges, LANES), F32)] * 3 + [VM((2 * negs, LANES), F32), VM((edges, 2 * LANES), BF16),
                                                         VM((negs, 2 * LANES), BF16), VM((2 * LANES, negs), F32)]
            if shift:
                scratch += [VM((edges, 2 * LANES), BF16)] * 3 + [VM(losses.shape, F32), sems((2, steps)), sems((2, steps)), sems((2,))]
            else:
                scratch += [VM((edges, 2 * LANES), F32)]
            g_h, g_t, g_n, g_rel, loss = pl.pallas_call(
                functools.partial(bucket_kernel, shift, groups),
                out_shape=[jax.ShapeDtypeStruct((2 * edges, LANES), F32)] * 2
                + [jax.ShapeDtypeStruct((2 * negs, LANES), F32), jax.ShapeDtypeStruct((2 * rel_pad, LANES), F32), jax.ShapeDtypeStruct(losses.shape, F32)],
                in_specs=[smem] * 3 + [vmem] * 4, out_specs=[vmem] * 5, scratch_shapes=scratch,
                compiler_params=pltpu.CompilerParams(vmem_limit_bytes=VMEM_LIMIT, collective_id=0, has_side_effects=True) if shift else params,
                name='bucket',
            )(h_all, r_all, tail, table.reshape(part_rows, 2, LANES), rel.reshape(rel_pad, 2, LANES), r_all, tail)

            acc = pl.pallas_call(
                functools.partial(scatter_kernel, shift),
                out_shape=jax.ShapeDtypeStruct((2 * part_rows, LANES), F32),
                in_specs=[smem] * 2 + [vmem] * 3, out_specs=vmem,
                scratch_shapes=[VM((2 * part_rows, LANES), F32)] * 3,
                compiler_params=params, name='scatter_rows',
            )(h_all, tail, g_h, g_t, g_n)

            half = (2 * part_rows) // reps // 2
            block = VM((2, half, LANES), BF16)
            state_blocks = quarter // LANES
            table, state, rel, rel_state, losses, state_all = pl.pallas_call(
                functools.partial(update_kernel, width, learn_rate, groups, reps, shift, bucket_edges),
                out_shape=[jax.ShapeDtypeStruct(table.shape, F32), jax.ShapeDtypeStruct(state.shape, F32),
                           jax.ShapeDtypeStruct(rel.shape, F32), jax.ShapeDtypeStruct(rel_state.shape, F32),
                           jax.ShapeDtypeStruct(losses.shape, F32), jax.ShapeDtypeStruct((reps * state_blocks, LANES), F32)],
                in_specs=[vmem] * 8, out_specs=[vmem] * 6,
                scratch_shapes=[block] * 6 + [VM((half // SYNC_CHUNKS, LANES), F32), block, VM((2, 2, half, LANES), BF16), block,
                                              VM((groups, 2 * rel_pad, LANES), F32), VM((reps, 2 * rel_pad + losses.shape[0], LANES), F32), VM((2 * rel_pad, LANES), F32),
                                              VM((2 * rel_pad + losses.shape[0], LANES), F32), VM((state_blocks, LANES), F32),
                                              sems((2, 2, SYNC_CHUNKS)), sems((2, 2, SYNC_CHUNKS)), sems((2, 2, SYNC_CHUNKS)),
                                              sems((2, 2, 2, SYNC_CHUNKS)), sems((2, 2, SYNC_CHUNKS)), sems((2, groups - 1)), sems((2, reps - 1)), sems((2, reps - 1))],
                compiler_params=pltpu.CompilerParams(vmem_limit_bytes=VMEM_LIMIT, collective_id=1, has_side_effects=True), name='update',
            )(acc, table, state, g_rel, rel, rel_state, loss, losses)

        ent_out = pl.pallas_call(
            functools.partial(store_kernel, width // 2), grid=(row_grid,),
            out_shape=jax.ShapeDtypeStruct((width, part_rows), F32),
            in_specs=[pl.BlockSpec((2 * part_rows // row_grid, LANES), lambda i: (i, 0))],
            out_specs=pl.BlockSpec((width, part_rows // row_grid), lambda i: (0, i)), name='store_table')(table).T
        rel_out = deinterleave(rel, width)[:rel_count]
        return ent_out, state_all.reshape(part_rows), rel_out, losses[:groups, 0].reshape(1, groups)

    return jax.shard_map(device_fn, mesh=mesh, in_specs=(row_spec, P(('sweep', 'ent')), P('sweep', None), edge_spec, edge_spec, edge_spec, edge_spec, P(('sweep', 'ent'), None, None)), out_specs=(row_spec, P(('sweep', 'ent')), P('sweep', None), row_spec), check_vma=False)
```

time: 1440 us -> 1190 us (0.83)
  Pallas kernels: 1250 us -> 1160 us
  blocking collectives: 82.7 us -> 0 us
  local copies, waits for them, and re-layouts: 74.7 us -> 9.51 us
    pallas_call x16 -> x10, Pallas kernels: 318 us -> 164 us  [the longest x8 144 us: device_fn(): pl.pallas_call(functools.partial(scatter_kernel, shift), out_shape=jax.Sh...]
    pallas_call x8, Pallas kernels: 261 us -> 328 us  [device_fn(): pl.pallas_call(functools.partial(bucket_kernel, shift, groups), out_shape...]
    psum x1 -> x0, blocking collectives: 46 us -> none  [device_fn(): bucket_loss = lax.psum(spread, ('data', 'ent'))]
    all_gather x1 -> x0, blocking collectives: 36.7 us -> none  [device_fn(): state_out = lax.all_gather(state[:, 0], 'data', tiled=True)]
    unnamed x8 -> x21, local copies, waits for them, and re-layouts: 25.9 us -> 3.64 us
    slice x18 -> x2, local copies, waits for them, and re-layouts: 18.6 us -> 1.26 us  [the longest x1 0.63 us: device_fn(): moved = [packed[0:1]]]
  transfers between devices with their start and end apart: 7 -> 7, of which waited for: 0 -> 0; matrix products, arithmetic and copies ran while one was open for 3% -> 0% of each run, Pallas kernels for 77% -> 86%
where the time goes in v2:
time: 1190 us; the launch traced here: 1180 us
  Pallas kernels  1160 us (97%)
    pallas_call x8, Pallas kernels, device_fn(): pl.pallas_call(functools.partial(update_kernel, width, learn_rate, groups...  670 us
    pallas_call x8, Pallas kernels, device_fn(): pl.pallas_call(functools.partial(bucket_kernel, shift, groups), out_shape...  328 us
    pallas_call x8, Pallas kernels, device_fn(): pl.pallas_call(functools.partial(scatter_kernel, shift), out_shape=jax.Sh...  144 us
  transfers between devices with their start and end apart: 7, of which 0 were waited for; matrix products, arithmetic and copies ran while one was open for 0% of the time, Pallas kernels for 86%

profile of v2, /device:TPU:97, one launch (start us, length us, event | category | flops | bytes accessed | tf_op | source)
XLA Modules:
  0.0 1184.4 jit_solution(5358904928267464945)
XLA Ops:
  24.0 26.7 %bucket.8 = (f32[4096,128]{1,0:T(8,128)}, f32[4096,128]{1,0:T(8,128)}, f32[1536,128]{1,0:T(8,128)}, f32[32,128]{1,0:T(8,128)}, f32[8,128]{1,0:T(8,128)}) custom-call(s32[8,2048]{1,0:T(8,128)} %bitcast.50, s32[8,2048]{1,0:T(8,128)} %bitcast.34, s32[1,4864]{1,0:T(1,128)} %get-tuple-element.162.tail_ids.tail_vec, f32[8192,2,128]{2,1,0:T(2,128)} %bitcast.26, ...), custom_call_target="tpu_custom_call" | custom-call | tf_op jit(solution)/shard_map/bucket/pallas_call | solution.py:459
  50.8 17.5 %scatter_rows.8.acc_in = f32[16384,128]{1,0:T(8,128)} custom-call(s32[8,2048]{1,0:T(8,128)} %bitcast.51, s32[1,4864]{1,0:T(1,128)} %get-tuple-element.162.tail_ids.tail_vec, f32[4096,128]{1,0:T(8,128)} %get-tuple-element.83.gh, f32[4096,128]{1,0:T(8,128)} %get-tuple-element.84.gt_ref, f32[1536,128]{1,0:T(8,128)} %get-tuple-element.85.gn_ref), custom_call_target="tpu_custom_call" | custom-call | tf_op jit(solution)/shard_map/scatter_rows/pallas_call | solution.py:468
  70.8 85.1 %update.8 = (f32[16384,128]{1,0:T(8,128)}, f32[2048,128]{1,0:T(8,128)}, f32[32,128]{1,0:T(8,128)}, f32[16,128]{1,0:T(8,128)}, f32[8,128]{1,0:T(8,128)}, /*index=5*/f32[64,128]{1,0:T(8,128)}) custom-call(f32[16384,128]{1,0:T(8,128)} %scatter_rows.8.acc_in, f32[16384,128]{1,0:T(8,128)} %load_table.1.table_in, f32[2048,128]{1,0:T(8,128)} %broadcast_in_dim.12.state_in, ...), custom_call_target="tpu_custom_call" | custom-call | tf_op jit(solution)/shard_map/update/pallas_call | solution.py:479
  155.9 33.3 %bucket.9 = (f32[4096,128]{1,0:T(8,128)}, f32[4096,128]{1,0:T(8,128)}, f32[1536,128]{1,0:T(8,128)}, f32[32,128]{1,0:T(8,128)}, f32[8,128]{1,0:T(8,128)}) custom-call(s32[8,2048]{1,0:T(8,128)} %bitcast.52, s32[8,2048]{1,0:T(8,128)} %bitcast.36, s32[1,4864]{1,0:T(1,128)} %copy-done.6, f32[8192,2,128]{2,1,0:T(2,128)} %bitcast.32, f32[16,2,128]{2,1,0:T(2,128)} %bitcast.74, ...), custom_call_target="tpu_custom_call" | custom-call | tf_op jit(solution)/shard_map/bucket/pallas_call | solution.py:459
  189.2 18.0 %scatter_rows.9.acc_in = f32[16384,128]{1,0:T(8,128)} custom-call(s32[8,2048]{1,0:T(8,128)} %bitcast.53, s32[1,4864]{1,0:T(1,128)} %copy-done.6, f32[4096,128]{1,0:T(8,128)} %get-tuple-element.90.gh, f32[4096,128]{1,0:T(8,128)} %get-tuple-element.91.gt_ref, f32[1536,128]{1,0:T(8,128)} %get-tuple-element.92.gn_ref), custom_call_target="tpu_custom_call" | custom-call | tf_op jit(solution)/shard_map/scatter_rows/pallas_call | solution.py:468
  207.2 82.7 %update.9 = (f32[16384,128]{1,0:T(8,128)}, f32[2048,128]{1,0:T(8,128)}, f32[32,128]{1,0:T(8,128)}, f32[16,128]{1,0:T(8,128)}, f32[8,128]{1,0:T(8,128)}, /*index=5*/f32[64,128]{1,0:T(8,128)}) custom-call(f32[16384,128]{1,0:T(8,128)} %scatter_rows.9.acc_in, f32[16384,128]{1,0:T(8,128)} %get-tuple-element.88.table_in, f32[2048,128]{1,0:T(8,128)} %get-tuple-element.93.state_in, ...), custom_call_target="tpu_custom_call" | custom-call | tf_op jit(solution)/shard_map/update/pallas_call | solution.py:479
  290.0 43.3 %bucket.10 = (f32[4096,128]{1,0:T(8,128)}, f32[4096,128]{1,0:T(8,128)}, f32[1536,128]{1,0:T(8,128)}, f32[32,128]{1,0:T(8,128)}, f32[8,128]{1,0:T(8,128)}) custom-call(s32[8,2048]{1,0:T(8,128)} %bitcast.54, s32[8,2048]{1,0:T(8,128)} %bitcast.38, s32[1,4864]{1,0:T(1,128)} %copy-done.5, f32[8192,2,128]{2,1,0:T(2,128)} %bitcast.33, f32[16,2,128]{2,1,0:T(2,128)} %bitcast.75, ...), custom_call_target="tpu_custom_call" | custom-call | tf_op jit(solution)/shard_map/bucket/pallas_call | solution.py:459
  333.2 18.0 %scatter_rows.10.acc_in = f32[16384,128]{1,0:T(8,128)} custom-call(s32[8,2048]{1,0:T(8,128)} %bitcast.55, s32[1,4864]{1,0:T(1,128)} %copy-done.5, f32[4096,128]{1,0:T(8,128)} %get-tuple-element.100.gh, f32[4096,128]{1,0:T(8,128)} %get-tuple-element.101.gt_ref, f32[1536,128]{1,0:T(8,128)} %get-tuple-element.102.gn_ref), custom_call_target="tpu_custom_call" | custom-call | tf_op jit(solution)/shard_map/scatter_rows/pallas_call | solution.py:468
  351.2 85.5 %update.10 = (f32[16384,128]{1,0:T(8,128)}, f32[2048,128]{1,0:T(8,128)}, f32[32,128]{1,0:T(8,128)}, f32[16,128]{1,0:T(8,128)}, f32[8,128]{1,0:T(8,128)}, /*index=5*/f32[64,128]{1,0:T(8,128)}) custom-call(f32[16384,128]{1,0:T(8,128)} %scatter_rows.10.acc_in, f32[16384,128]{1,0:T(8,128)} %get-tuple-element.98.table_in, ...), custom_call_target="tpu_custom_call" | custom-call | tf_op jit(solution)/shard_map/update/pallas_call | solution.py:479
  437.4 45.7 %bucket.11 = (f32[4096,128]{1,0:T(8,128)}, f32[4096,128]{1,0:T(8,128)}, f32[1536,128]{1,0:T(8,128)}, f32[32,128]{1,0:T(8,128)}, f32[8,128]{1,0:T(8,128)}) custom-call(s32[8,2048]{1,0:T(8,128)} %bitcast.56, s32[8,2048]{1,0:T(8,128)} %bitcast.40, s32[1,4864]{1,0:T(1,128)} %copy-done.4, f32[8192,2,128]{2,1,0:T(2,128)} %bitcast.27, f32[16,2,128]{2,1,0:T(2,128)} %bitcast.69, ...), custom_call_target="tpu_custom_call" | custom-call | tf_op jit(solution)/shard_map/bucket/pallas_call | solution.py:459
  483.2 18.0 %scatter_rows.11.acc_in = f32[16384,128]{1,0:T(8,128)} custom-call(s32[8,2048]{1,0:T(8,128)} %bitcast.57, s32[1,4864]{1,0:T(1,128)} %copy-done.4, f32[4096,128]{1,0:T(8,128)} %get-tuple-element.110.gh, f32[4096,128]{1,0:T(8,128)} %get-tuple-element.111.gt_ref, f32[1536,128]{1,0:T(8,128)} %get-tuple-element.112.gn_ref), custom_call_target="tpu_custom_call" | custom-call | tf_op jit(solution)/shard_map/scatter_rows/pallas_call | solution.py:468
  501.2 82.8 %update.11 = (f32[16384,128]{1,0:T(8,128)}, f32[2048,128]{1,0:T(8,128)}, f32[32,128]{1,0:T(8,128)}, f32[16,128]{1,0:T(8,128)}, f32[8,128]{1,0:T(8,128)}, /*index=5*/f32[64,128]{1,0:T(8,128)}) custom-call(f32[16384,128]{1,0:T(8,128)} %scatter_rows.11.acc_in, f32[16384,128]{1,0:T(8,128)} %get-tuple-element.108.table_in, ...), custom_call_target="tpu_custom_call" | custom-call | tf_op jit(solution)/shard_map/update/pallas_call | solution.py:479
  584.6 55.1 %bucket.12 = (f32[4096,128]{1,0:T(8,128)}, f32[4096,128]{1,0:T(8,128)}, f32[1536,128]{1,0:T(8,128)}, f32[32,128]{1,0:T(8,128)}, f32[8,128]{1,0:T(8,128)}) custom-call(s32[8,2048]{1,0:T(8,128)} %bitcast.58, s32[8,2048]{1,0:T(8,128)} %bitcast.42, s32[1,4864]{1,0:T(1,128)} %copy-done.3, f32[8192,2,128]{2,1,0:T(2,128)} %bitcast.28, f32[16,2,128]{2,1,0:T(2,128)} %bitcast.70, ...), custom_call_target="tpu_custom_call" | custom-call | tf_op jit(solution)/shard_map/bucket/pallas_call | solution.py:459
  639.7 18.2 %scatter_rows.12.acc_in = f32[16384,128]{1,0:T(8,128)} custom-call(s32[8,2048]{1,0:T(8,128)} %bitcast.59, s32[1,4864]{1,0:T(1,128)} %copy-done.3, f32[4096,128]{1,0:T(8,128)} %get-tuple-element.120.gh, f32[4096,128]{1,0:T(8,128)} %get-tuple-element.121.gt_ref, f32[1536,128]{1,0:T(8,128)} %get-tuple-element.122.gn_ref), custom_call_target="tpu_custom_call" | custom-call | tf_op jit(solution)/shard_map/scatter_rows/pallas_call | solution.py:468
  657.9 83.8 %update.12 = (f32[16384,128]{1,0:T(8,128)}, f32[2048,128]{1,0:T(8,128)}, f32[32,128]{1,0:T(8,128)}, f32[16,128]{1,0:T(8,128)}, f32[8,128]{1,0:T(8,128)}, /*index=5*/f32[64,128]{1,0:T(8,128)}) custom-call(f32[16384,128]{1,0:T(8,128)} %scatter_rows.12.acc_in, f32[16384,128]{1,0:T(8,128)} %get-tuple-element.118.table_in, ...), custom_call_target="tpu_custom_call" | custom-call | tf_op jit(solution)/shard_map/update/pallas_call | solution.py:479
  742.3 46.6 %bucket.13 = (f32[4096,128]{1,0:T(8,128)}, f32[4096,128]{1,0:T(8,128)}, f32[1536,128]{1,0:T(8,128)}, f32[32,128]{1,0:T(8,128)}, f32[8,128]{1,0:T(8,128)}) custom-call(s32[8,2048]{1,0:T(8,128)} %bitcast.60, s32[8,2048]{1,0:T(8,128)} %bitcast.44, s32[1,4864]{1,0:T(1,128)} %copy-done.2, f32[8192,2,128]{2,1,0:T(2,128)} %bitcast.29, f32[16,2,128]{2,1,0:T(2,128)} %bitcast.71, ...), custom_call_target="tpu_custom_call" | custom-call | tf_op jit(solution)/shard_map/bucket/pallas_call | solution.py:459
  788.9 18.0 %scatter_rows.13.acc_in = f32[16384,128]{1,0:T(8,128)} custom-call(s32[8,2048]{1,0:T(8,128)} %bitcast.61, s32[1,4864]{1,0:T(1,128)} %copy-done.2, f32[4096,128]{1,0:T(8,128)} %get-tuple-element.130.gh, f32[4096,128]{1,0:T(8,128)} %get-tuple-element.131.gt_ref, f32[1536,128]{1,0:T(8,128)} %get-tuple-element.132.gn_ref), custom_call_target="tpu_custom_call" | custom-call | tf_op jit(solution)/shard_map/scatter_rows/pallas_call | solution.py:468
  806.9 83.0 %update.13 = (f32[16384,128]{1,0:T(8,128)}, f32[2048,128]{1,0:T(8,128)}, f32[32,128]{1,0:T(8,128)}, f32[16,128]{1,0:T(8,128)}, f32[8,128]{1,0:T(8,128)}, /*index=5*/f32[64,128]{1,0:T(8,128)}) custom-call(f32[16384,128]{1,0:T(8,128)} %scatter_rows.13.acc_in, f32[16384,128]{1,0:T(8,128)} %get-tuple-element.128.table_in, ...), custom_call_target="tpu_custom_call" | custom-call | tf_op jit(solution)/shard_map/update/pallas_call | solution.py:479
  890.5 44.1 %bucket.14 = (f32[4096,128]{1,0:T(8,128)}, f32[4096,128]{1,0:T(8,128)}, f32[1536,128]{1,0:T(8,128)}, f32[32,128]{1,0:T(8,128)}, f32[8,128]{1,0:T(8,128)}) custom-call(s32[8,2048]{1,0:T(8,128)} %bitcast.62, s32[8,2048]{1,0:T(8,128)} %bitcast.46, s32[1,4864]{1,0:T(1,128)} %copy-done.1, f32[8192,2,128]{2,1,0:T(2,128)} %bitcast.30, f32[16,2,128]{2,1,0:T(2,128)} %bitcast.72, ...), custom_call_target="tpu_custom_call" | custom-call | tf_op jit(solution)/shard_map/bucket/pallas_call | solution.py:459
  934.6 18.3 %scatter_rows.14.acc_in = f32[16384,128]{1,0:T(8,128)} custom-call(s32[8,2048]{1,0:T(8,128)} %bitcast.63, s32[1,4864]{1,0:T(1,128)} %copy-done.1, f32[4096,128]{1,0:T(8,128)} %get-tuple-element.140.gh, f32[4096,128]{1,0:T(8,128)} %get-tuple-element.141.gt_ref, f32[1536,128]{1,0:T(8,128)} %get-tuple-element.142.gn_ref), custom_call_target="tpu_custom_call" | custom-call | tf_op jit(solution)/shard_map/scatter_rows/pallas_call | solution.py:468
  952.9 82.3 %update.14 = (f32[16384,128]{1,0:T(8,128)}, f32[2048,128]{1,0:T(8,128)}, f32[32,128]{1,0:T(8,128)}, f32[16,128]{1,0:T(8,128)}, f32[8,128]{1,0:T(8,128)}, /*index=5*/f32[64,128]{1,0:T(8,128)}) custom-call(f32[16384,128]{1,0:T(8,128)} %scatter_rows.14.acc_in, f32[16384,128]{1,0:T(8,128)} %get-tuple-element.138.table_in, ...), custom_call_target="tpu_custom_call" | custom-call | tf_op jit(solution)/shard_map/update/pallas_call | solution.py:479
  1035.8 33.1 %bucket.15 = (f32[4096,128]{1,0:T(8,128)}, f32[4096,128]{1,0:T(8,128)}, f32[1536,128]{1,0:T(8,128)}, f32[32,128]{1,0:T(8,128)}, f32[8,128]{1,0:T(8,128)}) custom-call(s32[8,2048]{1,0:T(8,128)} %bitcast.64, s32[8,2048]{1,0:T(8,128)} %bitcast.48, s32[1,4864]{1,0:T(1,128)} %copy-done, f32[8192,2,128]{2,1,0:T(2,128)} %bitcast.31, f32[16,2,128]{2,1,0:T(2,128)} %bitcast.73, ...), custom_call_target="tpu_custom_call" | custom-call | tf_op jit(solution)/shard_map/bucket/pallas_call | solution.py:459
  1068.9 18.0 %scatter_rows.15.acc_in = f32[16384,128]{1,0:T(8,128)} custom-call(s32[8,2048]{1,0:T(8,128)} %bitcast.65, s32[1,4864]{1,0:T(1,128)} %copy-done, f32[4096,128]{1,0:T(8,128)} %get-tuple-element.150.gh, f32[4096,128]{1,0:T(8,128)} %get-tuple-element.151.gt_ref, f32[1536,128]{1,0:T(8,128)} %get-tuple-element.152.gn_ref), custom_call_target="tpu_custom_call" | custom-call | tf_op jit(solution)/shard_map/scatter_rows/pallas_call | solution.py:468
  1086.9 85.1 %update.15 = (f32[16384,128]{1,0:T(8,128)}, f32[2048,128]{1,0:T(8,128)}, f32[32,128]{1,0:T(8,128)}, f32[16,128]{1,0:T(8,128)}, f32[8,128]{1,0:T(8,128)}, /*index=5*/f32[64,128]{1,0:T(8,128)}) custom-call(f32[16384,128]{1,0:T(8,128)} %scatter_rows.15.acc_in, f32[16384,128]{1,0:T(8,128)} %get-tuple-element.148.table_in, ...), custom_call_target="tpu_custom_call" | custom-call | tf_op jit(solution)/shard_map/update/pallas_call | solution.py:479
  (50 shorter events, 40.8 us)
Async XLA Ops:
  2.2 8.4 collective-permute-start.6
  4.8 6.2 collective-permute-start.5
  6.2 430.6 %collective-permute-start.4 = (s32[1,4864]{1,0:T(1,128)S(1)}, s32[1,4864]{1,0:T(1,128)S(1)}, u32[]{:S(2)}, u32[]{:S(2)}) collective-permute-start(s32[1,4864]{1,0:T(1,128)S(1)} %get-tuple-element.165), channel_id=1, source_target_pairs={{0,3},{1,4},{2,5},{3,6},{4,7},{5,0},{6,1},{7,2},{8,11},{9,12},{10,... | collective-permute-start | bytes 58376 | tf_op jit(solution)/shard_map/ppermute | solution.py:431
  7.8 576.2 %collective-permute-start.3 = (s32[1,4864]{1,0:T(1,128)S(1)}, s32[1,4864]{1,0:T(1,128)S(1)}, u32[]{:S(2)}, u32[]{:S(2)}) collective-permute-start(s32[1,4864]{1,0:T(1,128)S(1)} %get-tuple-element.166), channel_id=1, source_target_pairs={{0,4},{1,5},{2,6},{3,7},{4,0},{5,1},{6,2},{7,3},{8,12},{9,13},{10,... | collective-permute-start | bytes 58376 | tf_op jit(solution)/shard_map/ppermute | solution.py:431
  8.1 733.6 %collective-permute-start.2 = (s32[1,4864]{1,0:T(1,128)S(1)}, s32[1,4864]{1,0:T(1,128)S(1)}, u32[]{:S(2)}, u32[]{:S(2)}) collective-permute-start(s32[1,4864]{1,0:T(1,128)S(1)} %get-tuple-element.167), channel_id=1, source_target_pairs={{0,5},{1,6},{2,7},{3,0},{4,1},{5,2},{6,3},{7,4},{8,13},{9,14},{10,... | collective-permute-start | bytes 58376 | tf_op jit(solution)/shard_map/ppermute | solution.py:431
  10.6 13.5 %copy-start.6 = (s32[1,4864]{1,0:T(1,128)}, s32[1,4864]{1,0:T(1,128)S(1)}, u32[]{:S(2)}) copy-start(s32[1,4864]{1,0:T(1,128)S(1)} %collective-permute-done.6.tail_ids.tail_vec) | copy-start | bytes 58372
  10.6 879.3 %collective-permute-start.1 = (s32[1,4864]{1,0:T(1,128)S(1)}, s32[1,4864]{1,0:T(1,128)S(1)}, u32[]{:S(2)}, u32[]{:S(2)}) collective-permute-start(s32[1,4864]{1,0:T(1,128)S(1)} %get-tuple-element.168), channel_id=1, source_target_pairs={{0,6},{1,7},{2,0},{3,1},{4,2},{5,3},{6,4},{7,5},{8,14},{9,15},{10,... | collective-permute-start | bytes 58376 | tf_op jit(solution)/shard_map/ppermute | solution.py:431
  11.1 13.0 %copy-start.5 = (s32[1,4864]{1,0:T(1,128)}, s32[1,4864]{1,0:T(1,128)S(1)}, u32[]{:S(2)}) copy-start(s32[1,4864]{1,0:T(1,128)S(1)} %collective-permute-done.5.tail_ids.tail_vec) | copy-start | bytes 58372
  11.1 1024.1 %collective-permute-start = (s32[1,4864]{1,0:T(1,128)S(1)}, s32[1,4864]{1,0:T(1,128)S(1)}, u32[]{:S(2)}, u32[]{:S(2)}) collective-permute-start(s32[1,4864]{1,0:T(1,128)S(1)} %get-tuple-element.169), channel_id=1, source_target_pairs={{0,7},{1,0},{2,1},{3,2},{4,3},{5,4},{6,5},{7,6},{8,15},{9,8},{10,9... | collective-permute-start | bytes 58376 | tf_op jit(solution)/shard_map/ppermute | solution.py:431
  50.8 17.5 %dynamic-slice-start = ((f32[8192]{0:T(1024)}, s32[]{:T(128)}), f32[2048]{0:T(1024)S(1)}, s32[]{:S(2)}) async-start(f32[8192]{0:T(1024)} %param.9, s32[]{:T(128)} %select_n.3), calls=%async_computation | async-start | bytes 16896 | tf_op jit(solution)/shard_map/dynamic_slice | solution.py:445
  436.8 0.6 copy-start.4
  584.0 0.6 copy-start.3
  741.7 0.6 copy-start.2
  889.9 0.6 copy-start.1
  1035.2 0.6 copy-start
  1172.0 10.0 copy-start.9
  1172.0 10.6 copy-start.8
  1172.0 11.3 copy-start.7

commit v3 on v2

--- a/solution.py
+++ b/solution.py
@@ -12,7 +12,7 @@
 LANES = 128
 EDGE_BLOCK = 256
 GATHER_UNROLL = 16
-SYNC_CHUNKS = 2
+SYNC_CHUNKS = 4
 VMEM_LIMIT = 60 * 1024 * 1024
 MESH = pl.DeviceIdType.MESH
 VM = pltpu.VMEM
@@ -217,12 +217,17 @@
         lax.fori_loop(0, steps, drain, 0)
 
 
-def scatter_kernel(shift, h_ids, tail_ids, gh, gt_ref, gn_ref, acc, acc_b, acc_c, acc_d):
+def scatter_kernel(shift, h_ids, tail_ids, gh_in, gt_in, gn_in, acc_out, acc, acc_b, acc_c, acc_d, gh, gt_ref, gn_ref, in_sems, out_sems):
     edges = gh.shape[0] // 2
     negs = gn_ref.shape[0] // 2
     table_rows = acc.shape[0]
-
     zero_rows = 512
+    pieces = 8
+    piece = table_rows // pieces
+
+    copies = [pltpu.make_async_copy(src, dst, in_sems.at[at]) for at, (src, dst) in enumerate(((gh_in, gh), (gt_in, gt_ref), (gn_in, gn_ref)))]
+    for copy in copies:
+        copy.start()
 
     def clear(step, _):
         rows = pl.ds(pl.multiple_of(step * zero_rows, zero_rows), zero_rows)
@@ -231,6 +236,8 @@
         return 0
 
     lax.fori_loop(0, table_rows // zero_rows, clear, 0)
+    for copy in copies:
+        copy.wait()
 
     def add_edges(step, _):
         base = step * GATHER_UNROLL
@@ -259,26 +266,86 @@
 
     lax.fori_loop(0, negs // GATHER_UNROLL, add_negs, 0)
 
-    def combine(step, _):
-        rows = pl.ds(pl.multiple_of(step * zero_rows, zero_rows), zero_rows)
+    def out_copy(at):
+        rows = pl.ds(pl.multiple_of(at * piece, piece), piece)
+        return pltpu.make_async_copy(acc.at[rows, :], acc_out.at[rows, :], out_sems.at[at])
+
+    def combine(at, _):
+        rows = pl.ds(pl.multiple_of(at * piece, piece), piece)
         acc[rows, :] = (acc[rows, :] + acc_b[rows, :]) + (acc_c[rows, :] + acc_d[rows, :])
-        return 0
-
-    lax.fori_loop(0, table_rows // zero_rows, combine, 0)
-
-
-def update_kernel(width, learn_rate, groups, reps, shift, bucket_edges, acc_in, table_in, state_in, grel_in, rel_in, rel_state_in, loss_in, losses_in,
+        out_copy(at).start()
+        return 0
+
+    lax.fori_loop(0, pieces, combine, 0)
+    for at in range(pieces):
+        out_copy(at).wait()
+
+
+def pieces_of(half):
+    found, at = [], 0
+    for bit in range(7, -1, -1):
+        if half >> bit & 1:
+            found.append((1 << bit, at))
+            at += 1 << bit
+    return found
+
+
+def pack_rows(half, x):
+    n = x.shape[0]
+    lane = lax.broadcasted_iota(jnp.int32, (1, LANES), 1)
+    out = []
+    for size, at in pieces_of(half):
+        groups = LANES // size
+        rows = n // groups
+        acc = None
+        for k in range(groups):
+            part = pltpu.roll(x[k * rows:(k + 1) * rows], (k * size - at) % LANES, 1)
+            acc = part if acc is None else jnp.where(lane < k * size, acc, part)
+        out.append(acc)
+    return jnp.concatenate(out, axis=0)
+
+
+def unpack_rows(half, n, x):
+    lane = lax.broadcasted_iota(jnp.int32, (1, LANES), 1)
+    out, start = None, 0
+    for size, at in pieces_of(half):
+        groups = LANES // size
+        rows = n // groups
+        block = x[start:start + rows]
+        start += rows
+        parts = jnp.concatenate([pltpu.roll(block, (at - k * size) % LANES, 1) for k in range(groups)], axis=0)
+        out = parts if out is None else jnp.where(lane < at, out, parts)
+    return jnp.where(lane < half, out, 0.0)
+
+
+def update_kernel(width, learn_rate, groups, reps, shift, bucket_edges, acc_hbm, table_hbm, state_in, grel_in, rel_in, rel_state_in, loss_in, losses_in,
                   table_out, state_out, rel_out, rel_state_out, losses_out, state_all,
-                  first_send, first_got, plain_send, plain_got, merged_send, merged_got, work,
-                  step_own, step_got, step_far, rel_x, rel_y, rel_send, rel_send_y, state_own,
+                  acc, table, first_send, first_got, plain_send, plain_got, merged_send, merged_got, work,
+                  step_own, step_got, step_far, rel_x, rel_y, rel_send, rel_send_y, state_own, acc_sems, table_sems, out_sems,
                   first_sems, plain_sems, merged_sems, own_sems, far_sems, rel_x_sems, rel_y_sems, state_sems):
     me = lax.axis_index('data')
     ent = lax.axis_index('ent')
+    used = width // 2
     peers = (lax.rem(me + 1, reps), lax.rem(me + reps - 1, reps))
-    far = lax.rem(me + 2, reps)
-    quarter = acc_in.shape[0] // reps
-    half = quarter // 2
+    peer_slots = (1, reps - 1)
+    half = acc.shape[2]
     chunk = half // SYNC_CHUNKS
+    sent = chunk * used // LANES
+
+    def part_rows(slot, which):
+        return pl.ds(pl.multiple_of((lax.rem(me + slot, reps) * 2 + which) * half, half), half)
+
+    def load(src, dst, sems, slot, which):
+        return pltpu.make_async_copy(src.at[part_rows(slot, which), :], dst.at[slot, which], sems.at[slot, which])
+
+    def save(slot, which):
+        return pltpu.make_async_copy(table.at[slot, which], table_out.at[part_rows(slot, which), :], out_sems.at[slot, which])
+
+    for slot, which in ((2, 0), (2, 1), (1, 1), (3, 0), (1, 0), (3, 1), (0, 0), (0, 1)):
+        load(acc_hbm, acc, acc_sems, slot, which).start()
+    for slot in range(reps):
+        for which in range(2):
+            load(table_hbm, table, table_sems, slot, which).start()
 
     barrier = pltpu.get_barrier_semaphore()
     for off in range(1, reps):
@@ -298,29 +365,50 @@
     for copy in x_copies:
         copy.start()
 
-    def rows_of(owner, which, k):
-        return pl.ds(pl.multiple_of(owner * quarter + which * half + k * chunk, chunk), chunk)
-
     def at_chunk(k):
-        return pl.ds(k * chunk, chunk)
-
-    first, plain, merged = {}, {}, {}
-    for k in range(SYNC_CHUNKS):
+        return pl.ds(pl.multiple_of(k * chunk, chunk), chunk)
+
+    def at_sent(k):
+        return pl.ds(pl.multiple_of(k * sent, sent), sent)
+
+    def first(side, k):
+        return remote(first_send.at[side, at_sent(k), :], first_got.at[side, at_sent(k), :], first_sems, (side, k), {'data': peers[side]})
+
+    def plain(side, k):
+        return remote(plain_send.at[side, at_sent(k), :], plain_got.at[side, at_sent(k), :], plain_sems, (side, k), {'data': peers[side]})
+
+    def merged(side, k):
+        return remote(merged_send.at[side, at_sent(k), :], merged_got.at[side, at_sent(k), :], merged_sems, (side, k), {'data': peers[side]})
+
+    def own(side, which, k):
+        return remote(step_own.at[which, at_sent(k), :], step_got.at[side, which, at_sent(k), :], own_sems, (side, which, k), {'data': peers[side]})
+
+    def spread(side, k):
+        return remote(step_got.at[side, side, at_sent(k), :], step_far.at[side, at_sent(k), :], far_sems, (side, k), {'data': peers[side]})
+
+    def send_first(k, _):
         for side in range(2):
-            first_send[side, at_chunk(k), :] = acc_in[rows_of(far, side, k), :].astype(BF16)
-            first[side, k] = remote(first_send.at[side, at_chunk(k), :], first_got.at[side, at_chunk(k), :], first_sems, (side, k), {'data': peers[side]})
-            first[side, k].start()
-    for k in range(SYNC_CHUNKS):
+            first_send[side, at_sent(k), :] = pack_rows(used, acc[2, side, at_chunk(k), :]).astype(BF16)
+            first(side, k).start()
+        return 0
+
+    def send_plain(k, _):
         for side in range(2):
-            plain_send[side, at_chunk(k), :] = acc_in[rows_of(peers[side], 1 - side, k), :].astype(BF16)
-            plain[side, k] = remote(plain_send.at[side, at_chunk(k), :], plain_got.at[side, at_chunk(k), :], plain_sems, (side, k), {'data': peers[side]})
-            plain[side, k].start()
-    for k in range(SYNC_CHUNKS):
+            plain_send[side, at_sent(k), :] = pack_rows(used, acc[peer_slots[side], 1 - side, at_chunk(k), :]).astype(BF16)
+            plain(side, k).start()
+        return 0
+
+    def send_merged(k, _):
         for side in range(2):
-            first[side, k].wait_recv()
-            merged_send[side, at_chunk(k), :] = (first_got[side, at_chunk(k), :].astype(F32) + acc_in[rows_of(peers[side], side, k), :]).astype(BF16)
-            merged[side, k] = remote(merged_send.at[side, at_chunk(k), :], merged_got.at[side, at_chunk(k), :], merged_sems, (side, k), {'data': peers[side]})
-            merged[side, k].start()
+            first(side, k).wait_recv()
+            merged_send[side, at_sent(k), :] = (first_got[side, at_sent(k), :].astype(F32) + pack_rows(used, acc[peer_slots[side], side, at_chunk(k), :])).astype(BF16)
+            merged(side, k).start()
+        return 0
+
+    for needed, body in ((((2, 0), (2, 1)), send_first), (((1, 1), (3, 0)), send_plain), (((1, 0), (3, 1)), send_merged)):
+        for slot, which in needed:
+            load(acc_hbm, acc, acc_sems, slot, which).wait()
+        lax.fori_loop(0, SYNC_CHUNKS, body, 0)
 
     for copy in x_copies:
         copy.wait()
@@ -335,36 +423,51 @@
     for copy in y_copies:
         copy.start()
 
-    own = {}
-    for k in range(SYNC_CHUNKS):
+    for which in range(2):
+        load(acc_hbm, acc, acc_sems, 0, which).wait()
+    for slot in range(reps):
         for which in range(2):
-            merged[which, k].wait_recv()
-            plain[1 - which, k].wait_recv()
-            work[...] = acc_in[rows_of(me, which, k), :] + (merged_got[which, at_chunk(k), :].astype(F32) + plain_got[1 - which, at_chunk(k), :].astype(F32))
-            n = chunk // 2
-            re_g, im_g = work[pl.ds(0, n, stride=2), :], work[pl.ds(1, n, stride=2), :]
-            places = pl.ds(which * (half // 2) + k * n, n)
+            load(table_hbm, table, table_sems, slot, which).wait()
+    n = chunk // 2
+    even, odd = pl.ds(0, n, stride=2), pl.ds(1, n, stride=2)
+
+    def step_rows(k, _):
+        for which in range(2):
+            merged(which, k).wait_recv()
+            plain(1 - which, k).wait_recv()
+            others = merged_got[which, at_sent(k), :].astype(F32) + plain_got[1 - which, at_sent(k), :].astype(F32)
+            work[...] = acc[0, which, at_chunk(k), :] + unpack_rows(used, chunk, others)
+            re_g, im_g = work[even, :], work[odd, :]
+            places = pl.ds(pl.multiple_of(which * (half // 2) + k * n, n), n)
             state = state_in[places, :] + jnp.sum(re_g * re_g + im_g * im_g, axis=1, keepdims=True) / width
             state_out[places, :] = state
             scale = learn_rate / jnp.sqrt(state + EPSILON)
-            work[pl.ds(0, n, stride=2), :] = re_g * scale
-            work[pl.ds(1, n, stride=2), :] = im_g * scale
-            step_own[which, at_chunk(k), :] = work[...].astype(BF16)
+            work[even, :] = re_g * scale
+            work[odd, :] = im_g * scale
+            moves = work[...]
+            step_own[which, at_sent(k), :] = pack_rows(used, moves).astype(BF16)
             for side in range(2):
-                own[side, which, k] = remote(step_own.at[which, at_chunk(k), :], step_got.at[side, which, at_chunk(k), :], own_sems, (side, which, k), {'data': peers[side]})
-                own[side, which, k].start()
-
-    spread = {}
-    for k in range(SYNC_CHUNKS):
+                own(side, which, k).start()
+            table[0, which, at_chunk(k), :] -= moves.astype(BF16).astype(F32)
+        return 0
+
+    lax.fori_loop(0, SYNC_CHUNKS, step_rows, 0)
+    for which in range(2):
+        save(0, which).start()
+
+    def take_near(k, _):
         for which in range(2):
-            for side in range(2):
-                own[side, which, k].wait_recv()
+            for side in (which, 1 - which):
+                own(side, which, k).wait_recv()
                 if side == which:
-                    spread[side, k] = remote(step_got.at[side, which, at_chunk(k), :], step_far.at[side, at_chunk(k), :], far_sems, (side, k), {'data': peers[side]})
-                    spread[side, k].start()
-            for owner, ref in ((me, step_own.at[which]), (peers[1], step_got.at[0, which]), (peers[0], step_got.at[1, which])):
-                rows = rows_of(owner, which, k)
-                table_out[rows, :] = table_in[rows, :] - ref[at_chunk(k), :].astype(F32)
+                    spread(side, k).start()
+                table[peer_slots[1 - side], which, at_chunk(k), :] -= unpack_rows(used, chunk, step_got[side, which, at_sent(k), :].astype(F32))
+        return 0
+
+    lax.fori_loop(0, SYNC_CHUNKS, take_near, 0)
+    for slot in peer_slots:
+        for which in range(2):
+            save(slot, which).start()
 
     for copy in y_copies:
         copy.wait()
@@ -395,14 +498,26 @@
     else:
         state_all[...] = jnp.zeros_like(state_all)
 
-    for k in range(SYNC_CHUNKS):
+    def take_far(k, _):
         for side in range(2):
-            spread[side, k].wait_recv()
-            rows = rows_of(far, side, k)
-            table_out[rows, :] = table_in[rows, :] - step_far[side, at_chunk(k), :].astype(F32)
-    for group_of in (first, plain, merged, own, spread):
-        for copy in group_of.values():
-            copy.wait_send()
+            spread(side, k).wait_recv()
+            table[2, side, at_chunk(k), :] -= unpack_rows(used, chunk, step_far[side, at_sent(k), :].astype(F32))
+        return 0
+
+    lax.fori_loop(0, SYNC_CHUNKS, take_far, 0)
+    for which in range(2):
+        save(2, which).start()
+
+    def drain(k, _):
+        for side in range(2):
+            for copy in (first(side, k), plain(side, k), merged(side, k), own(side, 0, k), own(side, 1, k), spread(side, k)):
+                copy.wait_send()
+        return 0
+
+    lax.fori_loop(0, SYNC_CHUNKS, drain, 0)
+    for slot in range(reps):
+        for which in range(2):
+            save(slot, which).wait()
     for copy in state_copies:
         copy.wait()
 
@@ -446,6 +561,7 @@
         losses = jnp.zeros((-(-groups // 8) * 8, LANES), F32)
 
         smem = pl.BlockSpec(memory_space=pltpu.SMEM)
+        hbm = pl.BlockSpec(memory_space=pl.ANY)
         sems = pltpu.SemaphoreType.DMA
         steps = edges // EDGE_BLOCK
         for shift in range(groups):
@@ -468,23 +584,24 @@
             acc = pl.pallas_call(
                 functools.partial(scatter_kernel, shift),
                 out_shape=jax.ShapeDtypeStruct((2 * part_rows, LANES), F32),
-                in_specs=[smem] * 2 + [vmem] * 3, out_specs=vmem,
-                scratch_shapes=[VM((2 * part_rows, LANES), F32)] * 3,
+                in_specs=[smem] * 2 + [hbm] * 3, out_specs=hbm,
+                scratch_shapes=[VM((2 * part_rows, LANES), F32)] * 4 + [VM((2 * edges, LANES), F32)] * 2 + [VM((2 * negs, LANES), F32), sems((3,)), sems((8,))],
                 compiler_params=params, name='scatter_rows',
             )(h_all, tail, g_h, g_t, g_n)
 
             half = (2 * part_rows) // reps // 2
-            block = VM((2, half, LANES), BF16)
+            half_sent = half * (width // 2) // LANES
+            block = VM((2, half_sent, LANES), BF16)
             state_blocks = quarter // LANES
             table, state, rel, rel_state, losses, state_all = pl.pallas_call(
                 functools.partial(update_kernel, width, learn_rate, groups, reps, shift, bucket_edges),
                 out_shape=[jax.ShapeDtypeStruct(table.shape, F32), jax.ShapeDtypeStruct(state.shape, F32),
                            jax.ShapeDtypeStruct(rel.shape, F32), jax.ShapeDtypeStruct(rel_state.shape, F32),
                            jax.ShapeDtypeStruct(losses.shape, F32), jax.ShapeDtypeStruct((reps * state_blocks, LANES), F32)],
-                in_specs=[vmem] * 8, out_specs=[vmem] * 6,
-                scratch_shapes=[block] * 6 + [VM((half // SYNC_CHUNKS, LANES), F32), block, VM((2, 2, half, LANES), BF16), block,
+                in_specs=[hbm] * 2 + [vmem] * 6, out_specs=[hbm] + [vmem] * 5,
+                scratch_shapes=[VM((reps, 2, half, LANES), F32)] * 2 + [block] * 6 + [VM((half // SYNC_CHUNKS, LANES), F32), block, VM((2, 2, half_sent, LANES), BF16), block,
                                               VM((groups, 2 * rel_pad, LANES), F32), VM((reps, 2 * rel_pad + losses.shape[0], LANES), F32), VM((2 * rel_pad, LANES), F32),
-                                              VM((2 * rel_pad + losses.shape[0], LANES), F32), VM((state_blocks, LANES), F32),
+                                              VM((2 * rel_pad + losses.shape[0], LANES), F32), VM((state_blocks, LANES), F32), sems((reps, 2)), sems((reps, 2)), sems((reps, 2)),
                                               sems((2, 2, SYNC_CHUNKS)), sems((2, 2, SYNC_CHUNKS)), sems((2, 2, SYNC_CHUNKS)),
                                               sems((2, 2, 2, SYNC_CHUNKS)), sems((2, 2, SYNC_CHUNKS)), sems((2, groups - 1)), sems((2, reps - 1)), sems((2, reps - 1))],
                 compiler_params=pltpu.CompilerParams(vmem_limit_bytes=VMEM_LIMIT, collective_id=1, has_side_effects=True), name='update',

time: 1190 us -> 1030 us (0.87)
  Pallas kernels: 1160 us -> 996 us
    pallas_call x8, Pallas kernels: 670 us -> 515 us  [device_fn(): pl.pallas_call(functools.partial(update_kernel, width, learn_rate, groups...]
    pallas_call x8, Pallas kernels: 144 us -> 131 us  [device_fn(): pl.pallas_call(functools.partial(scatter_kernel, shift), out_shape=jax.Sh...]
where the time goes in v3:
time: 1030 us; the launch traced here: 1020 us
  Pallas kernels  996 us (97%)
  starting transfers between devices  10.3 us (1%)
    pallas_call x8, Pallas kernels, device_fn(): pl.pallas_call(functools.partial(update_kernel, width, learn_rate, groups...  515 us
    pallas_call x8, Pallas kernels, device_fn(): pl.pallas_call(functools.partial(bucket_kernel, shift, groups), out_shape...  330 us
    pallas_call x8, Pallas kernels, device_fn(): pl.pallas_call(functools.partial(scatter_kernel, shift), out_shape=jax.Sh...  131 us
  transfers between devices with their start and end apart: 7, of which 0 were waited for; matrix products, arithmetic and copies ran while one was open for 0% of the time, Pallas kernels for 86%

profile of v3, /device:TPU:97, one launch (start us, length us, event | category | flops | bytes accessed | tf_op | source)
XLA Modules:
  0.0 1018.3 jit_solution(4574840670449084350)
XLA Ops:
  24.0 26.7 %bucket.8 = (f32[4096,128]{1,0:T(8,128)}, f32[4096,128]{1,0:T(8,128)}, f32[1536,128]{1,0:T(8,128)}, f32[32,128]{1,0:T(8,128)}, f32[8,128]{1,0:T(8,128)}) custom-call(s32[8,2048]{1,0:T(8,128)} %bitcast.50, s32[8,2048]{1,0:T(8,128)} %bitcast.34, s32[1,4864]{1,0:T(1,128)} %get-tuple-element.162.tail_ids.tail_vec, f32[8192,2,128]{2,1,0:T(2,128)} %bitcast.26, ...), custom_call_target="tpu_custom_call" | custom-call | tf_op jit(solution)/shard_map/bucket/pallas_call | solution.py:575
  50.8 16.0 %scatter_rows.8.acc_hbm = f32[16384,128]{1,0:T(8,128)} custom-call(s32[8,2048]{1,0:T(8,128)} %bitcast.51, s32[1,4864]{1,0:T(1,128)} %get-tuple-element.162.tail_ids.tail_vec, f32[4096,128]{1,0:T(8,128)} %get-tuple-element.83.gh_in, f32[4096,128]{1,0:T(8,128)} %get-tuple-element.84.gt_in, f32[1536,128]{1,0:T(8,128)} %get-tuple-element.85.gn_in), custom_call_target="tpu_custom_call" | custom-call | tf_op jit(solution)/shard_map/scatter_rows/pallas_call | solution.py:584
  69.3 65.7 %update.8 = (f32[16384,128]{1,0:T(8,128)}, f32[2048,128]{1,0:T(8,128)}, f32[32,128]{1,0:T(8,128)}, f32[16,128]{1,0:T(8,128)}, f32[8,128]{1,0:T(8,128)}, /*index=5*/f32[64,128]{1,0:T(8,128)}) custom-call(f32[16384,128]{1,0:T(8,128)} %scatter_rows.8.acc_hbm, f32[16384,128]{1,0:T(8,128)} %load_table.1.table_hbm, f32[2048,128]{1,0:T(8,128)} %broadcast_in_dim.12.state_in, ...), custom_call_target="tpu_custom_call" | custom-call | tf_op jit(solution)/shard_map/update/pallas_call | solution.py:596
  135.0 33.3 %bucket.9 = (f32[4096,128]{1,0:T(8,128)}, f32[4096,128]{1,0:T(8,128)}, f32[1536,128]{1,0:T(8,128)}, f32[32,128]{1,0:T(8,128)}, f32[8,128]{1,0:T(8,128)}) custom-call(s32[8,2048]{1,0:T(8,128)} %bitcast.52, s32[8,2048]{1,0:T(8,128)} %bitcast.36, s32[1,4864]{1,0:T(1,128)} %copy-done.6, f32[8192,2,128]{2,1,0:T(2,128)} %bitcast.32, f32[16,2,128]{2,1,0:T(2,128)} %bitcast.74, ...), custom_call_target="tpu_custom_call" | custom-call | tf_op jit(solution)/shard_map/bucket/pallas_call | solution.py:575
  168.3 16.4 %scatter_rows.9.acc_hbm = f32[16384,128]{1,0:T(8,128)} custom-call(s32[8,2048]{1,0:T(8,128)} %bitcast.53, s32[1,4864]{1,0:T(1,128)} %copy-done.6, f32[4096,128]{1,0:T(8,128)} %get-tuple-element.90.gh_in, f32[4096,128]{1,0:T(8,128)} %get-tuple-element.91.gt_in, f32[1536,128]{1,0:T(8,128)} %get-tuple-element.92.gn_in), custom_call_target="tpu_custom_call" | custom-call | tf_op jit(solution)/shard_map/scatter_rows/pallas_call | solution.py:584
  184.7 62.7 %update.9 = (f32[16384,128]{1,0:T(8,128)}, f32[2048,128]{1,0:T(8,128)}, f32[32,128]{1,0:T(8,128)}, f32[16,128]{1,0:T(8,128)}, f32[8,128]{1,0:T(8,128)}, /*index=5*/f32[64,128]{1,0:T(8,128)}) custom-call(f32[16384,128]{1,0:T(8,128)} %scatter_rows.9.acc_hbm, f32[16384,128]{1,0:T(8,128)} %get-tuple-element.88.table_hbm, ...), custom_call_target="tpu_custom_call" | custom-call | tf_op jit(solution)/shard_map/update/pallas_call | solution.py:596
  247.4 43.4 %bucket.10 = (f32[4096,128]{1,0:T(8,128)}, f32[4096,128]{1,0:T(8,128)}, f32[1536,128]{1,0:T(8,128)}, f32[32,128]{1,0:T(8,128)}, f32[8,128]{1,0:T(8,128)}) custom-call(s32[8,2048]{1,0:T(8,128)} %bitcast.54, s32[8,2048]{1,0:T(8,128)} %bitcast.38, s32[1,4864]{1,0:T(1,128)} %copy-done.5, f32[8192,2,128]{2,1,0:T(2,128)} %bitcast.33, f32[16,2,128]{2,1,0:T(2,128)} %bitcast.75, ...), custom_call_target="tpu_custom_call" | custom-call | tf_op jit(solution)/shard_map/bucket/pallas_call | solution.py:575
  290.9 16.4 %scatter_rows.10.acc_hbm = f32[16384,128]{1,0:T(8,128)} custom-call(s32[8,2048]{1,0:T(8,128)} %bitcast.55, s32[1,4864]{1,0:T(1,128)} %copy-done.5, f32[4096,128]{1,0:T(8,128)} %get-tuple-element.100.gh_in, f32[4096,128]{1,0:T(8,128)} %get-tuple-element.101.gt_in, f32[1536,128]{1,0:T(8,128)} %get-tuple-element.102.gn_in), custom_call_target="tpu_custom_call" | custom-call | tf_op jit(solution)/shard_map/scatter_rows/pallas_call | solution.py:584
  307.3 66.0 %update.10 = (f32[16384,128]{1,0:T(8,128)}, f32[2048,128]{1,0:T(8,128)}, f32[32,128]{1,0:T(8,128)}, f32[16,128]{1,0:T(8,128)}, f32[8,128]{1,0:T(8,128)}, /*index=5*/f32[64,128]{1,0:T(8,128)}) custom-call(f32[16384,128]{1,0:T(8,128)} %scatter_rows.10.acc_hbm, f32[16384,128]{1,0:T(8,128)} %get-tuple-element.98.table_hbm, ...), custom_call_target="tpu_custom_call" | custom-call | tf_op jit(solution)/shard_map/update/pallas_call | solution.py:596
  373.9 48.7 %bucket.11 = (f32[4096,128]{1,0:T(8,128)}, f32[4096,128]{1,0:T(8,128)}, f32[1536,128]{1,0:T(8,128)}, f32[32,128]{1,0:T(8,128)}, f32[8,128]{1,0:T(8,128)}) custom-call(s32[8,2048]{1,0:T(8,128)} %bitcast.56, s32[8,2048]{1,0:T(8,128)} %bitcast.40, s32[1,4864]{1,0:T(1,128)} %copy-done.4, f32[8192,2,128]{2,1,0:T(2,128)} %bitcast.27, f32[16,2,128]{2,1,0:T(2,128)} %bitcast.69, ...), custom_call_target="tpu_custom_call" | custom-call | tf_op jit(solution)/shard_map/bucket/pallas_call | solution.py:575
  422.6 16.4 %scatter_rows.11.acc_hbm = f32[16384,128]{1,0:T(8,128)} custom-call(s32[8,2048]{1,0:T(8,128)} %bitcast.57, s32[1,4864]{1,0:T(1,128)} %copy-done.4, f32[4096,128]{1,0:T(8,128)} %get-tuple-element.110.gh_in, f32[4096,128]{1,0:T(8,128)} %get-tuple-element.111.gt_in, f32[1536,128]{1,0:T(8,128)} %get-tuple-element.112.gn_in), custom_call_target="tpu_custom_call" | custom-call | tf_op jit(solution)/shard_map/scatter_rows/pallas_call | solution.py:584
  439.0 64.1 %update.11 = (f32[16384,128]{1,0:T(8,128)}, f32[2048,128]{1,0:T(8,128)}, f32[32,128]{1,0:T(8,128)}, f32[16,128]{1,0:T(8,128)}, f32[8,128]{1,0:T(8,128)}, /*index=5*/f32[64,128]{1,0:T(8,128)}) custom-call(f32[16384,128]{1,0:T(8,128)} %scatter_rows.11.acc_hbm, f32[16384,128]{1,0:T(8,128)} %get-tuple-element.108.table_hbm, ...), custom_call_target="tpu_custom_call" | custom-call | tf_op jit(solution)/shard_map/update/pallas_call | solution.py:596
  503.7 55.1 %bucket.12 = (f32[4096,128]{1,0:T(8,128)}, f32[4096,128]{1,0:T(8,128)}, f32[1536,128]{1,0:T(8,128)}, f32[32,128]{1,0:T(8,128)}, f32[8,128]{1,0:T(8,128)}) custom-call(s32[8,2048]{1,0:T(8,128)} %bitcast.58, s32[8,2048]{1,0:T(8,128)} %bitcast.42, s32[1,4864]{1,0:T(1,128)} %copy-done.3, f32[8192,2,128]{2,1,0:T(2,128)} %bitcast.28, f32[16,2,128]{2,1,0:T(2,128)} %bitcast.70, ...), custom_call_target="tpu_custom_call" | custom-call | tf_op jit(solution)/shard_map/bucket/pallas_call | solution.py:575
  558.8 16.6 %scatter_rows.12.acc_hbm = f32[16384,128]{1,0:T(8,128)} custom-call(s32[8,2048]{1,0:T(8,128)} %bitcast.59, s32[1,4864]{1,0:T(1,128)} %copy-done.3, f32[4096,128]{1,0:T(8,128)} %get-tuple-element.120.gh_in, f32[4096,128]{1,0:T(8,128)} %get-tuple-element.121.gt_in, f32[1536,128]{1,0:T(8,128)} %get-tuple-element.122.gn_in), custom_call_target="tpu_custom_call" | custom-call | tf_op jit(solution)/shard_map/scatter_rows/pallas_call | solution.py:584
  575.4 64.6 %update.12 = (f32[16384,128]{1,0:T(8,128)}, f32[2048,128]{1,0:T(8,128)}, f32[32,128]{1,0:T(8,128)}, f32[16,128]{1,0:T(8,128)}, f32[8,128]{1,0:T(8,128)}, /*index=5*/f32[64,128]{1,0:T(8,128)}) custom-call(f32[16384,128]{1,0:T(8,128)} %scatter_rows.12.acc_hbm, f32[16384,128]{1,0:T(8,128)} %get-tuple-element.118.table_hbm, ...), custom_call_target="tpu_custom_call" | custom-call | tf_op jit(solution)/shard_map/update/pallas_call | solution.py:596
  640.6 45.5 %bucket.13 = (f32[4096,128]{1,0:T(8,128)}, f32[4096,128]{1,0:T(8,128)}, f32[1536,128]{1,0:T(8,128)}, f32[32,128]{1,0:T(8,128)}, f32[8,128]{1,0:T(8,128)}) custom-call(s32[8,2048]{1,0:T(8,128)} %bitcast.60, s32[8,2048]{1,0:T(8,128)} %bitcast.44, s32[1,4864]{1,0:T(1,128)} %copy-done.2, f32[8192,2,128]{2,1,0:T(2,128)} %bitcast.29, f32[16,2,128]{2,1,0:T(2,128)} %bitcast.71, ...), custom_call_target="tpu_custom_call" | custom-call | tf_op jit(solution)/shard_map/bucket/pallas_call | solution.py:575
  686.2 16.4 %scatter_rows.13.acc_hbm = f32[16384,128]{1,0:T(8,128)} custom-call(s32[8,2048]{1,0:T(8,128)} %bitcast.61, s32[1,4864]{1,0:T(1,128)} %copy-done.2, f32[4096,128]{1,0:T(8,128)} %get-tuple-element.130.gh_in, f32[4096,128]{1,0:T(8,128)} %get-tuple-element.131.gt_in, f32[1536,128]{1,0:T(8,128)} %get-tuple-element.132.gn_in), custom_call_target="tpu_custom_call" | custom-call | tf_op jit(solution)/shard_map/scatter_rows/pallas_call | solution.py:584
  702.6 63.9 %update.13 = (f32[16384,128]{1,0:T(8,128)}, f32[2048,128]{1,0:T(8,128)}, f32[32,128]{1,0:T(8,128)}, f32[16,128]{1,0:T(8,128)}, f32[8,128]{1,0:T(8,128)}, /*index=5*/f32[64,128]{1,0:T(8,128)}) custom-call(f32[16384,128]{1,0:T(8,128)} %scatter_rows.13.acc_hbm, f32[16384,128]{1,0:T(8,128)} %get-tuple-element.128.table_hbm, ...), custom_call_target="tpu_custom_call" | custom-call | tf_op jit(solution)/shard_map/update/pallas_call | solution.py:596
  767.2 44.1 %bucket.14 = (f32[4096,128]{1,0:T(8,128)}, f32[4096,128]{1,0:T(8,128)}, f32[1536,128]{1,0:T(8,128)}, f32[32,128]{1,0:T(8,128)}, f32[8,128]{1,0:T(8,128)}) custom-call(s32[8,2048]{1,0:T(8,128)} %bitcast.62, s32[8,2048]{1,0:T(8,128)} %bitcast.46, s32[1,4864]{1,0:T(1,128)} %copy-done.1, f32[8192,2,128]{2,1,0:T(2,128)} %bitcast.30, f32[16,2,128]{2,1,0:T(2,128)} %bitcast.72, ...), custom_call_target="tpu_custom_call" | custom-call | tf_op jit(solution)/shard_map/bucket/pallas_call | solution.py:575
  811.3 16.4 %scatter_rows.14.acc_hbm = f32[16384,128]{1,0:T(8,128)} custom-call(s32[8,2048]{1,0:T(8,128)} %bitcast.63, s32[1,4864]{1,0:T(1,128)} %copy-done.1, f32[4096,128]{1,0:T(8,128)} %get-tuple-element.140.gh_in, f32[4096,128]{1,0:T(8,128)} %get-tuple-element.141.gt_in, f32[1536,128]{1,0:T(8,128)} %get-tuple-element.142.gn_in), custom_call_target="tpu_custom_call" | custom-call | tf_op jit(solution)/shard_map/scatter_rows/pallas_call | solution.py:584
  827.7 63.0 %update.14 = (f32[16384,128]{1,0:T(8,128)}, f32[2048,128]{1,0:T(8,128)}, f32[32,128]{1,0:T(8,128)}, f32[16,128]{1,0:T(8,128)}, f32[8,128]{1,0:T(8,128)}, /*index=5*/f32[64,128]{1,0:T(8,128)}) custom-call(f32[16384,128]{1,0:T(8,128)} %scatter_rows.14.acc_hbm, f32[16384,128]{1,0:T(8,128)} %get-tuple-element.138.table_hbm, ...), custom_call_target="tpu_custom_call" | custom-call | tf_op jit(solution)/shard_map/update/pallas_call | solution.py:596
  891.3 32.8 %bucket.15 = (f32[4096,128]{1,0:T(8,128)}, f32[4096,128]{1,0:T(8,128)}, f32[1536,128]{1,0:T(8,128)}, f32[32,128]{1,0:T(8,128)}, f32[8,128]{1,0:T(8,128)}) custom-call(s32[8,2048]{1,0:T(8,128)} %bitcast.64, s32[8,2048]{1,0:T(8,128)} %bitcast.48, s32[1,4864]{1,0:T(1,128)} %copy-done, f32[8192,2,128]{2,1,0:T(2,128)} %bitcast.31, f32[16,2,128]{2,1,0:T(2,128)} %bitcast.73, ...), custom_call_target="tpu_custom_call" | custom-call | tf_op jit(solution)/shard_map/bucket/pallas_call | solution.py:575
  924.1 16.4 %scatter_rows.15.acc_hbm = f32[16384,128]{1,0:T(8,128)} custom-call(s32[8,2048]{1,0:T(8,128)} %bitcast.65, s32[1,4864]{1,0:T(1,128)} %copy-done, f32[4096,128]{1,0:T(8,128)} %get-tuple-element.150.gh_in, f32[4096,128]{1,0:T(8,128)} %get-tuple-element.151.gt_in, f32[1536,128]{1,0:T(8,128)} %get-tuple-element.152.gn_in), custom_call_target="tpu_custom_call" | custom-call | tf_op jit(solution)/shard_map/scatter_rows/pallas_call | solution.py:584
  940.5 65.5 %update.15 = (f32[16384,128]{1,0:T(8,128)}, f32[2048,128]{1,0:T(8,128)}, f32[32,128]{1,0:T(8,128)}, f32[16,128]{1,0:T(8,128)}, f32[8,128]{1,0:T(8,128)}, /*index=5*/f32[64,128]{1,0:T(8,128)}) custom-call(f32[16384,128]{1,0:T(8,128)} %scatter_rows.15.acc_hbm, f32[16384,128]{1,0:T(8,128)} %get-tuple-element.148.table_hbm, ...), custom_call_target="tpu_custom_call" | custom-call | tf_op jit(solution)/shard_map/update/pallas_call | solution.py:596
  (50 shorter events, 40.8 us)
Async XLA Ops:
  2.2 8.4 collective-permute-start.6
  4.8 6.2 collective-permute-start.5
  6.2 367.1 %collective-permute-start.4 = (s32[1,4864]{1,0:T(1,128)S(1)}, s32[1,4864]{1,0:T(1,128)S(1)}, u32[]{:S(2)}, u32[]{:S(2)}) collective-permute-start(s32[1,4864]{1,0:T(1,128)S(1)} %get-tuple-element.165), channel_id=1, source_target_pairs={{0,3},{1,4},{2,5},{3,6},{4,7},{5,0},{6,1},{7,2},{8,11},{9,12},{10,... | collective-permute-start | bytes 58376 | tf_op jit(solution)/shard_map/ppermute | solution.py:546
  7.8 495.3 %collective-permute-start.3 = (s32[1,4864]{1,0:T(1,128)S(1)}, s32[1,4864]{1,0:T(1,128)S(1)}, u32[]{:S(2)}, u32[]{:S(2)}) collective-permute-start(s32[1,4864]{1,0:T(1,128)S(1)} %get-tuple-element.166), channel_id=1, source_target_pairs={{0,4},{1,5},{2,6},{3,7},{4,0},{5,1},{6,2},{7,3},{8,12},{9,13},{10,... | collective-permute-start | bytes 58376 | tf_op jit(solution)/shard_map/ppermute | solution.py:546
  8.1 631.9 %collective-permute-start.2 = (s32[1,4864]{1,0:T(1,128)S(1)}, s32[1,4864]{1,0:T(1,128)S(1)}, u32[]{:S(2)}, u32[]{:S(2)}) collective-permute-start(s32[1,4864]{1,0:T(1,128)S(1)} %get-tuple-element.167), channel_id=1, source_target_pairs={{0,5},{1,6},{2,7},{3,0},{4,1},{5,2},{6,3},{7,4},{8,13},{9,14},{10,... | collective-permute-start | bytes 58376 | tf_op jit(solution)/shard_map/ppermute | solution.py:546
  10.6 13.5 %copy-start.6 = (s32[1,4864]{1,0:T(1,128)}, s32[1,4864]{1,0:T(1,128)S(1)}, u32[]{:S(2)}) copy-start(s32[1,4864]{1,0:T(1,128)S(1)} %collective-permute-done.6.tail_ids.tail_vec) | copy-start | bytes 58372
  10.6 756.0 %collective-permute-start.1 = (s32[1,4864]{1,0:T(1,128)S(1)}, s32[1,4864]{1,0:T(1,128)S(1)}, u32[]{:S(2)}, u32[]{:S(2)}) collective-permute-start(s32[1,4864]{1,0:T(1,128)S(1)} %get-tuple-element.168), channel_id=1, source_target_pairs={{0,6},{1,7},{2,0},{3,1},{4,2},{5,3},{6,4},{7,5},{8,14},{9,15},{10,... | collective-permute-start | bytes 58376 | tf_op jit(solution)/shard_map/ppermute | solution.py:546
  11.1 13.0 %copy-start.5 = (s32[1,4864]{1,0:T(1,128)}, s32[1,4864]{1,0:T(1,128)S(1)}, u32[]{:S(2)}) copy-start(s32[1,4864]{1,0:T(1,128)S(1)} %collective-permute-done.5.tail_ids.tail_vec) | copy-start | bytes 58372
  11.1 879.7 %collective-permute-start = (s32[1,4864]{1,0:T(1,128)S(1)}, s32[1,4864]{1,0:T(1,128)S(1)}, u32[]{:S(2)}, u32[]{:S(2)}) collective-permute-start(s32[1,4864]{1,0:T(1,128)S(1)} %get-tuple-element.169), channel_id=1, source_target_pairs={{0,7},{1,0},{2,1},{3,2},{4,3},{5,4},{6,5},{7,6},{8,15},{9,8},{10,9... | collective-permute-start | bytes 58376 | tf_op jit(solution)/shard_map/ppermute | solution.py:546
  50.8 16.0 %dynamic-slice-start = ((f32[8192]{0:T(1024)}, s32[]{:T(128)}), f32[2048]{0:T(1024)S(1)}, s32[]{:S(2)}) async-start(f32[8192]{0:T(1024)} %param.9, s32[]{:T(128)} %select_n.3), calls=%async_computation | async-start | bytes 16896 | tf_op jit(solution)/shard_map/dynamic_slice | solution.py:560
  373.3 0.6 copy-start.4
  503.1 0.6 copy-start.3
  640.0 0.6 copy-start.2
  766.6 0.6 copy-start.1
  890.7 0.6 copy-start
  1006.0 10.0 copy-start.9
  1006.0 10.6 %copy-start.8 = (f32[32,128]{1,0:T(8,128)S(1)}, f32[32,128]{1,0:T(8,128)}, u32[]{:S(2)}) copy-start(f32[32,128]{1,0:T(8,128)} %get-tuple-element.160) | copy-start | bytes 49156
  1006.0 11.3 %copy-start.7 = (f32[64,128]{1,0:T(8,128)S(1)}, f32[64,128]{1,0:T(8,128)}, u32[]{:S(2)}) copy-start(f32[64,128]{1,0:T(8,128)} %get-tuple-element.159) | copy-start | bytes 98308

commit v4 on v3

--- a/solution.py
+++ b/solution.py
@@ -11,7 +11,8 @@
 EPSILON = 1e-8
 LANES = 128
 EDGE_BLOCK = 256
-GATHER_UNROLL = 16
+GATHER_UNROLL = 32
+SCATTER_UNROLL = 16
 SYNC_CHUNKS = 4
 VMEM_LIMIT = 60 * 1024 * 1024
 MESH = pl.DeviceIdType.MESH
@@ -58,11 +59,14 @@
         table_t[LANES:width, at:at + LANES] = moved.T[0:width - LANES, :]
 
 
-def bucket_kernel(shift, group, h_ids, r_ids, tail_ids, table, rel, r_vec, tail_vec,
-                  gh_ref, gt_ref, gn_ref, grel_ref, loss_ref,
-                  h_rows, r_rows, t_rows, n_rows, q_own, n_bf, gn_acc, *scratch):
-    edges = q_own.shape[0]
+def bucket_kernel(shift, group, used, h_ids, r_ids, tail_ids, table_hbm, rel, r_vec, tail_vec,
+                  gh_out, gt_out, gn_out, grel_ref, loss_ref,
+                  table, gh_ref, gt_ref, gn_ref, h_rows, r_rows, t_rows, n_rows, n_bf, gn_acc, table_sem, gh_sems, gt_sems, *scratch):
+    edges = h_rows.shape[0] // 2
     negs = n_bf.shape[0]
+    sent = 2 * EDGE_BLOCK * used // LANES
+    load = pltpu.make_async_copy(table_hbm, table, table_sem.at[0])
+    load.start()
     rel_pad = grel_ref.shape[0] // 2
     steps = edges // EDGE_BLOCK
 
@@ -72,21 +76,30 @@
     def halves(base, count):
         return pl.ds(pl.multiple_of(2 * base, 2), count, stride=2), pl.ds(2 * base + 1, count, stride=2)
 
+    def wire(step):
+        return pl.ds(pl.multiple_of(step * sent, sent), sent)
+
+    def out_copy(src, dst, sems, step):
+        rows = pl.ds(pl.multiple_of(2 * step * EDGE_BLOCK, 2 * EDGE_BLOCK), 2 * EDGE_BLOCK)
+        return pltpu.make_async_copy(src.at[rows, :], dst.at[rows, :], sems.at[step])
+
+    gn_copy = pltpu.make_async_copy(gn_ref, gn_out, table_sem.at[1])
+
     if shift:
-        q_got, gq_send, gq_got, loss_send, q_sems, gq_sems, loss_sems = scratch
+        q_own, q_got, gq_send, gq_got, loss_send, q_sems, gq_sems, loss_sems = scratch
         me = lax.axis_index('ent')
         ahead = lax.rem(me + shift, group)
         behind = lax.rem(me + group - shift, group)
 
         def q_copy(step):
             return pltpu.make_async_remote_copy(
-                src_ref=q_own.at[block(step), :], dst_ref=q_got.at[block(step), :],
+                src_ref=q_own.at[wire(step), :], dst_ref=q_got.at[wire(step), :],
                 send_sem=q_sems.at[0, step], recv_sem=q_sems.at[1, step],
                 device_id={'ent': ahead}, device_id_type=MESH)
 
         def gq_copy(step):
             return pltpu.make_async_remote_copy(
-                src_ref=gq_send.at[block(step), :], dst_ref=gq_got.at[block(step), :],
+                src_ref=gq_send.at[wire(step), :], dst_ref=gq_got.at[wire(step), :],
                 send_sem=gq_sems.at[0, step], recv_sem=gq_sems.at[1, step],
                 device_id={'ent': behind}, device_id_type=MESH)
 
@@ -94,10 +107,9 @@
         pl.semaphore_signal(barrier, inc=1, device_id={'ent': ahead}, device_id_type=MESH)
         pl.semaphore_signal(barrier, inc=1, device_id={'ent': behind}, device_id_type=MESH)
         pl.semaphore_wait(barrier, 2)
-        q_src, gq_src, gq_dst = q_got, gq_got, gq_send
     else:
-        gq_got, = scratch
-        q_src, gq_src, gq_dst = q_own, gq_got, gq_got
+        q_own, gq_got = scratch
+    load.wait()
 
     def ask(step, _):
         def gather(part, _):
@@ -105,18 +117,26 @@
             for off in range(GATHER_UNROLL):
                 at = base + off
                 h_rows[pair(at), :] = table[h_ids[shift, at]]
+            return 0
+
+        def gather_rel(part, _):
+            base = step * EDGE_BLOCK + part * GATHER_UNROLL
+            for off in range(GATHER_UNROLL):
+                at = base + off
                 r_rows[pair(at), :] = rel[r_ids[shift, at]]
             return 0
 
         lax.fori_loop(0, EDGE_BLOCK // GATHER_UNROLL, gather, 0)
-        rows = block(step)
+        lax.fori_loop(0, EDGE_BLOCK // GATHER_UNROLL, gather_rel, 0)
         even, odd = halves(step * EDGE_BLOCK, EDGE_BLOCK)
         re_h, im_h = h_rows[even, :], h_rows[odd, :]
         re_r, im_r = r_rows[even, :], r_rows[odd, :]
-        q_own[rows, 0:LANES] = (re_h * re_r - im_h * im_r).astype(BF16)
-        q_own[rows, LANES:2 * LANES] = (re_h * im_r + im_h * re_r).astype(BF16)
+        re_q, im_q = re_h * re_r - im_h * im_r, re_h * im_r + im_h * re_r
         if shift:
+            q_own[wire(step), :] = pack_rows(used, jnp.concatenate([re_q, im_q], axis=0)).astype(BF16)
             q_copy(step).start()
+        else:
+            q_own[block(step), :] = jnp.concatenate([re_q, im_q], axis=1).astype(BF16)
         return 0
 
     lax.fori_loop(0, steps, ask, 0)
@@ -147,9 +167,12 @@
     def answer(step, loss_acc):
         if shift:
             q_copy(step).wait_recv()
-        rows = block(step)
         even, odd = halves(step * EDGE_BLOCK, EDGE_BLOCK)
-        q = q_src[rows, :]
+        if shift:
+            wide = unpack_rows(used, 2 * EDGE_BLOCK, q_got[wire(step), :].astype(F32))
+            q = jnp.concatenate([wide[:EDGE_BLOCK], wide[EDGE_BLOCK:]], axis=1).astype(BF16)
+        else:
+            q = q_own[block(step), :]
         t = jnp.concatenate([t_rows[even, :].astype(BF16), t_rows[odd, :].astype(BF16)], axis=1).astype(F32)
         q_wide = q.astype(F32)
         n = n_bf[...]
@@ -164,13 +187,17 @@
         loss_acc = loss_acc + jnp.sum(w * (top + jnp.log(total) - pos), axis=0, keepdims=True)
         d_pos = w * (pos_exp / total - 1.0)
         d_neg = ((w / total) * neg_exp).astype(BF16)
-        gq_dst[rows, :] = (d_pos * t + jnp.dot(d_neg, n, preferred_element_type=F32)).astype(gq_dst.dtype)
+        g_q = d_pos * t + jnp.dot(d_neg, n, preferred_element_type=F32)
         g_tail = d_pos * q_wide
         gt_ref[even, :] = g_tail[:, 0:LANES]
         gt_ref[odd, :] = g_tail[:, LANES:2 * LANES]
         gn_acc[...] += lax.dot_general(q, d_neg, (((0,), (0,)), ((), ())), preferred_element_type=F32)
         if shift:
+            gq_send[wire(step), :] = pack_rows(used, jnp.concatenate([g_q[:, 0:LANES], g_q[:, LANES:2 * LANES]], axis=0)).astype(BF16)
             gq_copy(step).start()
+        else:
+            gq_got[block(step), :] = g_q
+        out_copy(gt_ref, gt_out, gt_sems, step).start()
         return loss_acc
 
     loss = lax.fori_loop(0, steps, answer, jnp.zeros((1, 1), F32))
@@ -184,17 +211,21 @@
         loss_ref[...] = jnp.broadcast_to(loss, loss_ref.shape)
     for half in range(2):
         gn_ref[pl.ds(half, negs, stride=2), :] = gn_acc[half * LANES:(half + 1) * LANES, :].T
+    gn_copy.start()
 
     def finish(step, carry):
         rel_re, rel_im = carry
         if shift:
             gq_copy(step).wait_recv()
-        rows = block(step)
+            wide = unpack_rows(used, 2 * EDGE_BLOCK, gq_got[wire(step), :].astype(F32))
+            re_g, im_g = wide[:EDGE_BLOCK], wide[EDGE_BLOCK:]
+        else:
+            re_g, im_g = gq_got[block(step), 0:LANES], gq_got[block(step), LANES:2 * LANES]
         even, odd = halves(step * EDGE_BLOCK, EDGE_BLOCK)
-        re_g, im_g = gq_src[rows, 0:LANES].astype(F32), gq_src[rows, LANES:2 * LANES].astype(F32)
         re_r, im_r = r_rows[even, :], r_rows[odd, :]
         gh_ref[even, :] = re_g * re_r + im_g * im_r
         gh_ref[odd, :] = im_g * re_r - re_g * im_r
+        out_copy(gh_ref, gh_out, gh_sems, step).start()
         re_h, im_h = h_rows[even, :], h_rows[odd, :]
         ids = r_vec[shift:shift + 1, pl.ds(pl.multiple_of(step * EDGE_BLOCK, EDGE_BLOCK), EDGE_BLOCK)]
         hot = (lax.broadcasted_iota(jnp.int32, (rel_pad, EDGE_BLOCK), 0) == ids).astype(F32)
@@ -208,13 +239,17 @@
     grel_ref[pl.ds(1, rel_pad, stride=2), :] = rel_im
     if shift:
         loss_copy.wait()
-
-        def drain(step, _):
+    gn_copy.wait()
+
+    def drain(step, _):
+        if shift:
             q_copy(step).wait_send()
             gq_copy(step).wait_send()
-            return 0
-
-        lax.fori_loop(0, steps, drain, 0)
+        out_copy(gt_ref, gt_out, gt_sems, step).wait()
+        out_copy(gh_ref, gh_out, gh_sems, step).wait()
+        return 0
+
+    lax.fori_loop(0, steps, drain, 0)
 
 
 def scatter_kernel(shift, h_ids, tail_ids, gh_in, gt_in, gn_in, acc_out, acc, acc_b, acc_c, acc_d, gh, gt_ref, gn_ref, in_sems, out_sems):
@@ -240,8 +275,8 @@
         copy.wait()
 
     def add_edges(step, _):
-        base = step * GATHER_UNROLL
-        for off in range(0, GATHER_UNROLL, 2):
+        base = step * SCATTER_UNROLL
+        for off in range(0, SCATTER_UNROLL, 2):
             at = base + off
             places = (pair(h_ids[shift, at]), pair(h_ids[shift, at + 1]), pair(tail_ids[0, at]), pair(tail_ids[0, at + 1]))
             refs = (acc, acc_b, acc_c, acc_d)
@@ -251,11 +286,11 @@
                 ref[place, :] = total
         return 0
 
-    lax.fori_loop(0, edges // GATHER_UNROLL, add_edges, 0)
+    lax.fori_loop(0, edges // SCATTER_UNROLL, add_edges, 0)
 
     def add_negs(step, _):
-        base = step * GATHER_UNROLL
-        for off in range(0, GATHER_UNROLL, 4):
+        base = step * SCATTER_UNROLL
+        for off in range(0, SCATTER_UNROLL, 4):
             at = base + off
             places = [pair(tail_ids[0, 2 * edges + at + k]) for k in range(4)]
             refs = (acc, acc_b, acc_c, acc_d)
@@ -264,7 +299,7 @@
                 ref[place, :] = total
         return 0
 
-    lax.fori_loop(0, negs // GATHER_UNROLL, add_negs, 0)
+    lax.fori_loop(0, negs // SCATTER_UNROLL, add_negs, 0)
 
     def out_copy(at):
         rows = pl.ds(pl.multiple_of(at * piece, piece), piece)
@@ -566,17 +601,18 @@
         steps = edges // EDGE_BLOCK
         for shift in range(groups):
             tail = moved[shift]
-            scratch = [VM((2 * edges, LANES), F32)] * 3 + [VM((2 * negs, LANES), F32), VM((edges, 2 * LANES), BF16),
-                                                         VM((negs, 2 * LANES), BF16), VM((2 * LANES, negs), F32)]
+            scratch = [VM((part_rows, 2, LANES), F32)] + [VM((2 * edges, LANES), F32)] * 2 + [VM((2 * negs, LANES), F32)]
+            scratch += [VM((2 * edges, LANES), F32)] * 3 + [VM((2 * negs, LANES), F32), VM((negs, 2 * LANES), BF16), VM((2 * LANES, negs), F32)]
+            scratch += [sems((2,)), sems((steps,)), sems((steps,))]
             if shift:
-                scratch += [VM((edges, 2 * LANES), BF16)] * 3 + [VM(losses.shape, F32), sems((2, steps)), sems((2, steps)), sems((2,))]
+                scratch += [VM((2 * edges * (width // 2) // LANES, LANES), BF16)] * 4 + [VM(losses.shape, F32), sems((2, steps)), sems((2, steps)), sems((2,))]
             else:
-                scratch += [VM((edges, 2 * LANES), F32)]
+                scratch += [VM((edges, 2 * LANES), BF16), VM((edges, 2 * LANES), F32)]
             g_h, g_t, g_n, g_rel, loss = pl.pallas_call(
-                functools.partial(bucket_kernel, shift, groups),
+                functools.partial(bucket_kernel, shift, groups, width // 2),
                 out_shape=[jax.ShapeDtypeStruct((2 * edges, LANES), F32)] * 2
                 + [jax.ShapeDtypeStruct((2 * negs, LANES), F32), jax.ShapeDtypeStruct((2 * rel_pad, LANES), F32), jax.ShapeDtypeStruct(losses.shape, F32)],
-                in_specs=[smem] * 3 + [vmem] * 4, out_specs=[vmem] * 5, scratch_shapes=scratch,
+                in_specs=[smem] * 3 + [hbm] + [vmem] * 3, out_specs=[hbm] * 3 + [vmem] * 2, scratch_shapes=scratch,
                 compiler_params=pltpu.CompilerParams(vmem_limit_bytes=VMEM_LIMIT, collective_id=0, has_side_effects=True) if shift else params,
                 name='bucket',
             )(h_all, r_all, tail, table.reshape(part_rows, 2, LANES), rel.reshape(rel_pad, 2, LANES), r_all, tail)

time: 1030 us -> 1020 us (level)
  transfers between devices with their start and end apart: 7 -> 7, of which waited for: 0 -> 0; matrix products, arithmetic and copies ran while one was open for 0% -> 0% of each run, Pallas kernels for 86% -> 85%
where the time goes in v4:
time: 1020 us; the launch traced here: 1010 us
  Pallas kernels  990 us (97%)
  starting transfers between devices  10.3 us (1%)
    pallas_call x8, Pallas kernels, device_fn(): pl.pallas_call(functools.partial(update_kernel, width, learn_rate, groups...  515 us
    pallas_call x8, Pallas kernels, device_fn(): pl.pallas_call(functools.partial(bucket_kernel, shift, groups, width // 2...  324 us
    pallas_call x8, Pallas kernels, device_fn(): pl.pallas_call(functools.partial(scatter_kernel, shift), out_shape=jax.Sh...  131 us
  transfers between devices with their start and end apart: 7, of which 0 were waited for; matrix products, arithmetic and copies ran while one was open for 0% of the time, Pallas kernels for 85%

profile of v4, /device:TPU:97, one launch (start us, length us, event | category | flops | bytes accessed | tf_op | source)
XLA Modules:
  0.0 1011.8 jit_solution(8665816501819811647)
XLA Ops:
  24.0 31.3 %bucket.8 = (f32[4096,128]{1,0:T(8,128)}, f32[4096,128]{1,0:T(8,128)}, f32[1536,128]{1,0:T(8,128)}, f32[32,128]{1,0:T(8,128)}, f32[8,128]{1,0:T(8,128)}) custom-call(s32[8,2048]{1,0:T(8,128)} %bitcast.50, s32[8,2048]{1,0:T(8,128)} %bitcast.34, s32[1,4864]{1,0:T(1,128)} %get-tuple-element.162.tail_ids.tail_vec, f32[8192,2,128]{2,1,0:T(2,128)} %bitcast.26, ...), custom_call_target="tpu_custom_call" | custom-call | tf_op jit(solution)/shard_map/bucket/pallas_call | solution.py:611
  55.4 16.0 %scatter_rows.8.acc_hbm = f32[16384,128]{1,0:T(8,128)} custom-call(s32[8,2048]{1,0:T(8,128)} %bitcast.51, s32[1,4864]{1,0:T(1,128)} %get-tuple-element.162.tail_ids.tail_vec, f32[4096,128]{1,0:T(8,128)} %get-tuple-element.83.gh_in, f32[4096,128]{1,0:T(8,128)} %get-tuple-element.84.gt_in, f32[1536,128]{1,0:T(8,128)} %get-tuple-element.85.gn_in), custom_call_target="tpu_custom_call" | custom-call | tf_op jit(solution)/shard_map/scatter_rows/pallas_call | solution.py:620
  73.9 65.7 %update.8 = (f32[16384,128]{1,0:T(8,128)}, f32[2048,128]{1,0:T(8,128)}, f32[32,128]{1,0:T(8,128)}, f32[16,128]{1,0:T(8,128)}, f32[8,128]{1,0:T(8,128)}, /*index=5*/f32[64,128]{1,0:T(8,128)}) custom-call(f32[16384,128]{1,0:T(8,128)} %scatter_rows.8.acc_hbm, f32[16384,128]{1,0:T(8,128)} %load_table.1.table_hbm, f32[2048,128]{1,0:T(8,128)} %broadcast_in_dim.12.state_in, ...), custom_call_target="tpu_custom_call" | custom-call | tf_op jit(solution)/shard_map/update/pallas_call | solution.py:632
  139.6 36.1 %bucket.9 = (f32[4096,128]{1,0:T(8,128)}, f32[4096,128]{1,0:T(8,128)}, f32[1536,128]{1,0:T(8,128)}, f32[32,128]{1,0:T(8,128)}, f32[8,128]{1,0:T(8,128)}) custom-call(s32[8,2048]{1,0:T(8,128)} %bitcast.52, s32[8,2048]{1,0:T(8,128)} %bitcast.36, s32[1,4864]{1,0:T(1,128)} %copy-done.6, f32[8192,2,128]{2,1,0:T(2,128)} %bitcast.32, f32[16,2,128]{2,1,0:T(2,128)} %bitcast.74, ...), custom_call_target="tpu_custom_call" | custom-call | tf_op jit(solution)/shard_map/bucket/pallas_call | solution.py:611
  175.7 16.4 %scatter_rows.9.acc_hbm = f32[16384,128]{1,0:T(8,128)} custom-call(s32[8,2048]{1,0:T(8,128)} %bitcast.53, s32[1,4864]{1,0:T(1,128)} %copy-done.6, f32[4096,128]{1,0:T(8,128)} %get-tuple-element.90.gh_in, f32[4096,128]{1,0:T(8,128)} %get-tuple-element.91.gt_in, f32[1536,128]{1,0:T(8,128)} %get-tuple-element.92.gn_in), custom_call_target="tpu_custom_call" | custom-call | tf_op jit(solution)/shard_map/scatter_rows/pallas_call | solution.py:620
  192.1 63.3 %update.9 = (f32[16384,128]{1,0:T(8,128)}, f32[2048,128]{1,0:T(8,128)}, f32[32,128]{1,0:T(8,128)}, f32[16,128]{1,0:T(8,128)}, f32[8,128]{1,0:T(8,128)}, /*index=5*/f32[64,128]{1,0:T(8,128)}) custom-call(f32[16384,128]{1,0:T(8,128)} %scatter_rows.9.acc_hbm, f32[16384,128]{1,0:T(8,128)} %get-tuple-element.88.table_hbm, ...), custom_call_target="tpu_custom_call" | custom-call | tf_op jit(solution)/shard_map/update/pallas_call | solution.py:632
  255.4 43.6 %bucket.10 = (f32[4096,128]{1,0:T(8,128)}, f32[4096,128]{1,0:T(8,128)}, f32[1536,128]{1,0:T(8,128)}, f32[32,128]{1,0:T(8,128)}, f32[8,128]{1,0:T(8,128)}) custom-call(s32[8,2048]{1,0:T(8,128)} %bitcast.54, s32[8,2048]{1,0:T(8,128)} %bitcast.38, s32[1,4864]{1,0:T(1,128)} %copy-done.5, f32[8192,2,128]{2,1,0:T(2,128)} %bitcast.33, f32[16,2,128]{2,1,0:T(2,128)} %bitcast.75, ...), custom_call_target="tpu_custom_call" | custom-call | tf_op jit(solution)/shard_map/bucket/pallas_call | solution.py:611
  298.9 16.4 %scatter_rows.10.acc_hbm = f32[16384,128]{1,0:T(8,128)} custom-call(s32[8,2048]{1,0:T(8,128)} %bitcast.55, s32[1,4864]{1,0:T(1,128)} %copy-done.5, f32[4096,128]{1,0:T(8,128)} %get-tuple-element.100.gh_in, f32[4096,128]{1,0:T(8,128)} %get-tuple-element.101.gt_in, f32[1536,128]{1,0:T(8,128)} %get-tuple-element.102.gn_in), custom_call_target="tpu_custom_call" | custom-call | tf_op jit(solution)/shard_map/scatter_rows/pallas_call | solution.py:620
  315.3 65.0 %update.10 = (f32[16384,128]{1,0:T(8,128)}, f32[2048,128]{1,0:T(8,128)}, f32[32,128]{1,0:T(8,128)}, f32[16,128]{1,0:T(8,128)}, f32[8,128]{1,0:T(8,128)}, /*index=5*/f32[64,128]{1,0:T(8,128)}) custom-call(f32[16384,128]{1,0:T(8,128)} %scatter_rows.10.acc_hbm, f32[16384,128]{1,0:T(8,128)} %get-tuple-element.98.table_hbm, ...), custom_call_target="tpu_custom_call" | custom-call | tf_op jit(solution)/shard_map/update/pallas_call | solution.py:632
  381.0 42.4 %bucket.11 = (f32[4096,128]{1,0:T(8,128)}, f32[4096,128]{1,0:T(8,128)}, f32[1536,128]{1,0:T(8,128)}, f32[32,128]{1,0:T(8,128)}, f32[8,128]{1,0:T(8,128)}) custom-call(s32[8,2048]{1,0:T(8,128)} %bitcast.56, s32[8,2048]{1,0:T(8,128)} %bitcast.40, s32[1,4864]{1,0:T(1,128)} %copy-done.4, f32[8192,2,128]{2,1,0:T(2,128)} %bitcast.27, f32[16,2,128]{2,1,0:T(2,128)} %bitcast.69, ...), custom_call_target="tpu_custom_call" | custom-call | tf_op jit(solution)/shard_map/bucket/pallas_call | solution.py:611
  423.4 16.4 %scatter_rows.11.acc_hbm = f32[16384,128]{1,0:T(8,128)} custom-call(s32[8,2048]{1,0:T(8,128)} %bitcast.57, s32[1,4864]{1,0:T(1,128)} %copy-done.4, f32[4096,128]{1,0:T(8,128)} %get-tuple-element.110.gh_in, f32[4096,128]{1,0:T(8,128)} %get-tuple-element.111.gt_in, f32[1536,128]{1,0:T(8,128)} %get-tuple-element.112.gn_in), custom_call_target="tpu_custom_call" | custom-call | tf_op jit(solution)/shard_map/scatter_rows/pallas_call | solution.py:620
  439.8 65.8 %update.11 = (f32[16384,128]{1,0:T(8,128)}, f32[2048,128]{1,0:T(8,128)}, f32[32,128]{1,0:T(8,128)}, f32[16,128]{1,0:T(8,128)}, f32[8,128]{1,0:T(8,128)}, /*index=5*/f32[64,128]{1,0:T(8,128)}) custom-call(f32[16384,128]{1,0:T(8,128)} %scatter_rows.11.acc_hbm, f32[16384,128]{1,0:T(8,128)} %get-tuple-element.108.table_hbm, ...), custom_call_target="tpu_custom_call" | custom-call | tf_op jit(solution)/shard_map/update/pallas_call | solution.py:632
  506.2 47.0 %bucket.12 = (f32[4096,128]{1,0:T(8,128)}, f32[4096,128]{1,0:T(8,128)}, f32[1536,128]{1,0:T(8,128)}, f32[32,128]{1,0:T(8,128)}, f32[8,128]{1,0:T(8,128)}) custom-call(s32[8,2048]{1,0:T(8,128)} %bitcast.58, s32[8,2048]{1,0:T(8,128)} %bitcast.42, s32[1,4864]{1,0:T(1,128)} %copy-done.3, f32[8192,2,128]{2,1,0:T(2,128)} %bitcast.28, f32[16,2,128]{2,1,0:T(2,128)} %bitcast.70, ...), custom_call_target="tpu_custom_call" | custom-call | tf_op jit(solution)/shard_map/bucket/pallas_call | solution.py:611
  553.2 16.4 %scatter_rows.12.acc_hbm = f32[16384,128]{1,0:T(8,128)} custom-call(s32[8,2048]{1,0:T(8,128)} %bitcast.59, s32[1,4864]{1,0:T(1,128)} %copy-done.3, f32[4096,128]{1,0:T(8,128)} %get-tuple-element.120.gh_in, f32[4096,128]{1,0:T(8,128)} %get-tuple-element.121.gt_in, f32[1536,128]{1,0:T(8,128)} %get-tuple-element.122.gn_in), custom_call_target="tpu_custom_call" | custom-call | tf_op jit(solution)/shard_map/scatter_rows/pallas_call | solution.py:620
  569.6 64.0 %update.12 = (f32[16384,128]{1,0:T(8,128)}, f32[2048,128]{1,0:T(8,128)}, f32[32,128]{1,0:T(8,128)}, f32[16,128]{1,0:T(8,128)}, f32[8,128]{1,0:T(8,128)}, /*index=5*/f32[64,128]{1,0:T(8,128)}) custom-call(f32[16384,128]{1,0:T(8,128)} %scatter_rows.12.acc_hbm, f32[16384,128]{1,0:T(8,128)} %get-tuple-element.118.table_hbm, ...), custom_call_target="tpu_custom_call" | custom-call | tf_op jit(solution)/shard_map/update/pallas_call | solution.py:632
  634.2 44.5 %bucket.13 = (f32[4096,128]{1,0:T(8,128)}, f32[4096,128]{1,0:T(8,128)}, f32[1536,128]{1,0:T(8,128)}, f32[32,128]{1,0:T(8,128)}, f32[8,128]{1,0:T(8,128)}) custom-call(s32[8,2048]{1,0:T(8,128)} %bitcast.60, s32[8,2048]{1,0:T(8,128)} %bitcast.44, s32[1,4864]{1,0:T(1,128)} %copy-done.2, f32[8192,2,128]{2,1,0:T(2,128)} %bitcast.29, f32[16,2,128]{2,1,0:T(2,128)} %bitcast.71, ...), custom_call_target="tpu_custom_call" | custom-call | tf_op jit(solution)/shard_map/bucket/pallas_call | solution.py:611
  678.7 16.4 %scatter_rows.13.acc_hbm = f32[16384,128]{1,0:T(8,128)} custom-call(s32[8,2048]{1,0:T(8,128)} %bitcast.61, s32[1,4864]{1,0:T(1,128)} %copy-done.2, f32[4096,128]{1,0:T(8,128)} %get-tuple-element.130.gh_in, f32[4096,128]{1,0:T(8,128)} %get-tuple-element.131.gt_in, f32[1536,128]{1,0:T(8,128)} %get-tuple-element.132.gn_in), custom_call_target="tpu_custom_call" | custom-call | tf_op jit(solution)/shard_map/scatter_rows/pallas_call | solution.py:620
  695.1 63.1 %update.13 = (f32[16384,128]{1,0:T(8,128)}, f32[2048,128]{1,0:T(8,128)}, f32[32,128]{1,0:T(8,128)}, f32[16,128]{1,0:T(8,128)}, f32[8,128]{1,0:T(8,128)}, /*index=5*/f32[64,128]{1,0:T(8,128)}) custom-call(f32[16384,128]{1,0:T(8,128)} %scatter_rows.13.acc_hbm, f32[16384,128]{1,0:T(8,128)} %get-tuple-element.128.table_hbm, ...), custom_call_target="tpu_custom_call" | custom-call | tf_op jit(solution)/shard_map/update/pallas_call | solution.py:632
  758.9 43.9 %bucket.14 = (f32[4096,128]{1,0:T(8,128)}, f32[4096,128]{1,0:T(8,128)}, f32[1536,128]{1,0:T(8,128)}, f32[32,128]{1,0:T(8,128)}, f32[8,128]{1,0:T(8,128)}) custom-call(s32[8,2048]{1,0:T(8,128)} %bitcast.62, s32[8,2048]{1,0:T(8,128)} %bitcast.46, s32[1,4864]{1,0:T(1,128)} %copy-done.1, f32[8192,2,128]{2,1,0:T(2,128)} %bitcast.30, f32[16,2,128]{2,1,0:T(2,128)} %bitcast.72, ...), custom_call_target="tpu_custom_call" | custom-call | tf_op jit(solution)/shard_map/bucket/pallas_call | solution.py:611
  802.8 16.4 %scatter_rows.14.acc_hbm = f32[16384,128]{1,0:T(8,128)} custom-call(s32[8,2048]{1,0:T(8,128)} %bitcast.63, s32[1,4864]{1,0:T(1,128)} %copy-done.1, f32[4096,128]{1,0:T(8,128)} %get-tuple-element.140.gh_in, f32[4096,128]{1,0:T(8,128)} %get-tuple-element.141.gt_in, f32[1536,128]{1,0:T(8,128)} %get-tuple-element.142.gn_in), custom_call_target="tpu_custom_call" | custom-call | tf_op jit(solution)/shard_map/scatter_rows/pallas_call | solution.py:620
  819.2 63.2 %update.14 = (f32[16384,128]{1,0:T(8,128)}, f32[2048,128]{1,0:T(8,128)}, f32[32,128]{1,0:T(8,128)}, f32[16,128]{1,0:T(8,128)}, f32[8,128]{1,0:T(8,128)}, /*index=5*/f32[64,128]{1,0:T(8,128)}) custom-call(f32[16384,128]{1,0:T(8,128)} %scatter_rows.14.acc_hbm, f32[16384,128]{1,0:T(8,128)} %get-tuple-element.138.table_hbm, ...), custom_call_target="tpu_custom_call" | custom-call | tf_op jit(solution)/shard_map/update/pallas_call | solution.py:632
  883.0 35.5 %bucket.15 = (f32[4096,128]{1,0:T(8,128)}, f32[4096,128]{1,0:T(8,128)}, f32[1536,128]{1,0:T(8,128)}, f32[32,128]{1,0:T(8,128)}, f32[8,128]{1,0:T(8,128)}) custom-call(s32[8,2048]{1,0:T(8,128)} %bitcast.64, s32[8,2048]{1,0:T(8,128)} %bitcast.48, s32[1,4864]{1,0:T(1,128)} %copy-done, f32[8192,2,128]{2,1,0:T(2,128)} %bitcast.31, f32[16,2,128]{2,1,0:T(2,128)} %bitcast.73, ...), custom_call_target="tpu_custom_call" | custom-call | tf_op jit(solution)/shard_map/bucket/pallas_call | solution.py:611
  918.6 16.4 %scatter_rows.15.acc_hbm = f32[16384,128]{1,0:T(8,128)} custom-call(s32[8,2048]{1,0:T(8,128)} %bitcast.65, s32[1,4864]{1,0:T(1,128)} %copy-done, f32[4096,128]{1,0:T(8,128)} %get-tuple-element.150.gh_in, f32[4096,128]{1,0:T(8,128)} %get-tuple-element.151.gt_in, f32[1536,128]{1,0:T(8,128)} %get-tuple-element.152.gn_in), custom_call_target="tpu_custom_call" | custom-call | tf_op jit(solution)/shard_map/scatter_rows/pallas_call | solution.py:620
  935.0 64.6 %update.15 = (f32[16384,128]{1,0:T(8,128)}, f32[2048,128]{1,0:T(8,128)}, f32[32,128]{1,0:T(8,128)}, f32[16,128]{1,0:T(8,128)}, f32[8,128]{1,0:T(8,128)}, /*index=5*/f32[64,128]{1,0:T(8,128)}) custom-call(f32[16384,128]{1,0:T(8,128)} %scatter_rows.15.acc_hbm, f32[16384,128]{1,0:T(8,128)} %get-tuple-element.148.table_hbm, ...), custom_call_target="tpu_custom_call" | custom-call | tf_op jit(solution)/shard_map/update/pallas_call | solution.py:632
  (50 shorter events, 40.8 us)
Async XLA Ops:
  2.2 8.4 collective-permute-start.6
  4.8 6.2 collective-permute-start.5
  6.2 374.2 %collective-permute-start.4 = (s32[1,4864]{1,0:T(1,128)S(1)}, s32[1,4864]{1,0:T(1,128)S(1)}, u32[]{:S(2)}, u32[]{:S(2)}) collective-permute-start(s32[1,4864]{1,0:T(1,128)S(1)} %get-tuple-element.165), channel_id=1, source_target_pairs={{0,3},{1,4},{2,5},{3,6},{4,7},{5,0},{6,1},{7,2},{8,11},{9,12},{10,... | collective-permute-start | bytes 58376 | tf_op jit(solution)/shard_map/ppermute | solution.py:581
  7.8 497.8 %collective-permute-start.3 = (s32[1,4864]{1,0:T(1,128)S(1)}, s32[1,4864]{1,0:T(1,128)S(1)}, u32[]{:S(2)}, u32[]{:S(2)}) collective-permute-start(s32[1,4864]{1,0:T(1,128)S(1)} %get-tuple-element.166), channel_id=1, source_target_pairs={{0,4},{1,5},{2,6},{3,7},{4,0},{5,1},{6,2},{7,3},{8,12},{9,13},{10,... | collective-permute-start | bytes 58376 | tf_op jit(solution)/shard_map/ppermute | solution.py:581
  8.1 625.5 %collective-permute-start.2 = (s32[1,4864]{1,0:T(1,128)S(1)}, s32[1,4864]{1,0:T(1,128)S(1)}, u32[]{:S(2)}, u32[]{:S(2)}) collective-permute-start(s32[1,4864]{1,0:T(1,128)S(1)} %get-tuple-element.167), channel_id=1, source_target_pairs={{0,5},{1,6},{2,7},{3,0},{4,1},{5,2},{6,3},{7,4},{8,13},{9,14},{10,... | collective-permute-start | bytes 58376 | tf_op jit(solution)/shard_map/ppermute | solution.py:581
  10.6 13.5 %copy-start.6 = (s32[1,4864]{1,0:T(1,128)}, s32[1,4864]{1,0:T(1,128)S(1)}, u32[]{:S(2)}) copy-start(s32[1,4864]{1,0:T(1,128)S(1)} %collective-permute-done.6.tail_ids.tail_vec) | copy-start | bytes 58372
  10.6 747.7 %collective-permute-start.1 = (s32[1,4864]{1,0:T(1,128)S(1)}, s32[1,4864]{1,0:T(1,128)S(1)}, u32[]{:S(2)}, u32[]{:S(2)}) collective-permute-start(s32[1,4864]{1,0:T(1,128)S(1)} %get-tuple-element.168), channel_id=1, source_target_pairs={{0,6},{1,7},{2,0},{3,1},{4,2},{5,3},{6,4},{7,5},{8,14},{9,15},{10,... | collective-permute-start | bytes 58376 | tf_op jit(solution)/shard_map/ppermute | solution.py:581
  11.1 13.0 %copy-start.5 = (s32[1,4864]{1,0:T(1,128)}, s32[1,4864]{1,0:T(1,128)S(1)}, u32[]{:S(2)}) copy-start(s32[1,4864]{1,0:T(1,128)S(1)} %collective-permute-done.5.tail_ids.tail_vec) | copy-start | bytes 58372
  11.1 871.3 %collective-permute-start = (s32[1,4864]{1,0:T(1,128)S(1)}, s32[1,4864]{1,0:T(1,128)S(1)}, u32[]{:S(2)}, u32[]{:S(2)}) collective-permute-start(s32[1,4864]{1,0:T(1,128)S(1)} %get-tuple-element.169), channel_id=1, source_target_pairs={{0,7},{1,0},{2,1},{3,2},{4,3},{5,4},{6,5},{7,6},{8,15},{9,8},{10,9... | collective-permute-start | bytes 58376 | tf_op jit(solution)/shard_map/ppermute | solution.py:581
  55.4 16.0 %dynamic-slice-start = ((f32[8192]{0:T(1024)}, s32[]{:T(128)}), f32[2048]{0:T(1024)S(1)}, s32[]{:S(2)}) async-start(f32[8192]{0:T(1024)} %param.9, s32[]{:T(128)} %select_n.3), calls=%async_computation | async-start | bytes 16896 | tf_op jit(solution)/shard_map/dynamic_slice | solution.py:595
  380.4 0.6 copy-start.4
  505.6 0.6 copy-start.3
  633.6 0.6 copy-start.2
  758.2 0.6 copy-start.1
  882.4 0.6 copy-start
  999.6 10.0 copy-start.9
  999.6 10.6 %copy-start.8 = (f32[32,128]{1,0:T(8,128)S(1)}, f32[32,128]{1,0:T(8,128)}, u32[]{:S(2)}) copy-start(f32[32,128]{1,0:T(8,128)} %get-tuple-element.160) | copy-start | bytes 49156
  999.6 11.3 %copy-start.7 = (f32[64,128]{1,0:T(8,128)S(1)}, f32[64,128]{1,0:T(8,128)}, u32[]{:S(2)}) copy-start(f32[64,128]{1,0:T(8,128)} %get-tuple-element.159) | copy-start | bytes 98308

commit v5 on v4

--- a/solution.py
+++ b/solution.py
@@ -59,7 +59,7 @@
         table_t[LANES:width, at:at + LANES] = moved.T[0:width - LANES, :]
 
 
-def bucket_kernel(shift, group, used, h_ids, r_ids, tail_ids, table_hbm, rel, r_vec, tail_vec,
+def bucket_kernel(shift, group, used, head_ids, tail_ids, table_hbm, rel, head_vec, tail_vec,
                   gh_out, gt_out, gn_out, grel_ref, loss_ref,
                   table, gh_ref, gt_ref, gn_ref, h_rows, r_rows, t_rows, n_rows, n_bf, gn_acc, table_sem, gh_sems, gt_sems, *scratch):
     edges = h_rows.shape[0] // 2
@@ -116,14 +116,14 @@
             base = step * EDGE_BLOCK + part * GATHER_UNROLL
             for off in range(GATHER_UNROLL):
                 at = base + off
-                h_rows[pair(at), :] = table[h_ids[shift, at]]
+                h_rows[pair(at), :] = table[head_ids[0, at]]
             return 0
 
         def gather_rel(part, _):
             base = step * EDGE_BLOCK + part * GATHER_UNROLL
             for off in range(GATHER_UNROLL):
                 at = base + off
-                r_rows[pair(at), :] = rel[r_ids[shift, at]]
+                r_rows[pair(at), :] = rel[head_ids[0, edges + at]]
             return 0
 
         lax.fori_loop(0, EDGE_BLOCK // GATHER_UNROLL, gather, 0)
@@ -227,7 +227,7 @@
         gh_ref[odd, :] = im_g * re_r - re_g * im_r
         out_copy(gh_ref, gh_out, gh_sems, step).start()
         re_h, im_h = h_rows[even, :], h_rows[odd, :]
-        ids = r_vec[shift:shift + 1, pl.ds(pl.multiple_of(step * EDGE_BLOCK, EDGE_BLOCK), EDGE_BLOCK)]
+        ids = head_vec[0:1, pl.ds(pl.multiple_of(edges + step * EDGE_BLOCK, EDGE_BLOCK), EDGE_BLOCK)]
         hot = (lax.broadcasted_iota(jnp.int32, (rel_pad, EDGE_BLOCK), 0) == ids).astype(F32)
         rel_re = rel_re + jnp.dot(hot, re_g * re_h + im_g * im_h, precision=lax.Precision.HIGHEST, preferred_element_type=F32)
         rel_im = rel_im + jnp.dot(hot, im_g * re_h - re_g * im_h, precision=lax.Precision.HIGHEST, preferred_element_type=F32)
@@ -252,7 +252,7 @@
     lax.fori_loop(0, steps, drain, 0)
 
 
-def scatter_kernel(shift, h_ids, tail_ids, gh_in, gt_in, gn_in, acc_out, acc, acc_b, acc_c, acc_d, gh, gt_ref, gn_ref, in_sems, out_sems):
+def scatter_kernel(head_ids, tail_ids, gh_in, gt_in, gn_in, acc_out, acc, acc_b, acc_c, acc_d, gh, gt_ref, gn_ref, in_sems, out_sems):
     edges = gh.shape[0] // 2
     negs = gn_ref.shape[0] // 2
     table_rows = acc.shape[0]
@@ -278,7 +278,7 @@
         base = step * SCATTER_UNROLL
         for off in range(0, SCATTER_UNROLL, 2):
             at = base + off
-            places = (pair(h_ids[shift, at]), pair(h_ids[shift, at + 1]), pair(tail_ids[0, at]), pair(tail_ids[0, at + 1]))
+            places = (pair(head_ids[0, at]), pair(head_ids[0, at + 1]), pair(tail_ids[0, at]), pair(tail_ids[0, at + 1]))
             refs = (acc, acc_b, acc_c, acc_d)
             terms = (gh[pair(at), :], gh[pair(at + 1), :], gt_ref[pair(at), :], gt_ref[pair(at + 1), :])
             sums = [ref[place, :] + term for ref, place, term in zip(refs, places, terms)]
@@ -580,8 +580,7 @@
         for shift in range(1, groups):
             moved.append(lax.ppermute(packed[shift:shift + 1], 'ent', [(src, (src + shift) % groups) for src in range(groups)]))
 
-        h_all = head_idx[0]
-        r_all = rel_idx[0]
+        owned = jnp.concatenate([head_idx[0], rel_idx[0]], axis=1)
         row_grid = 8
         params = pltpu.CompilerParams(vmem_limit_bytes=VMEM_LIMIT)
         table = pl.pallas_call(
@@ -601,6 +600,7 @@
         steps = edges // EDGE_BLOCK
         for shift in range(groups):
             tail = moved[shift]
+            head = owned[shift:shift + 1]
             scratch = [VM((part_rows, 2, LANES), F32)] + [VM((2 * edges, LANES), F32)] * 2 + [VM((2 * negs, LANES), F32)]
             scratch += [VM((2 * edges, LANES), F32)] * 3 + [VM((2 * negs, LANES), F32), VM((negs, 2 * LANES), BF16), VM((2 * LANES, negs), F32)]
             scratch += [sems((2,)), sems((steps,)), sems((steps,))]
@@ -612,18 +612,18 @@
                 functools.partial(bucket_kernel, shift, groups, width // 2),
                 out_shape=[jax.ShapeDtypeStruct((2 * edges, LANES), F32)] * 2
                 + [jax.ShapeDtypeStruct((2 * negs, LANES), F32), jax.ShapeDtypeStruct((2 * rel_pad, LANES), F32), jax.ShapeDtypeStruct(losses.shape, F32)],
-                in_specs=[smem] * 3 + [hbm] + [vmem] * 3, out_specs=[hbm] * 3 + [vmem] * 2, scratch_shapes=scratch,
+                in_specs=[smem] * 2 + [hbm] + [vmem] * 3, out_specs=[hbm] * 3 + [vmem] * 2, scratch_shapes=scratch,
                 compiler_params=pltpu.CompilerParams(vmem_limit_bytes=VMEM_LIMIT, collective_id=0, has_side_effects=True) if shift else params,
                 name='bucket',
-            )(h_all, r_all, tail, table.reshape(part_rows, 2, LANES), rel.reshape(rel_pad, 2, LANES), r_all, tail)
+            )(head, tail, table.reshape(part_rows, 2, LANES), rel.reshape(rel_pad, 2, LANES), head, tail)
 
             acc = pl.pallas_call(
-                functools.partial(scatter_kernel, shift),
+                scatter_kernel,
                 out_shape=jax.ShapeDtypeStruct((2 * part_rows, LANES), F32),
                 in_specs=[smem] * 2 + [hbm] * 3, out_specs=hbm,
                 scratch_shapes=[VM((2 * part_rows, LANES), F32)] * 4 + [VM((2 * edges, LANES), F32)] * 2 + [VM((2 * negs, LANES), F32), sems((3,)), sems((8,))],
                 compiler_params=params, name='scatter_rows',
-            )(h_all, tail, g_h, g_t, g_n)
+            )(head, tail, g_h, g_t, g_n)
 
             half = (2 * part_rows) // reps // 2
             half_sent = half * (width // 2) // LANES

time: 1020 us -> 953 us (0.934)
  Pallas kernels: 990 us -> 917 us
    pallas_call x8, Pallas kernels: 324 us -> 271 us  [device_fn(): pl.pallas_call(functools.partial(bucket_kernel, shift, groups, width // 2...]
    pallas_call x8, Pallas kernels: 131 us -> 111 us  [device_fn(): pl.pallas_call(scatter_kernel, out_shape=jax.ShapeDtypeStruct((2 * part_r...]
  transfers between devices with their start and end apart: 7 -> 7, of which waited for: 0 -> 0; matrix products, arithmetic and copies ran while one was open for 0% -> 1% of each run, Pallas kernels for 85% -> 85%
where the time goes in v5:
time: 953 us; the launch traced here: 941 us
  Pallas kernels  917 us (96%)
  starting transfers between devices  10.3 us (1%)
    pallas_call x8, Pallas kernels, device_fn(): pl.pallas_call(functools.partial(update_kernel, width, learn_rate, groups...  515 us
    pallas_call x8, Pallas kernels, device_fn(): pl.pallas_call(functools.partial(bucket_kernel, shift, groups, width // 2...  271 us
    pallas_call x8, Pallas kernels, device_fn(): pl.pallas_call(scatter_kernel, out_shape=jax.ShapeDtypeStruct((2 * part_r...  111 us
  transfers between devices with their start and end apart: 7, of which 0 were waited for; matrix products, arithmetic and copies ran while one was open for 1% of the time, Pallas kernels for 85%

profile of v5, /device:TPU:97, one launch (start us, length us, event | category | flops | bytes accessed | tf_op | source)
XLA Modules:
  0.0 941.0 jit_solution(4668419574067788568)
XLA Ops:
  26.3 25.1 %bucket.8 = (f32[4096,128]{1,0:T(8,128)}, f32[4096,128]{1,0:T(8,128)}, f32[1536,128]{1,0:T(8,128)}, f32[32,128]{1,0:T(8,128)}, f32[8,128]{1,0:T(8,128)}) custom-call(s32[1,4096]{1,0:T(1,128)} %get-tuple-element.170.head_ids.head_vec, s32[1,4864]{1,0:T(1,128)} %get-tuple-element.162.tail_ids.tail_vec, f32[8192,2,128]{2,1,0:T(2,128)} %bitcast.26, ...), custom_call_target="tpu_custom_call" | custom-call | tf_op jit(solution)/shard_map/bucket/pallas_call | solution.py:611
  51.4 14.0 %scatter_rows.8.acc_hbm = f32[16384,128]{1,0:T(8,128)} custom-call(s32[1,4096]{1,0:T(1,128)} %get-tuple-element.170.head_ids.head_vec, s32[1,4864]{1,0:T(1,128)} %get-tuple-element.162.tail_ids.tail_vec, f32[4096,128]{1,0:T(8,128)} %get-tuple-element.83.gh_in, f32[4096,128]{1,0:T(8,128)} %get-tuple-element.84.gt_in, f32[1536,128]{1,0:T(8,128)} %get-tuple-element.85.gn_in), custom_call_target="tpu_custom_call" | custom-call | tf_op jit(solution)/shard_map/scatter_rows/pallas_call | solution.py:620
  67.9 65.7 %update.8 = (f32[16384,128]{1,0:T(8,128)}, f32[2048,128]{1,0:T(8,128)}, f32[32,128]{1,0:T(8,128)}, f32[16,128]{1,0:T(8,128)}, f32[8,128]{1,0:T(8,128)}, /*index=5*/f32[64,128]{1,0:T(8,128)}) custom-call(f32[16384,128]{1,0:T(8,128)} %scatter_rows.8.acc_hbm, f32[16384,128]{1,0:T(8,128)} %load_table.1.table_hbm, f32[2048,128]{1,0:T(8,128)} %broadcast_in_dim.12.state_in, ...), custom_call_target="tpu_custom_call" | custom-call | tf_op jit(solution)/shard_map/update/pallas_call | solution.py:632
  133.5 28.7 %bucket.9 = (f32[4096,128]{1,0:T(8,128)}, f32[4096,128]{1,0:T(8,128)}, f32[1536,128]{1,0:T(8,128)}, f32[32,128]{1,0:T(8,128)}, f32[8,128]{1,0:T(8,128)}) custom-call(s32[1,4096]{1,0:T(1,128)} %get-tuple-element.177.head_ids.head_vec, s32[1,4864]{1,0:T(1,128)} %copy-done.6, f32[8192,2,128]{2,1,0:T(2,128)} %bitcast.32, f32[16,2,128]{2,1,0:T(2,128)} %bitcast.42, ...), custom_call_target="tpu_custom_call" | custom-call | tf_op jit(solution)/shard_map/bucket/pallas_call | solution.py:611
  162.2 13.8 %scatter_rows.9.acc_hbm = f32[16384,128]{1,0:T(8,128)} custom-call(s32[1,4096]{1,0:T(1,128)} %get-tuple-element.177.head_ids.head_vec, s32[1,4864]{1,0:T(1,128)} %copy-done.6, f32[4096,128]{1,0:T(8,128)} %get-tuple-element.90.gh_in, f32[4096,128]{1,0:T(8,128)} %get-tuple-element.91.gt_in, f32[1536,128]{1,0:T(8,128)} %get-tuple-element.92.gn_in), custom_call_target="tpu_custom_call" | custom-call | tf_op jit(solution)/shard_map/scatter_rows/pallas_call | solution.py:620
  176.1 63.3 %update.9 = (f32[16384,128]{1,0:T(8,128)}, f32[2048,128]{1,0:T(8,128)}, f32[32,128]{1,0:T(8,128)}, f32[16,128]{1,0:T(8,128)}, f32[8,128]{1,0:T(8,128)}, /*index=5*/f32[64,128]{1,0:T(8,128)}) custom-call(f32[16384,128]{1,0:T(8,128)} %scatter_rows.9.acc_hbm, f32[16384,128]{1,0:T(8,128)} %get-tuple-element.88.table_hbm, ...), custom_call_target="tpu_custom_call" | custom-call | tf_op jit(solution)/shard_map/update/pallas_call | solution.py:632
  239.4 36.2 %bucket.10 = (f32[4096,128]{1,0:T(8,128)}, f32[4096,128]{1,0:T(8,128)}, f32[1536,128]{1,0:T(8,128)}, f32[32,128]{1,0:T(8,128)}, f32[8,128]{1,0:T(8,128)}) custom-call(s32[1,4096]{1,0:T(1,128)} %get-tuple-element.176.head_ids.head_vec, s32[1,4864]{1,0:T(1,128)} %copy-done.5, f32[8192,2,128]{2,1,0:T(2,128)} %bitcast.33, f32[16,2,128]{2,1,0:T(2,128)} %bitcast.43, ...), custom_call_target="tpu_custom_call" | custom-call | tf_op jit(solution)/shard_map/bucket/pallas_call | solution.py:611
  275.5 13.8 %scatter_rows.10.acc_hbm = f32[16384,128]{1,0:T(8,128)} custom-call(s32[1,4096]{1,0:T(1,128)} %get-tuple-element.176.head_ids.head_vec, s32[1,4864]{1,0:T(1,128)} %copy-done.5, f32[4096,128]{1,0:T(8,128)} %get-tuple-element.100.gh_in, f32[4096,128]{1,0:T(8,128)} %get-tuple-element.101.gt_in, f32[1536,128]{1,0:T(8,128)} %get-tuple-element.102.gn_in), custom_call_target="tpu_custom_call" | custom-call | tf_op jit(solution)/shard_map/scatter_rows/pallas_call | solution.py:620
  289.4 65.1 %update.10 = (f32[16384,128]{1,0:T(8,128)}, f32[2048,128]{1,0:T(8,128)}, f32[32,128]{1,0:T(8,128)}, f32[16,128]{1,0:T(8,128)}, f32[8,128]{1,0:T(8,128)}, /*index=5*/f32[64,128]{1,0:T(8,128)}) custom-call(f32[16384,128]{1,0:T(8,128)} %scatter_rows.10.acc_hbm, f32[16384,128]{1,0:T(8,128)} %get-tuple-element.98.table_hbm, ...), custom_call_target="tpu_custom_call" | custom-call | tf_op jit(solution)/shard_map/update/pallas_call | solution.py:632
  355.1 35.3 %bucket.11 = (f32[4096,128]{1,0:T(8,128)}, f32[4096,128]{1,0:T(8,128)}, f32[1536,128]{1,0:T(8,128)}, f32[32,128]{1,0:T(8,128)}, f32[8,128]{1,0:T(8,128)}) custom-call(s32[1,4096]{1,0:T(1,128)} %get-tuple-element.175.head_ids.head_vec, s32[1,4864]{1,0:T(1,128)} %copy-done.4, f32[8192,2,128]{2,1,0:T(2,128)} %bitcast.28, f32[16,2,128]{2,1,0:T(2,128)} %bitcast.38, ...), custom_call_target="tpu_custom_call" | custom-call | tf_op jit(solution)/shard_map/bucket/pallas_call | solution.py:611
  390.3 13.8 %scatter_rows.11.acc_hbm = f32[16384,128]{1,0:T(8,128)} custom-call(s32[1,4096]{1,0:T(1,128)} %get-tuple-element.175.head_ids.head_vec, s32[1,4864]{1,0:T(1,128)} %copy-done.4, f32[4096,128]{1,0:T(8,128)} %get-tuple-element.110.gh_in, f32[4096,128]{1,0:T(8,128)} %get-tuple-element.111.gt_in, f32[1536,128]{1,0:T(8,128)} %get-tuple-element.112.gn_in), custom_call_target="tpu_custom_call" | custom-call | tf_op jit(solution)/shard_map/scatter_rows/pallas_call | solution.py:620
  404.2 65.5 %update.11 = (f32[16384,128]{1,0:T(8,128)}, f32[2048,128]{1,0:T(8,128)}, f32[32,128]{1,0:T(8,128)}, f32[16,128]{1,0:T(8,128)}, f32[8,128]{1,0:T(8,128)}, /*index=5*/f32[64,128]{1,0:T(8,128)}) custom-call(f32[16384,128]{1,0:T(8,128)} %scatter_rows.11.acc_hbm, f32[16384,128]{1,0:T(8,128)} %get-tuple-element.108.table_hbm, ...), custom_call_target="tpu_custom_call" | custom-call | tf_op jit(solution)/shard_map/update/pallas_call | solution.py:632
  470.4 44.0 %bucket.12 = (f32[4096,128]{1,0:T(8,128)}, f32[4096,128]{1,0:T(8,128)}, f32[1536,128]{1,0:T(8,128)}, f32[32,128]{1,0:T(8,128)}, f32[8,128]{1,0:T(8,128)}) custom-call(s32[1,4096]{1,0:T(1,128)} %get-tuple-element.174.head_ids.head_vec, s32[1,4864]{1,0:T(1,128)} %copy-done.3, f32[8192,2,128]{2,1,0:T(2,128)} %bitcast.29, f32[16,2,128]{2,1,0:T(2,128)} %bitcast.39, ...), custom_call_target="tpu_custom_call" | custom-call | tf_op jit(solution)/shard_map/bucket/pallas_call | solution.py:611
  514.4 13.8 %scatter_rows.12.acc_hbm = f32[16384,128]{1,0:T(8,128)} custom-call(s32[1,4096]{1,0:T(1,128)} %get-tuple-element.174.head_ids.head_vec, s32[1,4864]{1,0:T(1,128)} %copy-done.3, f32[4096,128]{1,0:T(8,128)} %get-tuple-element.120.gh_in, f32[4096,128]{1,0:T(8,128)} %get-tuple-element.121.gt_in, f32[1536,128]{1,0:T(8,128)} %get-tuple-element.122.gn_in), custom_call_target="tpu_custom_call" | custom-call | tf_op jit(solution)/shard_map/scatter_rows/pallas_call | solution.py:620
  528.2 64.4 %update.12 = (f32[16384,128]{1,0:T(8,128)}, f32[2048,128]{1,0:T(8,128)}, f32[32,128]{1,0:T(8,128)}, f32[16,128]{1,0:T(8,128)}, f32[8,128]{1,0:T(8,128)}, /*index=5*/f32[64,128]{1,0:T(8,128)}) custom-call(f32[16384,128]{1,0:T(8,128)} %scatter_rows.12.acc_hbm, f32[16384,128]{1,0:T(8,128)} %get-tuple-element.118.table_hbm, ...), custom_call_target="tpu_custom_call" | custom-call | tf_op jit(solution)/shard_map/update/pallas_call | solution.py:632
  593.2 37.1 %bucket.13 = (f32[4096,128]{1,0:T(8,128)}, f32[4096,128]{1,0:T(8,128)}, f32[1536,128]{1,0:T(8,128)}, f32[32,128]{1,0:T(8,128)}, f32[8,128]{1,0:T(8,128)}) custom-call(s32[1,4096]{1,0:T(1,128)} %get-tuple-element.173.head_ids.head_vec, s32[1,4864]{1,0:T(1,128)} %copy-done.2, f32[8192,2,128]{2,1,0:T(2,128)} %bitcast.30, f32[16,2,128]{2,1,0:T(2,128)} %bitcast.40, ...), custom_call_target="tpu_custom_call" | custom-call | tf_op jit(solution)/shard_map/bucket/pallas_call | solution.py:611
  630.4 13.8 %scatter_rows.13.acc_hbm = f32[16384,128]{1,0:T(8,128)} custom-call(s32[1,4096]{1,0:T(1,128)} %get-tuple-element.173.head_ids.head_vec, s32[1,4864]{1,0:T(1,128)} %copy-done.2, f32[4096,128]{1,0:T(8,128)} %get-tuple-element.130.gh_in, f32[4096,128]{1,0:T(8,128)} %get-tuple-element.131.gt_in, f32[1536,128]{1,0:T(8,128)} %get-tuple-element.132.gn_in), custom_call_target="tpu_custom_call" | custom-call | tf_op jit(solution)/shard_map/scatter_rows/pallas_call | solution.py:620
  644.2 63.1 %update.13 = (f32[16384,128]{1,0:T(8,128)}, f32[2048,128]{1,0:T(8,128)}, f32[32,128]{1,0:T(8,128)}, f32[16,128]{1,0:T(8,128)}, f32[8,128]{1,0:T(8,128)}, /*index=5*/f32[64,128]{1,0:T(8,128)}) custom-call(f32[16384,128]{1,0:T(8,128)} %scatter_rows.13.acc_hbm, f32[16384,128]{1,0:T(8,128)} %get-tuple-element.128.table_hbm, ...), custom_call_target="tpu_custom_call" | custom-call | tf_op jit(solution)/shard_map/update/pallas_call | solution.py:632
  707.9 36.5 %bucket.14 = (f32[4096,128]{1,0:T(8,128)}, f32[4096,128]{1,0:T(8,128)}, f32[1536,128]{1,0:T(8,128)}, f32[32,128]{1,0:T(8,128)}, f32[8,128]{1,0:T(8,128)}) custom-call(s32[1,4096]{1,0:T(1,128)} %get-tuple-element.172.head_ids.head_vec, s32[1,4864]{1,0:T(1,128)} %copy-done.1, f32[8192,2,128]{2,1,0:T(2,128)} %bitcast.31, f32[16,2,128]{2,1,0:T(2,128)} %bitcast.41, ...), custom_call_target="tpu_custom_call" | custom-call | tf_op jit(solution)/shard_map/bucket/pallas_call | solution.py:611
  744.4 13.8 %scatter_rows.14.acc_hbm = f32[16384,128]{1,0:T(8,128)} custom-call(s32[1,4096]{1,0:T(1,128)} %get-tuple-element.172.head_ids.head_vec, s32[1,4864]{1,0:T(1,128)} %copy-done.1, f32[4096,128]{1,0:T(8,128)} %get-tuple-element.140.gh_in, f32[4096,128]{1,0:T(8,128)} %get-tuple-element.141.gt_in, f32[1536,128]{1,0:T(8,128)} %get-tuple-element.142.gn_in), custom_call_target="tpu_custom_call" | custom-call | tf_op jit(solution)/shard_map/scatter_rows/pallas_call | solution.py:620
  758.3 63.0 %update.14 = (f32[16384,128]{1,0:T(8,128)}, f32[2048,128]{1,0:T(8,128)}, f32[32,128]{1,0:T(8,128)}, f32[16,128]{1,0:T(8,128)}, f32[8,128]{1,0:T(8,128)}, /*index=5*/f32[64,128]{1,0:T(8,128)}) custom-call(f32[16384,128]{1,0:T(8,128)} %scatter_rows.14.acc_hbm, f32[16384,128]{1,0:T(8,128)} %get-tuple-element.138.table_hbm, ...), custom_call_target="tpu_custom_call" | custom-call | tf_op jit(solution)/shard_map/update/pallas_call | solution.py:632
  821.9 28.2 %bucket.15 = (f32[4096,128]{1,0:T(8,128)}, f32[4096,128]{1,0:T(8,128)}, f32[1536,128]{1,0:T(8,128)}, f32[32,128]{1,0:T(8,128)}, f32[8,128]{1,0:T(8,128)}) custom-call(s32[1,4096]{1,0:T(1,128)} %get-tuple-element.171.head_ids.head_vec, s32[1,4864]{1,0:T(1,128)} %copy-done, f32[8192,2,128]{2,1,0:T(2,128)} %bitcast.27, f32[16,2,128]{2,1,0:T(2,128)} %bitcast.37, ...), custom_call_target="tpu_custom_call" | custom-call | tf_op jit(solution)/shard_map/bucket/pallas_call | solution.py:611
  850.1 13.8 %scatter_rows.15.acc_hbm = f32[16384,128]{1,0:T(8,128)} custom-call(s32[1,4096]{1,0:T(1,128)} %get-tuple-element.171.head_ids.head_vec, s32[1,4864]{1,0:T(1,128)} %copy-done, f32[4096,128]{1,0:T(8,128)} %get-tuple-element.150.gh_in, f32[4096,128]{1,0:T(8,128)} %get-tuple-element.151.gt_in, f32[1536,128]{1,0:T(8,128)} %get-tuple-element.152.gn_in), custom_call_target="tpu_custom_call" | custom-call | tf_op jit(solution)/shard_map/scatter_rows/pallas_call | solution.py:620
  864.0 64.8 %update.15 = (f32[16384,128]{1,0:T(8,128)}, f32[2048,128]{1,0:T(8,128)}, f32[32,128]{1,0:T(8,128)}, f32[16,128]{1,0:T(8,128)}, f32[8,128]{1,0:T(8,128)}, /*index=5*/f32[64,128]{1,0:T(8,128)}) custom-call(f32[16384,128]{1,0:T(8,128)} %scatter_rows.15.acc_hbm, f32[16384,128]{1,0:T(8,128)} %get-tuple-element.148.table_hbm, ...), custom_call_target="tpu_custom_call" | custom-call | tf_op jit(solution)/shard_map/update/pallas_call | solution.py:632
  (51 shorter events, 43.0 us)
Async XLA Ops:
  2.2 8.4 collective-permute-start.6
  4.8 6.2 collective-permute-start.5
  6.2 348.3 %collective-permute-start.4 = (s32[1,4864]{1,0:T(1,128)S(1)}, s32[1,4864]{1,0:T(1,128)S(1)}, u32[]{:S(2)}, u32[]{:S(2)}) collective-permute-start(s32[1,4864]{1,0:T(1,128)S(1)} %get-tuple-element.165), channel_id=1, source_target_pairs={{0,3},{1,4},{2,5},{3,6},{4,7},{5,0},{6,1},{7,2},{8,11},{9,12},{10,... | collective-permute-start | bytes 58376 | tf_op jit(solution)/shard_map/ppermute | solution.py:581
  7.8 461.9 %collective-permute-start.3 = (s32[1,4864]{1,0:T(1,128)S(1)}, s32[1,4864]{1,0:T(1,128)S(1)}, u32[]{:S(2)}, u32[]{:S(2)}) collective-permute-start(s32[1,4864]{1,0:T(1,128)S(1)} %get-tuple-element.166), channel_id=1, source_target_pairs={{0,4},{1,5},{2,6},{3,7},{4,0},{5,1},{6,2},{7,3},{8,12},{9,13},{10,... | collective-permute-start | bytes 58376 | tf_op jit(solution)/shard_map/ppermute | solution.py:581
  8.1 584.5 %collective-permute-start.2 = (s32[1,4864]{1,0:T(1,128)S(1)}, s32[1,4864]{1,0:T(1,128)S(1)}, u32[]{:S(2)}, u32[]{:S(2)}) collective-permute-start(s32[1,4864]{1,0:T(1,128)S(1)} %get-tuple-element.167), channel_id=1, source_target_pairs={{0,5},{1,6},{2,7},{3,0},{4,1},{5,2},{6,3},{7,4},{8,13},{9,14},{10,... | collective-permute-start | bytes 58376 | tf_op jit(solution)/shard_map/ppermute | solution.py:581
  10.6 15.7 %copy-start.6 = (s32[1,4864]{1,0:T(1,128)}, s32[1,4864]{1,0:T(1,128)S(1)}, u32[]{:S(2)}) copy-start(s32[1,4864]{1,0:T(1,128)S(1)} %collective-permute-done.6.tail_ids.tail_vec) | copy-start | bytes 58372
  10.6 696.7 %collective-permute-start.1 = (s32[1,4864]{1,0:T(1,128)S(1)}, s32[1,4864]{1,0:T(1,128)S(1)}, u32[]{:S(2)}, u32[]{:S(2)}) collective-permute-start(s32[1,4864]{1,0:T(1,128)S(1)} %get-tuple-element.168), channel_id=1, source_target_pairs={{0,6},{1,7},{2,0},{3,1},{4,2},{5,3},{6,4},{7,5},{8,14},{9,15},{10,... | collective-permute-start | bytes 58376 | tf_op jit(solution)/shard_map/ppermute | solution.py:581
  11.1 15.2 %copy-start.5 = (s32[1,4864]{1,0:T(1,128)}, s32[1,4864]{1,0:T(1,128)S(1)}, u32[]{:S(2)}) copy-start(s32[1,4864]{1,0:T(1,128)S(1)} %collective-permute-done.5.tail_ids.tail_vec) | copy-start | bytes 58372
  11.1 810.3 %collective-permute-start = (s32[1,4864]{1,0:T(1,128)S(1)}, s32[1,4864]{1,0:T(1,128)S(1)}, u32[]{:S(2)}, u32[]{:S(2)}) collective-permute-start(s32[1,4864]{1,0:T(1,128)S(1)} %get-tuple-element.169), channel_id=1, source_target_pairs={{0,7},{1,0},{2,1},{3,2},{4,3},{5,4},{6,5},{7,6},{8,15},{9,8},{10,9... | collective-permute-start | bytes 58376 | tf_op jit(solution)/shard_map/ppermute | solution.py:581
  51.4 14.0 %dynamic-slice-start = ((f32[8192]{0:T(1024)}, s32[]{:T(128)}), f32[2048]{0:T(1024)S(1)}, s32[]{:S(2)}) async-start(f32[8192]{0:T(1024)} %param.9, s32[]{:T(128)} %select_n.3), calls=%async_computation | async-start | bytes 16896 | tf_op jit(solution)/shard_map/dynamic_slice | solution.py:594
  354.5 0.6 copy-start.4
  469.7 0.6 copy-start.3
  592.6 0.6 copy-start.2
  707.3 0.6 copy-start.1
  821.3 0.6 copy-start
  928.8 10.0 %copy-start.9 = (f32[8,128]{1,0:T(8,128)S(1)}, f32[8,128]{1,0:T(8,128)}, u32[]{:S(2)}) copy-start(f32[8,128]{1,0:T(8,128)} %get-tuple-element.161) | copy-start | bytes 12292
  928.8 10.6 %copy-start.8 = (f32[32,128]{1,0:T(8,128)S(1)}, f32[32,128]{1,0:T(8,128)}, u32[]{:S(2)}) copy-start(f32[32,128]{1,0:T(8,128)} %get-tuple-element.160) | copy-start | bytes 49156
  928.8 11.3 %copy-start.7 = (f32[64,128]{1,0:T(8,128)S(1)}, f32[64,128]{1,0:T(8,128)}, u32[]{:S(2)}) copy-start(f32[64,128]{1,0:T(8,128)} %get-tuple-element.159) | copy-start | bytes 98308
